TPU v7x, 32 devices: a whole 2x2x4 slice. The times are simulated.
32 devices in a mesh: runs: 2 (over y), gx: 4 (over z), gy: 2 (over x), gz: 2 (over core).
Axes of the slice: x: 2, y: 2, z: 4, core: 2. Of those that a mesh axis runs over, the one named last changes fastest.
Arguments:
- positions: float32 [3, 8, 4096], P(None, None, ('runs', 'gx', 'gy', 'gz')), parts along dimension 2, as said below
- velocities: float32 [3, 8, 4096], P(None, None, ('runs', 'gx', 'gy', 'gz')), parts along dimension 2, may hold values from -5 to 5
- send_list: int32 [5696], P(('runs', 'gx', 'gy', 'gz')), parts along dimension 0, may hold values from 0 to 127
- pair_list: int32 [2, 57344], P(None, ('runs', 'gx', 'gy', 'gz')), parts along dimension 1, may hold values from 0 to 306, as said below
- constraint_flags: int32 [7, 4096], P(None, ('runs', 'gx', 'gy', 'gz')), parts along dimension 1, may hold values 0 or 1
Outputs:
- final_positions: float32 [3, 8, 4096], P(None, None, ('runs', 'gx', 'gy', 'gz')), parts along dimension 2
- final_velocities: float32 [3, 8, 4096], P(None, None, ('runs', 'gx', 'gy', 'gz')), parts along dimension 2
- energies: float32 [6, 2], P('runs'), parts along dimension 0
There are 2 independent parts, one for each index of `runs`. A program takes and returns all parts, laid end to end along the dimension named above; each array names one. Nothing has to cross between parts.
Inputs may be any that keep to these rules, and one draw needn't show every extreme that they name: `pair_list`: each domain's 1792 slots name clusters of its extended set: 0 to 127 its own, then its received zone blocks in order; padding slots hold 306 in both rows; every cluster appears in a slot with itself; no unordered pair appears twice. `positions`: eight beads of a cluster lie in its cell of side 1, the cells of a domain filling a box of 1 by 8 by 16; neighbouring beads of a cluster are between 0.25 and 0.6 apart.
All inputs are finite; a program needn't handle non-finite values. No bound on the sum of `constraint_flags` on one device may be relied on, other than what follows from the above.
Results may differ from a plain program's by a relative error of at most 0.0003.
Values sent between devices are 32-bit elements; how exact they have to be, the bound alone decides.
No kernel may reach another device: no remote copies, remote signals or barrier semaphores. Data moves between devices by JAX's collectives and lax.ppermute only.
A program may use at most 64 MiB of HBM per device.

v0:
```python
import jax
import jax.numpy as jnp
import numpy as np
from jax import lax
from jax.sharding import PartitionSpec as P

CX = 1
CY = 8
CZ = 16
ITERS = 3
NORDER = 4


time_step = 0.02
strength = 2.0
root_half = 0.7071067811865476
zone_list = ((1, 0, 0), (0, 1, 0), (0, 0, 1), (1, 1, 0), (1, 0, 1), (0, 1, 1), (1, 1, 1))


def from_behind(value, axis, by):
    count = lax.axis_size(axis)
    return lax.ppermute(value, axis, [(i, (i + by) % count) for i in range(count)])


def zone_sizes():
    return tuple(
        (
            (CX if direction[0] == 0 else 1)
            * (CY if direction[1] == 0 else 1)
            * (CZ if direction[2] == 0 else 1)
            for direction in zone_list
        )
    )


def split_blocks(packed, block_sizes):
    pieces = []
    position = 0
    for length in block_sizes:
        pieces.append(packed[:, :, position : position + length])
        position += length
    return pieces


def shell_offsets():
    block_sizes = zone_sizes()
    columns = []
    for number in range(7):
        direction = zone_list[number]
        column = np.array(
            [[direction[0] * CX], [direction[1] * CY], [direction[2] * CZ]], np.float32
        )
        columns.append(np.tile(column, (1, block_sizes[number])))
    return jnp.asarray(np.concatenate(columns, axis=1))[:, None, :]


def share_coords(coords, send_list):
    sizes_all = zone_sizes()
    outgoing = split_blocks(jnp.take(coords, send_list, axis=2), sizes_all)
    along_y = from_behind(
        jnp.concatenate([outgoing[1], outgoing[3], outgoing[5], outgoing[6]], axis=2), "gy", -1
    )
    got_y = split_blocks(along_y, [sizes_all[1], sizes_all[3], sizes_all[5], sizes_all[6]])
    along_x = from_behind(
        jnp.concatenate([outgoing[0], outgoing[4], got_y[1], got_y[3]], axis=2), "gx", -1
    )
    got_x = split_blocks(along_x, [sizes_all[0], sizes_all[4], sizes_all[3], sizes_all[6]])
    along_z = from_behind(
        jnp.concatenate([outgoing[2], got_x[1], got_y[2], got_x[3]], axis=2), "gz", -1
    )
    got_z = split_blocks(along_z, [sizes_all[2], sizes_all[4], sizes_all[5], sizes_all[6]])
    received = [got_x[0], got_y[0], got_z[0], got_x[2], got_z[1], got_z[2], got_z[3]]
    return jnp.concatenate(received, axis=2) + shell_offsets()


def return_forces(halo_forces):
    sizes_all = zone_sizes()
    outgoing = split_blocks(halo_forces, sizes_all)
    along_z = from_behind(
        jnp.concatenate([outgoing[2], outgoing[4], outgoing[5], outgoing[6]], axis=2), "gz", 1
    )
    got_z = split_blocks(along_z, [sizes_all[2], sizes_all[4], sizes_all[5], sizes_all[6]])
    along_x = from_behind(
        jnp.concatenate([outgoing[0], outgoing[3], got_z[1], got_z[3]], axis=2), "gx", 1
    )
    got_x = split_blocks(along_x, [sizes_all[0], sizes_all[3], sizes_all[4], sizes_all[6]])
    settled = [got_x[0], got_z[0], got_x[2]]
    pending = [got_x[1], got_z[2], got_x[3]]
    along_y = from_behind(
        jnp.concatenate([outgoing[1], pending[0], pending[1], pending[2]], axis=2), "gy", 1
    )
    got_y = split_blocks(along_y, [sizes_all[1], sizes_all[3], sizes_all[5], sizes_all[6]])
    return jnp.concatenate(
        [settled[0], got_y[0], settled[1], got_y[1], settled[2], got_y[2], got_y[3]], axis=2
    )


def pair_tables(pair_list, extended_count):
    rows = lax.broadcasted_iota(jnp.int32, (extended_count, pair_list.shape[1]), 0)
    first_table = (rows == pair_list[0][None, :]).astype(jnp.float32)
    second_table = (rows == pair_list[1][None, :]).astype(jnp.float32)
    return (first_table, second_table)


def domain_forces(extended, pair_list, tables):
    extended_count = extended.shape[2]
    slot_count = pair_list.shape[1]
    first_ids = pair_list[0]
    second_ids = pair_list[1]
    flat = extended.reshape(24, extended_count)
    first_coords = jnp.dot(flat, tables[0], precision=lax.Precision.HIGHEST).reshape(
        3, 8, slot_count
    )
    second_coords = jnp.dot(flat, tables[1], precision=lax.Precision.HIGHEST).reshape(
        3, 8, slot_count
    )
    separation = first_coords[:, :, None, :] - second_coords[:, None, :, :]
    scaled = jnp.sum(separation * separation, axis=0)
    intersect = jnp.maximum(1.0 - scaled, 0.0)
    bead_row = lax.broadcasted_iota(jnp.int32, (8, 8, 1), 0)
    bead_column = lax.broadcasted_iota(jnp.int32, (8, 8, 1), 1)
    self_pair = (first_ids == second_ids)[None, None, :]
    usable = (first_ids < extended_count - 1)[None, None, :]
    weight = (jnp.where(self_pair, bead_row < bead_column, True) & usable).astype(jnp.float32)
    energy = strength * jnp.sum(weight * intersect * intersect * intersect)
    magnitude = 6.0 * strength * weight * intersect * intersect
    pushing = magnitude[None] * separation
    on_first = jnp.sum(pushing, axis=2).reshape(24, slot_count)
    on_second = (-jnp.sum(pushing, axis=1)).reshape(24, slot_count)
    contract = (((1,), (1,)), ((), ()))
    forces = lax.dot_general(on_first, tables[0], contract, precision=lax.Precision.HIGHEST)
    forces = forces + lax.dot_general(
        on_second, tables[1], contract, precision=lax.Precision.HIGHEST
    )
    return (forces.reshape(3, 8, extended_count), energy)


def local_forces(coords, send_list, pair_list, tables):
    halo_coords = share_coords(coords, send_list)
    dummy_cluster = jnp.zeros((3, 8, 1), jnp.float32)
    extended = jnp.concatenate([coords, halo_coords, dummy_cluster], axis=2)
    forces, energy = domain_forces(extended, pair_list, tables)
    cluster_count = coords.shape[2]
    returned = return_forces(forces[:, :, cluster_count : cluster_count + send_list.shape[0]])
    home_forces = forces[:, :, :cluster_count].at[:, :, send_list].add(returned)
    return (home_forces, energy)


def link_vectors(coords):
    return coords[:, :-1, :] - coords[:, 1:, :]


def link_lengths(coords):
    vectors = link_vectors(coords)
    return jnp.sqrt(jnp.sum(vectors * vectors, axis=0))


def expand(coupling, source):
    coupling_down = jnp.pad(coupling, ((1, 0), (0, 0)))
    coupling_up = jnp.pad(coupling, ((0, 1), (0, 0)))
    series = source
    result = source
    for expansion in range(NORDER):
        series = (
            coupling_down * jnp.pad(series, ((1, 0), (0, 0)))[:-1]
            + coupling_up * jnp.pad(series, ((0, 1), (0, 0)))[1:]
        )
        result = result + series
    return result


def apply_links(coords, directions, solution):
    shifts = directions * (root_half * solution)[None]
    return (
        coords
        - jnp.pad(shifts, ((0, 0), (0, 1), (0, 0)))
        + jnp.pad(shifts, ((0, 0), (1, 0), (0, 0)))
    )


def constrain(previous, updated, rest_length, link_flags):
    old_vectors = link_vectors(previous)
    directions = (
        old_vectors / jnp.maximum(jnp.sqrt(jnp.sum(old_vectors * old_vectors, axis=0)), 0.2)[None]
    )
    coupling = (
        0.5
        * jnp.sum(directions[:, :-1] * directions[:, 1:], axis=0)
        * link_flags[:-1]
        * link_flags[1:]
    )
    projected = jnp.sum(directions * link_vectors(updated), axis=0)
    solution = expand(coupling, link_flags * root_half * (projected - rest_length))
    updated = apply_links(updated, directions, solution)
    vectors = link_vectors(updated)
    squared = jnp.sum(vectors * vectors, axis=0)
    target = jnp.sqrt(
        jnp.maximum(2.0 * rest_length * rest_length - squared, 0.25 * rest_length * rest_length)
    )
    solution = expand(coupling, link_flags * root_half * (rest_length - target))
    updated = apply_links(updated, directions, solution)
    return updated


def on_device(positions, velocities, send_list, pair_list, constraint_flags):
    link_flags = constraint_flags.astype(jnp.float32)
    rest_length = link_lengths(positions)
    bead_total = 8 * positions.shape[2] * lax.axis_size(("gx", "gy", "gz"))
    tables = pair_tables(pair_list, positions.shape[2] + send_list.shape[0] + 1)
    forces, potential = local_forces(positions, send_list, pair_list, tables)
    energy_rows = []
    for iteration in range(ITERS):
        half_speed = velocities + 0.5 * time_step * forces
        updated = constrain(positions, positions + time_step * half_speed, rest_length, link_flags)
        half_speed = (updated - positions) / time_step
        forces, potential = local_forces(updated, send_list, pair_list, tables)
        velocities = half_speed + 0.5 * time_step * forces
        positions = updated
        kinetic = 0.5 * jnp.sum(velocities * velocities)
        energy_rows.append(jnp.stack([potential, kinetic]))
    energies = jnp.stack(energy_rows)
    energies = lax.psum(energies, ("gx", "gy", "gz"))
    return (positions, velocities, energies / bead_total)


def solution(mesh):
    return jax.shard_map(
        on_device,
        mesh=mesh,
        in_specs=(
            P(None, None, ("runs", "gx", "gy", "gz")),
            P(None, None, ("runs", "gx", "gy", "gz")),
            P(("runs", "gx", "gy", "gz")),
            P(None, ("runs", "gx", "gy", "gz")),
            P(None, ("runs", "gx", "gy", "gz")),
        ),
        out_specs=(
            P(None, None, ("runs", "gx", "gy", "gz")),
            P(None, None, ("runs", "gx", "gy", "gz")),
            P("runs", None),
        ),
        check_vma=False,
    )
```

profile of v0, /device:TPU:0, one launch (start us, length us, event | category | flops | bytes accessed | tf_op | source)
XLA Modules:
  0.0 178.5 jit_solution(6793706241259081876)
XLA Ops:
  4.1 3.0 %collective-permute-start = (f32[3,8,34]{2,1,0:T(8,128)S(1)}, f32[3,8,34]{2,1,0:T(8,128)S(1)}, u32[]{:S(2)}, u32[]{:S(2)}) collective-permute-start(f32[3,8,34]{2,1,0:T(8,128)S(1)} %pad_maximum_fusion.8), channel_id=1, source_target_pairs={{0,2},{2,0},{1,3},{3,1},{4,6},{6,4},{5,7},{7,5},{8,10},{10,8},{9,1... | collective-permute-start | bytes 9800 | tf_op jit(solution)/shard_map/ppermute | solution.py:22
  7.2 1.5 collective-permute-done
  9.0 4.1 %collective-permute-start.1 = (f32[3,8,153]{2,1,0:T(8,128)S(1)}, f32[3,8,153]{2,1,0:T(8,128)S(1)}, u32[]{:S(2)}, u32[]{:S(2)}) collective-permute-start(f32[3,8,153]{2,1,0:T(8,128)S(1)} %pad_maximum_fusion), channel_id=1, source_target_pairs={{0,12},{4,0},{8,4},{12,8},{1,13},{5,1},{9,5},{13,9},{2,14},{6,2},{... | collective-permute-start | bytes 44072 | tf_op jit(solution)/shard_map/ppermute | solution.py:22
  13.2 1.5 collective-permute-done.1
  23.0 5.6 %collective-permute-done.4 = f32[3,8,153]{2,1,0:T(8,128)S(1)} collective-permute-done((f32[3,8,153]{2,1,0:T(8,128)S(1)}, f32[3,8,153]{2,1,0:T(8,128)S(1)}, u32[]{:S(2)}, u32[]{:S(2)}) %collective-permute-start.4) | collective-permute-done | bytes 14720 | tf_op jit(solution)/shard_map/ppermute | solution.py:22
  28.7 1.5 collective-permute-start.5
  30.5 2.0 %collective-permute-done.5 = f32[3,8,34]{2,1,0:T(8,128)S(1)} collective-permute-done((f32[3,8,34]{2,1,0:T(8,128)S(1)}, f32[3,8,34]{2,1,0:T(8,128)S(1)}, u32[]{:S(2)}, u32[]{:S(2)}) %collective-permute-start.5) | collective-permute-done | bytes 3296 | tf_op jit(solution)/shard_map/ppermute | solution.py:22
  32.9 7.2 %scatter_fusion = f32[3,8,128]{1,0,2:T(4,128)S(1)} fusion(f32[3,8,128]{1,0,2:T(4,128)S(1)} %copy.120, s32[178]{0:T(256)S(1)} %compare_select_fusion, f32[178,3,8]{2,1,0:T(4,128)S(1)} %copy.102), kind=kCustom, calls=%fused_computation.4 | custom fusion | flops 4272 | bytes 51976 | tf_op jit(solution)/shard_map/scatter-add | solution.py:145
  41.9 1.5 collective-permute-start.6
  43.4 2.1 %collective-permute-done.6 = f32[3,8,34]{2,1,0:T(8,128)S(1)} collective-permute-done((f32[3,8,34]{2,1,0:T(8,128)S(1)}, f32[3,8,34]{2,1,0:T(8,128)S(1)}, u32[]{:S(2)}, u32[]{:S(2)}) %collective-permute-start.6) | collective-permute-done | bytes 3296 | tf_op jit(solution)/shard_map/ppermute | solution.py:22
  45.8 2.0 %collective-permute-start.7 = (f32[3,8,153]{2,1,0:T(8,128)S(1)}, f32[3,8,153]{2,1,0:T(8,128)S(1)}, u32[]{:S(2)}, u32[]{:S(2)}) collective-permute-start(f32[3,8,153]{2,1,0:T(8,128)S(1)} %pad_maximum_fusion.2), channel_id=1, source_target_pairs={{0,12},{4,0},{8,4},{12,8},{1,13},{5,1},{9,5},{13,9},{2,14},{6,2},{... | collective-permute-start | bytes 44072 | tf_op jit(solution)/shard_map/ppermute | solution.py:22
  47.8 1.8 %collective-permute-done.7 = f32[3,8,153]{2,1,0:T(8,128)S(1)} collective-permute-done((f32[3,8,153]{2,1,0:T(8,128)S(1)}, f32[3,8,153]{2,1,0:T(8,128)S(1)}, u32[]{:S(2)}, u32[]{:S(2)}) %collective-permute-start.7) | collective-permute-done | bytes 14720 | tf_op jit(solution)/shard_map/ppermute | solution.py:22
  57.8 5.6 %collective-permute-done.10 = f32[3,8,153]{2,1,0:T(8,128)S(1)} collective-permute-done((f32[3,8,153]{2,1,0:T(8,128)S(1)}, f32[3,8,153]{2,1,0:T(8,128)S(1)}, u32[]{:S(2)}, u32[]{:S(2)}) %collective-permute-start.10) | collective-permute-done | bytes 14720 | tf_op jit(solution)/shard_map/ppermute | solution.py:22
  63.5 1.5 collective-permute-start.11
  65.3 2.0 %collective-permute-done.11 = f32[3,8,34]{2,1,0:T(8,128)S(1)} collective-permute-done((f32[3,8,34]{2,1,0:T(8,128)S(1)}, f32[3,8,34]{2,1,0:T(8,128)S(1)}, u32[]{:S(2)}, u32[]{:S(2)}) %collective-permute-start.11) | collective-permute-done | bytes 3296 | tf_op jit(solution)/shard_map/ppermute | solution.py:22
  67.7 7.2 %scatter_fusion.1 = f32[3,8,128]{1,0,2:T(4,128)S(1)} fusion(f32[3,8,128]{1,0,2:T(4,128)S(1)} %copy.121, s32[178]{0:T(256)S(1)} %compare_select_fusion, f32[178,3,8]{2,1,0:T(4,128)S(1)} %copy.107), kind=kCustom, calls=%fused_computation.5 | custom fusion | flops 4272 | bytes 51976 | tf_op jit(solution)/shard_map/scatter-add | solution.py:145
  76.7 1.5 collective-permute-start.12
  78.3 2.1 %collective-permute-done.12 = f32[3,8,34]{2,1,0:T(8,128)S(1)} collective-permute-done((f32[3,8,34]{2,1,0:T(8,128)S(1)}, f32[3,8,34]{2,1,0:T(8,128)S(1)}, u32[]{:S(2)}, u32[]{:S(2)}) %collective-permute-start.12) | collective-permute-done | bytes 3296 | tf_op jit(solution)/shard_map/ppermute | solution.py:22
  80.6 2.0 %collective-permute-start.13 = (f32[3,8,153]{2,1,0:T(8,128)S(1)}, f32[3,8,153]{2,1,0:T(8,128)S(1)}, u32[]{:S(2)}, u32[]{:S(2)}) collective-permute-start(f32[3,8,153]{2,1,0:T(8,128)S(1)} %pad_maximum_fusion.4), channel_id=1, source_target_pairs={{0,12},{4,0},{8,4},{12,8},{1,13},{5,1},{9,5},{13,9},{2,14},{6,2},{... | collective-permute-start | bytes 44072 | tf_op jit(solution)/shard_map/ppermute | solution.py:22
  82.7 1.8 %collective-permute-done.13 = f32[3,8,153]{2,1,0:T(8,128)S(1)} collective-permute-done((f32[3,8,153]{2,1,0:T(8,128)S(1)}, f32[3,8,153]{2,1,0:T(8,128)S(1)}, u32[]{:S(2)}, u32[]{:S(2)}) %collective-permute-start.13) | collective-permute-done | bytes 14720 | tf_op jit(solution)/shard_map/ppermute | solution.py:22
  92.4 5.6 %collective-permute-done.16 = f32[3,8,153]{2,1,0:T(8,128)S(1)} collective-permute-done((f32[3,8,153]{2,1,0:T(8,128)S(1)}, f32[3,8,153]{2,1,0:T(8,128)S(1)}, u32[]{:S(2)}, u32[]{:S(2)}) %collective-permute-start.16) | collective-permute-done | bytes 14720 | tf_op jit(solution)/shard_map/ppermute | solution.py:22
  98.2 1.5 collective-permute-start.17
  99.9 2.0 %collective-permute-done.17 = f32[3,8,34]{2,1,0:T(8,128)S(1)} collective-permute-done((f32[3,8,34]{2,1,0:T(8,128)S(1)}, f32[3,8,34]{2,1,0:T(8,128)S(1)}, u32[]{:S(2)}, u32[]{:S(2)}) %collective-permute-start.17) | collective-permute-done | bytes 3296 | tf_op jit(solution)/shard_map/ppermute | solution.py:22
  102.4 7.2 %scatter_fusion.2 = f32[3,8,128]{1,0,2:T(4,128)S(1)} fusion(f32[3,8,128]{1,0,2:T(4,128)S(1)} %copy.122, s32[178]{0:T(256)S(1)} %compare_select_fusion, f32[178,3,8]{2,1,0:T(4,128)S(1)} %copy.112), kind=kCustom, calls=%fused_computation.6 | custom fusion | flops 4272 | bytes 51976 | tf_op jit(solution)/shard_map/scatter-add | solution.py:145
  111.9 1.5 collective-permute-start.18
  113.5 2.1 %collective-permute-done.18 = f32[3,8,34]{2,1,0:T(8,128)S(1)} collective-permute-done((f32[3,8,34]{2,1,0:T(8,128)S(1)}, f32[3,8,34]{2,1,0:T(8,128)S(1)}, u32[]{:S(2)}, u32[]{:S(2)}) %collective-permute-start.18) | collective-permute-done | bytes 3296 | tf_op jit(solution)/shard_map/ppermute | solution.py:22
  115.9 2.2 %collective-permute-start.19 = (f32[3,8,153]{2,1,0:T(8,128)S(1)}, f32[3,8,153]{2,1,0:T(8,128)S(1)}, u32[]{:S(2)}, u32[]{:S(2)}) collective-permute-start(f32[3,8,153]{2,1,0:T(8,128)S(1)} %pad_maximum_fusion.6), channel_id=1, source_target_pairs={{0,12},{4,0},{8,4},{12,8},{1,13},{5,1},{9,5},{13,9},{2,14},{6,2},{... | collective-permute-start | bytes 44072 | tf_op jit(solution)/shard_map/ppermute | solution.py:22
  118.1 1.8 %collective-permute-done.19 = f32[3,8,153]{2,1,0:T(8,128)S(1)} collective-permute-done((f32[3,8,153]{2,1,0:T(8,128)S(1)}, f32[3,8,153]{2,1,0:T(8,128)S(1)}, u32[]{:S(2)}, u32[]{:S(2)}) %collective-permute-start.19) | collective-permute-done | bytes 14720 | tf_op jit(solution)/shard_map/ppermute | solution.py:22
  131.3 3.1 %collective-permute-done.22 = f32[3,8,153]{2,1,0:T(8,128)S(1)} collective-permute-done((f32[3,8,153]{2,1,0:T(8,128)S(1)}, f32[3,8,153]{2,1,0:T(8,128)S(1)}, u32[]{:S(2)}, u32[]{:S(2)}) %collective-permute-start.22) | collective-permute-done | bytes 14720 | tf_op jit(solution)/shard_map/ppermute | solution.py:22
  134.5 1.5 collective-permute-start.23
  138.7 7.2 %scatter_fusion.3 = f32[3,8,128]{1,0,2:T(4,128)S(1)} fusion(f32[3,8,128]{1,0,2:T(4,128)S(1)} %copy.123, s32[178]{0:T(256)S(1)} %compare_select_fusion, f32[178,3,8]{2,1,0:T(4,128)S(1)} %copy.117), kind=kCustom, calls=%fused_computation.7 | custom fusion | flops 4272 | bytes 51976 | tf_op jit(solution)/shard_map/scatter-add | solution.py:145
  147.9 29.9 %psum.7 = f32[3,2]{1,0:T(4,128)S(1)} all-reduce(f32[3,2]{1,0:T(4,128)S(1)} %pad_maximum_fusion.24), channel_id=1, replica_groups=mesh['runs'=2,'gx'=4,'gy'=2,'gz'=2] {'gx','gy','gz'}, use_global_device_ids=true, to_apply=%region_34.36 | all-reduce | flops 6 | bytes 48 | tf_op jit(solution)/shard_map/psum | solution.py:222
  (294 shorter events, 50.0 us)
Async XLA Ops:
  2.0 5.2 %copy-start.4 = (s32[2,1792]{1,0:T(2,128)S(1)}, s32[2,1792]{1,0:T(2,128)}, u32[]{:S(2)}) copy-start(s32[2,1792]{1,0:T(2,128)} %param.14) | copy-start | bytes 43012
  3.9 12.3 %copy-start.3 = (f32[3,178]{1,0:T(4,128)S(1)}, f32[3,178]{1,0:T(4,128)}, u32[]{:S(2)}) copy-start(f32[3,178]{1,0:T(4,128)} %constant.57.clone) | copy-start | bytes 6412
  3.9 12.3 %copy-start = (f32[3,8,128]{2,1,0:T(8,128)S(1)}, f32[3,8,128]{2,1,0:T(8,128)}, u32[]{:S(2)}) copy-start(f32[3,8,128]{2,1,0:T(8,128)} %param.11) | copy-start | bytes 36868
  4.1 4.7 %collective-permute-start = (f32[3,8,34]{2,1,0:T(8,128)S(1)}, f32[3,8,34]{2,1,0:T(8,128)S(1)}, u32[]{:S(2)}, u32[]{:S(2)}) collective-permute-start(f32[3,8,34]{2,1,0:T(8,128)S(1)} %pad_maximum_fusion.8), channel_id=1, source_target_pairs={{0,2},{2,0},{1,3},{3,1},{4,6},{6,4},{5,7},{7,5},{8,10},{10,8},{9,1... | collective-permute-start | bytes 9800 | tf_op jit(solution)/shard_map/ppermute | solution.py:22
  9.0 5.7 %collective-permute-start.1 = (f32[3,8,153]{2,1,0:T(8,128)S(1)}, f32[3,8,153]{2,1,0:T(8,128)S(1)}, u32[]{:S(2)}, u32[]{:S(2)}) collective-permute-start(f32[3,8,153]{2,1,0:T(8,128)S(1)} %pad_maximum_fusion), channel_id=1, source_target_pairs={{0,12},{4,0},{8,4},{12,8},{1,13},{5,1},{9,5},{13,9},{2,14},{6,2},{... | collective-permute-start | bytes 44072 | tf_op jit(solution)/shard_map/ppermute | solution.py:22
  14.8 1.2 collective-permute-start.2
  19.8 10.4 %copy-start.1 = (s32[7,128]{1,0:T(8,128)S(1)}, s32[7,128]{1,0:T(8,128)}, u32[]{:S(2)}) copy-start(s32[7,128]{1,0:T(8,128)} %param.15) | copy-start | bytes 10756
  21.2 1.2 collective-permute-start.3
  22.7 5.9 %collective-permute-start.4 = (f32[3,8,153]{2,1,0:T(8,128)S(1)}, f32[3,8,153]{2,1,0:T(8,128)S(1)}, u32[]{:S(2)}, u32[]{:S(2)}) collective-permute-start(f32[3,8,153]{2,1,0:T(8,128)S(1)} %pad_maximum_fusion.1), channel_id=1, source_target_pairs={{0,4},{4,8},{8,12},{12,0},{1,5},{5,9},{9,13},{13,1},{2,6},{6,10},{... | collective-permute-start | bytes 44072 | tf_op jit(solution)/shard_map/ppermute | solution.py:22
  28.7 3.7 %collective-permute-start.5 = (f32[3,8,34]{2,1,0:T(8,128)S(1)}, f32[3,8,34]{2,1,0:T(8,128)S(1)}, u32[]{:S(2)}, u32[]{:S(2)}) collective-permute-start(f32[3,8,34]{2,1,0:T(8,128)S(1)} %pad_maximum_fusion.11), channel_id=1, source_target_pairs={{0,2},{2,0},{1,3},{3,1},{4,6},{6,4},{5,7},{7,5},{8,10},{10,8},{9,1... | collective-permute-start | bytes 9800 | tf_op jit(solution)/shard_map/ppermute | solution.py:22
  30.5 9.7 %copy-start.5 = (f32[3,8,128]{2,1,0:T(8,128)S(1)}, f32[3,8,128]{2,1,0:T(8,128)}, u32[]{:S(2)}) copy-start(f32[3,8,128]{2,1,0:T(8,128)} %param.12) | copy-start | bytes 36868
  41.9 3.7 %collective-permute-start.6 = (f32[3,8,34]{2,1,0:T(8,128)S(1)}, f32[3,8,34]{2,1,0:T(8,128)S(1)}, u32[]{:S(2)}, u32[]{:S(2)}) collective-permute-start(f32[3,8,34]{2,1,0:T(8,128)S(1)} %pad_maximum_fusion.12), channel_id=1, source_target_pairs={{0,2},{2,0},{1,3},{3,1},{4,6},{6,4},{5,7},{7,5},{8,10},{10,8},{9,1... | collective-permute-start | bytes 9800 | tf_op jit(solution)/shard_map/ppermute | solution.py:22
  45.8 3.8 %collective-permute-start.7 = (f32[3,8,153]{2,1,0:T(8,128)S(1)}, f32[3,8,153]{2,1,0:T(8,128)S(1)}, u32[]{:S(2)}, u32[]{:S(2)}) collective-permute-start(f32[3,8,153]{2,1,0:T(8,128)S(1)} %pad_maximum_fusion.2), channel_id=1, source_target_pairs={{0,12},{4,0},{8,4},{12,8},{1,13},{5,1},{9,5},{13,9},{2,14},{6,2},{... | collective-permute-start | bytes 44072 | tf_op jit(solution)/shard_map/ppermute | solution.py:22
  49.8 1.2 collective-permute-start.8
  56.2 1.2 collective-permute-start.9
  57.6 5.8 %collective-permute-start.10 = (f32[3,8,153]{2,1,0:T(8,128)S(1)}, f32[3,8,153]{2,1,0:T(8,128)S(1)}, u32[]{:S(2)}, u32[]{:S(2)}) collective-permute-start(f32[3,8,153]{2,1,0:T(8,128)S(1)} %pad_maximum_fusion.3), channel_id=1, source_target_pairs={{0,4},{4,8},{8,12},{12,0},{1,5},{5,9},{9,13},{13,1},{2,6},{6,10},{... | collective-permute-start | bytes 44072 | tf_op jit(solution)/shard_map/ppermute | solution.py:22
  63.5 3.7 %collective-permute-start.11 = (f32[3,8,34]{2,1,0:T(8,128)S(1)}, f32[3,8,34]{2,1,0:T(8,128)S(1)}, u32[]{:S(2)}, u32[]{:S(2)}) collective-permute-start(f32[3,8,34]{2,1,0:T(8,128)S(1)} %pad_maximum_fusion.15), channel_id=1, source_target_pairs={{0,2},{2,0},{1,3},{3,1},{4,6},{6,4},{5,7},{7,5},{8,10},{10,8},{9,1... | collective-permute-start | bytes 9800 | tf_op jit(solution)/shard_map/ppermute | solution.py:22
  76.7 3.7 %collective-permute-start.12 = (f32[3,8,34]{2,1,0:T(8,128)S(1)}, f32[3,8,34]{2,1,0:T(8,128)S(1)}, u32[]{:S(2)}, u32[]{:S(2)}) collective-permute-start(f32[3,8,34]{2,1,0:T(8,128)S(1)} %pad_maximum_fusion.16), channel_id=1, source_target_pairs={{0,2},{2,0},{1,3},{3,1},{4,6},{6,4},{5,7},{7,5},{8,10},{10,8},{9,1... | collective-permute-start | bytes 9800 | tf_op jit(solution)/shard_map/ppermute | solution.py:22
  80.6 3.8 %collective-permute-start.13 = (f32[3,8,153]{2,1,0:T(8,128)S(1)}, f32[3,8,153]{2,1,0:T(8,128)S(1)}, u32[]{:S(2)}, u32[]{:S(2)}) collective-permute-start(f32[3,8,153]{2,1,0:T(8,128)S(1)} %pad_maximum_fusion.4), channel_id=1, source_target_pairs={{0,12},{4,0},{8,4},{12,8},{1,13},{5,1},{9,5},{13,9},{2,14},{6,2},{... | collective-permute-start | bytes 44072 | tf_op jit(solution)/shard_map/ppermute | solution.py:22
  84.6 1.2 collective-permute-start.14
  91.0 1.2 collective-permute-start.15
  92.4 5.6 %collective-permute-start.16 = (f32[3,8,153]{2,1,0:T(8,128)S(1)}, f32[3,8,153]{2,1,0:T(8,128)S(1)}, u32[]{:S(2)}, u32[]{:S(2)}) collective-permute-start(f32[3,8,153]{2,1,0:T(8,128)S(1)} %pad_maximum_fusion.5), channel_id=1, source_target_pairs={{0,4},{4,8},{8,12},{12,0},{1,5},{5,9},{9,13},{13,1},{2,6},{6,10},{... | collective-permute-start | bytes 44072 | tf_op jit(solution)/shard_map/ppermute | solution.py:22
  98.2 3.7 %collective-permute-start.17 = (f32[3,8,34]{2,1,0:T(8,128)S(1)}, f32[3,8,34]{2,1,0:T(8,128)S(1)}, u32[]{:S(2)}, u32[]{:S(2)}) collective-permute-start(f32[3,8,34]{2,1,0:T(8,128)S(1)} %pad_maximum_fusion.19), channel_id=1, source_target_pairs={{0,2},{2,0},{1,3},{3,1},{4,6},{6,4},{5,7},{7,5},{8,10},{10,8},{9,1... | collective-permute-start | bytes 9800 | tf_op jit(solution)/shard_map/ppermute | solution.py:22
  110.5 35.4 %copy-start.2 = (f32[3,8,128]{2,1,0:T(8,128)}, f32[3,8,128]{2,1,0:T(8,128)S(1)}, u32[]{:S(2)}) copy-start(f32[3,8,128]{2,1,0:T(8,128)S(1)} %pad_add_fusion) | copy-start | bytes 36868
  111.9 3.7 %collective-permute-start.18 = (f32[3,8,34]{2,1,0:T(8,128)S(1)}, f32[3,8,34]{2,1,0:T(8,128)S(1)}, u32[]{:S(2)}, u32[]{:S(2)}) collective-permute-start(f32[3,8,34]{2,1,0:T(8,128)S(1)} %pad_maximum_fusion.20), channel_id=1, source_target_pairs={{0,2},{2,0},{1,3},{3,1},{4,6},{6,4},{5,7},{7,5},{8,10},{10,8},{9,1... | collective-permute-start | bytes 9800 | tf_op jit(solution)/shard_map/ppermute | solution.py:22
  115.9 4.0 %collective-permute-start.19 = (f32[3,8,153]{2,1,0:T(8,128)S(1)}, f32[3,8,153]{2,1,0:T(8,128)S(1)}, u32[]{:S(2)}, u32[]{:S(2)}) collective-permute-start(f32[3,8,153]{2,1,0:T(8,128)S(1)} %pad_maximum_fusion.6), channel_id=1, source_target_pairs={{0,12},{4,0},{8,4},{12,8},{1,13},{5,1},{9,5},{13,9},{2,14},{6,2},{... | collective-permute-start | bytes 44072 | tf_op jit(solution)/shard_map/ppermute | solution.py:22
  120.1 1.2 collective-permute-start.20
  127.3 1.2 collective-permute-start.21
  128.8 5.6 %collective-permute-start.22 = (f32[3,8,153]{2,1,0:T(8,128)S(1)}, f32[3,8,153]{2,1,0:T(8,128)S(1)}, u32[]{:S(2)}, u32[]{:S(2)}) collective-permute-start(f32[3,8,153]{2,1,0:T(8,128)S(1)} %pad_maximum_fusion.7), channel_id=1, source_target_pairs={{0,4},{4,8},{8,12},{12,0},{1,5},{5,9},{9,13},{13,1},{2,6},{6,10},{... | collective-permute-start | bytes 44072 | tf_op jit(solution)/shard_map/ppermute | solution.py:22
  134.5 3.7 %collective-permute-start.23 = (f32[3,8,34]{2,1,0:T(8,128)S(1)}, f32[3,8,34]{2,1,0:T(8,128)S(1)}, u32[]{:S(2)}, u32[]{:S(2)}) collective-permute-start(f32[3,8,34]{2,1,0:T(8,128)S(1)} %pad_maximum_fusion.23), channel_id=1, source_target_pairs={{0,2},{2,0},{1,3},{3,1},{4,6},{6,4},{5,7},{7,5},{8,10},{10,8},{9,1... | collective-permute-start | bytes 9800 | tf_op jit(solution)/shard_map/ppermute | solution.py:22
where the time goes:
time: 179 us
  waiting for transfers between devices  50.2 us (28%)
  other arithmetic  38.8 us (22%)
  blocking collectives  29.9 us (17%)
  starting transfers between devices  25.1 us (14%)
  matrix products  15.5 us (9%)
  local copies, waits for them, and re-layouts  13.6 us (8%)
  between operations  5.39 us (3%)
    ppermute x24, waiting for transfers between devices, from_behind(): lax.ppermute(value, axis, [(i, (i + by) % count) for i in range(count)])  50.2 us
    psum x1, blocking collectives, on_device(): energies = lax.psum(energies, ('gx', 'gy', 'gz'))  29.9 us
    scatter-add x4, other arithmetic, local_forces(): home_forces = forces[:, :, :cluster_count].at[:, :, send_list].add(returned)  28.6 us
    ppermute x24, starting transfers between devices, from_behind(): lax.ppermute(value, axis, [(i, (i + by) % count) for i in range(count)])  25.1 us
    slice x92, local copies, waits for them, and re-layouts, split_blocks(): pieces.append(packed[:, :, position:position + length])  4.99 us
    dot_general x4, matrix products, domain_forces(): lax.dot_general(on_first, tables[0], contract, precision=lax.Precision.HI...  4.36 us
    dot_general x4, matrix products, domain_forces(): lax.dot_general(on_second, tables[1], contract, precision=lax.Precision.H...  4.27 us
    gather x8, local copies, waits for them, and re-layouts, share_coords(): outgoing = split_blocks(jnp.take(coords, send_list, axis=2), sizes_all)  3.98 us
  transfers between devices with their start and end apart: 24, of which 24 were waited for; matrix products, arithmetic and copies ran while one was open for 1% of the time, Pallas kernels for 0%

commit v1 on v0

--- a/solution.py
+++ b/solution.py
@@ -54,9 +54,12 @@
     return jnp.asarray(np.concatenate(columns, axis=1))[:, None, :]
 
 
-def share_coords(coords, send_list):
+def share_coords(coords, send_table):
     sizes_all = zone_sizes()
-    outgoing = split_blocks(jnp.take(coords, send_list, axis=2), sizes_all)
+    chosen = jnp.dot(
+        coords.reshape(24, -1), send_table, precision=lax.Precision.HIGHEST
+    ).reshape(3, 8, -1)
+    outgoing = split_blocks(chosen, sizes_all)
     along_y = from_behind(
         jnp.concatenate([outgoing[1], outgoing[3], outgoing[5], outgoing[6]], axis=2), "gy", -1
     )
@@ -135,14 +138,18 @@
     return (forces.reshape(3, 8, extended_count), energy)
 
 
-def local_forces(coords, send_list, pair_list, tables):
-    halo_coords = share_coords(coords, send_list)
+def local_forces(coords, send_table, pair_list, tables):
+    halo_coords = share_coords(coords, send_table)
     dummy_cluster = jnp.zeros((3, 8, 1), jnp.float32)
     extended = jnp.concatenate([coords, halo_coords, dummy_cluster], axis=2)
     forces, energy = domain_forces(extended, pair_list, tables)
     cluster_count = coords.shape[2]
-    returned = return_forces(forces[:, :, cluster_count : cluster_count + send_list.shape[0]])
-    home_forces = forces[:, :, :cluster_count].at[:, :, send_list].add(returned)
+    returned = return_forces(forces[:, :, cluster_count : cluster_count + send_table.shape[1]])
+    contract = (((1,), (1,)), ((), ()))
+    added = lax.dot_general(
+        returned.reshape(24, -1), send_table, contract, precision=lax.Precision.HIGHEST
+    )
+    home_forces = forces[:, :, :cluster_count] + added.reshape(3, 8, -1)
     return (home_forces, energy)
 
 
@@ -202,24 +209,37 @@
     return updated
 
 
+def total_over(value, axis):
+    count = lax.axis_size(axis)
+    if count > 4:
+        return lax.psum(value, axis)
+    total = value
+    for by in range(1, count):
+        total = total + from_behind(value, axis, by)
+    return total
+
+
 def on_device(positions, velocities, send_list, pair_list, constraint_flags):
     link_flags = constraint_flags.astype(jnp.float32)
     rest_length = link_lengths(positions)
     bead_total = 8 * positions.shape[2] * lax.axis_size(("gx", "gy", "gz"))
     tables = pair_tables(pair_list, positions.shape[2] + send_list.shape[0] + 1)
-    forces, potential = local_forces(positions, send_list, pair_list, tables)
+    owned = lax.broadcasted_iota(jnp.int32, (positions.shape[2], send_list.shape[0]), 0)
+    send_table = (owned == send_list[None, :]).astype(jnp.float32)
+    forces, potential = local_forces(positions, send_table, pair_list, tables)
     energy_rows = []
     for iteration in range(ITERS):
         half_speed = velocities + 0.5 * time_step * forces
         updated = constrain(positions, positions + time_step * half_speed, rest_length, link_flags)
         half_speed = (updated - positions) / time_step
-        forces, potential = local_forces(updated, send_list, pair_list, tables)
+        forces, potential = local_forces(updated, send_table, pair_list, tables)
         velocities = half_speed + 0.5 * time_step * forces
         positions = updated
         kinetic = 0.5 * jnp.sum(velocities * velocities)
         energy_rows.append(jnp.stack([potential, kinetic]))
     energies = jnp.stack(energy_rows)
-    energies = lax.psum(energies, ("gx", "gy", "gz"))
+    for axis in ("gz", "gy", "gx"):
+        energies = total_over(energies, axis)
     return (positions, velocities, energies / bead_total)
 
 

time: 179 us -> 127 us (0.71)
  other arithmetic: 38.8 us -> 6.97 us
  blocking collectives: 29.9 us -> 0 us
  waiting for transfers between devices: 50.2 us -> 57.1 us
  local copies, waits for them, and re-layouts: 13.6 us -> 7.38 us
  starting transfers between devices: 25.1 us -> 29.9 us
  matrix products: 15.5 us -> 20.1 us
    psum x1 -> x0, blocking collectives: 29.9 us -> none  [on_device(): energies = lax.psum(energies, ('gx', 'gy', 'gz'))]
    scatter-add x4 -> x0, other arithmetic: 28.6 us -> none  [local_forces(): home_forces = forces[:, :, :cluster_count].at[:, :, send_list].add(returned)]
    ppermute x24 -> x29, waiting for transfers between devices: 50.2 us -> 57.1 us  [from_behind(): lax.ppermute(value, axis, [(i, (i + by) % count) for i in range(count)])]
    ppermute x24 -> x29, starting transfers between devices: 25.1 us -> 29.9 us  [from_behind(): lax.ppermute(value, axis, [(i, (i + by) % count) for i in range(count)])]
    dot_general x0 -> x8, matrix products: none -> 4.52 us  [the longest x4 2.77 us: local_forces(): lax.dot_general(returned.reshape(24, -1), send_table, contract, precision...]
    gather x8 -> x0, local copies, waits for them, and re-layouts: 3.98 us -> none  [share_coords(): outgoing = split_blocks(jnp.take(coords, send_list, axis=2), sizes_all)]
    reduce_sum x2 -> x0, other arithmetic: 1.87 us -> none  [on_device(): kinetic = 0.5 * jnp.sum(velocities * velocities)]
  transfers between devices with their start and end apart: 24 -> 29, of which waited for: 24 -> 29; matrix products, arithmetic and copies ran while one was open for 1% -> 2% of each run, Pallas kernels for 0% -> 0%
where the time goes in v1:
time: 127 us
  waiting for transfers between devices  57.1 us (45%)
  starting transfers between devices  29.9 us (24%)
  matrix products  20.1 us (16%)
  local copies, waits for them, and re-layouts  7.38 us (6%)
  other arithmetic  6.97 us (5%)
  between operations  5.33 us (4%)
    ppermute x29, waiting for transfers between devices, from_behind(): lax.ppermute(value, axis, [(i, (i + by) % count) for i in range(count)])  57.1 us
    ppermute x29, starting transfers between devices, from_behind(): lax.ppermute(value, axis, [(i, (i + by) % count) for i in range(count)])  29.9 us
    slice x92, local copies, waits for them, and re-layouts, split_blocks(): pieces.append(packed[:, :, position:position + length])  5.12 us
    dot_general x4, matrix products, domain_forces(): lax.dot_general(on_first, tables[0], contract, precision=lax.Precision.HI...  4.36 us
    dot_general x4, matrix products, domain_forces(): lax.dot_general(on_second, tables[1], contract, precision=lax.Precision.H...  4.27 us
    dot_general x4, matrix products, domain_forces(): jnp.dot(flat, tables[1], precision=lax.Precision.HIGHEST)  3.46 us
    dot_general x4, matrix products, domain_forces(): jnp.dot(flat, tables[0], precision=lax.Precision.HIGHEST)  3.45 us
    dot_general x4, matrix products, local_forces(): lax.dot_general(returned.reshape(24, -1), send_table, contract, precision...  2.77 us
  transfers between devices with their start and end apart: 29, of which 29 were waited for; matrix products, arithmetic and copies ran while one was open for 2% of the time, Pallas kernels for 0%

profile of v1, /device:TPU:0, one launch (start us, length us, event | category | flops | bytes accessed | tf_op | source)
XLA Modules:
  0.0 126.7 jit_solution(7093597709891666988)
XLA Ops:
  1.9 3.0 %collective-permute-start = (f32[3,8,34]{2,1,0:T(8,128)S(1)}, f32[3,8,34]{2,1,0:T(8,128)S(1)}, u32[]{:S(2)}, u32[]{:S(2)}) collective-permute-start(f32[3,8,34]{2,1,0:T(8,128)S(1)} %pad_maximum_fusion.8), channel_id=1, source_target_pairs={{0,2},{2,0},{1,3},{3,1},{4,6},{6,4},{5,7},{7,5},{8,10},{10,8},{9,1... | collective-permute-start | bytes 9800 | tf_op jit(solution)/shard_map/ppermute | solution.py:22
  6.8 4.1 %collective-permute-start.1 = (f32[3,8,153]{2,1,0:T(8,128)S(1)}, f32[3,8,153]{2,1,0:T(8,128)S(1)}, u32[]{:S(2)}, u32[]{:S(2)}) collective-permute-start(f32[3,8,153]{2,1,0:T(8,128)S(1)} %pad_maximum_fusion), channel_id=1, source_target_pairs={{0,12},{4,0},{8,4},{12,8},{1,13},{5,1},{9,5},{13,9},{2,14},{6,2},{... | collective-permute-start | bytes 44072 | tf_op jit(solution)/shard_map/ppermute | solution.py:22
  11.0 1.5 %collective-permute-done.1 = f32[3,8,153]{2,1,0:T(8,128)S(1)} collective-permute-done((f32[3,8,153]{2,1,0:T(8,128)S(1)}, f32[3,8,153]{2,1,0:T(8,128)S(1)}, u32[]{:S(2)}, u32[]{:S(2)}) %collective-permute-start.1) | collective-permute-done | bytes 14720 | tf_op jit(solution)/shard_map/ppermute | solution.py:22
  20.7 5.6 %collective-permute-done.4 = f32[3,8,153]{2,1,0:T(8,128)S(1)} collective-permute-done((f32[3,8,153]{2,1,0:T(8,128)S(1)}, f32[3,8,153]{2,1,0:T(8,128)S(1)}, u32[]{:S(2)}, u32[]{:S(2)}) %collective-permute-start.4) | collective-permute-done | bytes 14720 | tf_op jit(solution)/shard_map/ppermute | solution.py:22
  26.5 1.5 %collective-permute-start.5 = (f32[3,8,34]{2,1,0:T(8,128)S(1)}, f32[3,8,34]{2,1,0:T(8,128)S(1)}, u32[]{:S(2)}, u32[]{:S(2)}) collective-permute-start(f32[3,8,34]{2,1,0:T(8,128)S(1)} %pad_maximum_fusion.11), channel_id=1, source_target_pairs={{0,2},{2,0},{1,3},{3,1},{4,6},{6,4},{5,7},{7,5},{8,10},{10,8},{9,1... | collective-permute-start | bytes 9800 | tf_op jit(solution)/shard_map/ppermute | solution.py:22
  28.1 2.1 %collective-permute-done.5 = f32[3,8,34]{2,1,0:T(8,128)S(1)} collective-permute-done((f32[3,8,34]{2,1,0:T(8,128)S(1)}, f32[3,8,34]{2,1,0:T(8,128)S(1)}, u32[]{:S(2)}, u32[]{:S(2)}) %collective-permute-start.5) | collective-permute-done | bytes 3296 | tf_op jit(solution)/shard_map/ppermute | solution.py:22
  31.5 1.5 %collective-permute-start.6 = (f32[3,8,34]{2,1,0:T(8,128)S(1)}, f32[3,8,34]{2,1,0:T(8,128)S(1)}, u32[]{:S(2)}, u32[]{:S(2)}) collective-permute-start(f32[3,8,34]{2,1,0:T(8,128)S(1)} %pad_maximum_fusion.12), channel_id=1, source_target_pairs={{0,2},{2,0},{1,3},{3,1},{4,6},{6,4},{5,7},{7,5},{8,10},{10,8},{9,1... | collective-permute-start | bytes 9800 | tf_op jit(solution)/shard_map/ppermute | solution.py:22
  33.1 2.1 %collective-permute-done.6 = f32[3,8,34]{2,1,0:T(8,128)S(1)} collective-permute-done((f32[3,8,34]{2,1,0:T(8,128)S(1)}, f32[3,8,34]{2,1,0:T(8,128)S(1)}, u32[]{:S(2)}, u32[]{:S(2)}) %collective-permute-start.6) | collective-permute-done | bytes 3296 | tf_op jit(solution)/shard_map/ppermute | solution.py:22
  35.4 2.0 %collective-permute-start.7 = (f32[3,8,153]{2,1,0:T(8,128)S(1)}, f32[3,8,153]{2,1,0:T(8,128)S(1)}, u32[]{:S(2)}, u32[]{:S(2)}) collective-permute-start(f32[3,8,153]{2,1,0:T(8,128)S(1)} %pad_maximum_fusion.2), channel_id=1, source_target_pairs={{0,12},{4,0},{8,4},{12,8},{1,13},{5,1},{9,5},{13,9},{2,14},{6,2},{... | collective-permute-start | bytes 44072 | tf_op jit(solution)/shard_map/ppermute | solution.py:22
  37.5 1.8 %collective-permute-done.7 = f32[3,8,153]{2,1,0:T(8,128)S(1)} collective-permute-done((f32[3,8,153]{2,1,0:T(8,128)S(1)}, f32[3,8,153]{2,1,0:T(8,128)S(1)}, u32[]{:S(2)}, u32[]{:S(2)}) %collective-permute-start.7) | collective-permute-done | bytes 14720 | tf_op jit(solution)/shard_map/ppermute | solution.py:22
  47.2 5.6 %collective-permute-done.10 = f32[3,8,153]{2,1,0:T(8,128)S(1)} collective-permute-done((f32[3,8,153]{2,1,0:T(8,128)S(1)}, f32[3,8,153]{2,1,0:T(8,128)S(1)}, u32[]{:S(2)}, u32[]{:S(2)}) %collective-permute-start.10) | collective-permute-done | bytes 14720 | tf_op jit(solution)/shard_map/ppermute | solution.py:22
  53.0 1.5 %collective-permute-start.11 = (f32[3,8,34]{2,1,0:T(8,128)S(1)}, f32[3,8,34]{2,1,0:T(8,128)S(1)}, u32[]{:S(2)}, u32[]{:S(2)}) collective-permute-start(f32[3,8,34]{2,1,0:T(8,128)S(1)} %pad_maximum_fusion.15), channel_id=1, source_target_pairs={{0,2},{2,0},{1,3},{3,1},{4,6},{6,4},{5,7},{7,5},{8,10},{10,8},{9,1... | collective-permute-start | bytes 9800 | tf_op jit(solution)/shard_map/ppermute | solution.py:22
  54.5 2.1 %collective-permute-done.11 = f32[3,8,34]{2,1,0:T(8,128)S(1)} collective-permute-done((f32[3,8,34]{2,1,0:T(8,128)S(1)}, f32[3,8,34]{2,1,0:T(8,128)S(1)}, u32[]{:S(2)}, u32[]{:S(2)}) %collective-permute-start.11) | collective-permute-done | bytes 3296 | tf_op jit(solution)/shard_map/ppermute | solution.py:22
  57.9 1.5 %collective-permute-start.12 = (f32[3,8,34]{2,1,0:T(8,128)S(1)}, f32[3,8,34]{2,1,0:T(8,128)S(1)}, u32[]{:S(2)}, u32[]{:S(2)}) collective-permute-start(f32[3,8,34]{2,1,0:T(8,128)S(1)} %pad_maximum_fusion.16), channel_id=1, source_target_pairs={{0,2},{2,0},{1,3},{3,1},{4,6},{6,4},{5,7},{7,5},{8,10},{10,8},{9,1... | collective-permute-start | bytes 9800 | tf_op jit(solution)/shard_map/ppermute | solution.py:22
  59.5 2.1 %collective-permute-done.12 = f32[3,8,34]{2,1,0:T(8,128)S(1)} collective-permute-done((f32[3,8,34]{2,1,0:T(8,128)S(1)}, f32[3,8,34]{2,1,0:T(8,128)S(1)}, u32[]{:S(2)}, u32[]{:S(2)}) %collective-permute-start.12) | collective-permute-done | bytes 3296 | tf_op jit(solution)/shard_map/ppermute | solution.py:22
  61.9 2.2 %collective-permute-start.13 = (f32[3,8,153]{2,1,0:T(8,128)S(1)}, f32[3,8,153]{2,1,0:T(8,128)S(1)}, u32[]{:S(2)}, u32[]{:S(2)}) collective-permute-start(f32[3,8,153]{2,1,0:T(8,128)S(1)} %pad_maximum_fusion.4), channel_id=1, source_target_pairs={{0,12},{4,0},{8,4},{12,8},{1,13},{5,1},{9,5},{13,9},{2,14},{6,2},{... | collective-permute-start | bytes 44072 | tf_op jit(solution)/shard_map/ppermute | solution.py:22
  64.1 1.8 %collective-permute-done.13 = f32[3,8,153]{2,1,0:T(8,128)S(1)} collective-permute-done((f32[3,8,153]{2,1,0:T(8,128)S(1)}, f32[3,8,153]{2,1,0:T(8,128)S(1)}, u32[]{:S(2)}, u32[]{:S(2)}) %collective-permute-start.13) | collective-permute-done | bytes 14720 | tf_op jit(solution)/shard_map/ppermute | solution.py:22
  73.8 5.6 %collective-permute-done.16 = f32[3,8,153]{2,1,0:T(8,128)S(1)} collective-permute-done((f32[3,8,153]{2,1,0:T(8,128)S(1)}, f32[3,8,153]{2,1,0:T(8,128)S(1)}, u32[]{:S(2)}, u32[]{:S(2)}) %collective-permute-start.16) | collective-permute-done | bytes 14720 | tf_op jit(solution)/shard_map/ppermute | solution.py:22
  79.6 1.5 %collective-permute-start.17 = (f32[3,8,34]{2,1,0:T(8,128)S(1)}, f32[3,8,34]{2,1,0:T(8,128)S(1)}, u32[]{:S(2)}, u32[]{:S(2)}) collective-permute-start(f32[3,8,34]{2,1,0:T(8,128)S(1)} %pad_maximum_fusion.19), channel_id=1, source_target_pairs={{0,2},{2,0},{1,3},{3,1},{4,6},{6,4},{5,7},{7,5},{8,10},{10,8},{9,1... | collective-permute-start | bytes 9800 | tf_op jit(solution)/shard_map/ppermute | solution.py:22
  81.2 2.1 %collective-permute-done.17 = f32[3,8,34]{2,1,0:T(8,128)S(1)} collective-permute-done((f32[3,8,34]{2,1,0:T(8,128)S(1)}, f32[3,8,34]{2,1,0:T(8,128)S(1)}, u32[]{:S(2)}, u32[]{:S(2)}) %collective-permute-start.17) | collective-permute-done | bytes 3296 | tf_op jit(solution)/shard_map/ppermute | solution.py:22
  85.2 1.5 %collective-permute-start.18 = (f32[3,8,34]{2,1,0:T(8,128)S(1)}, f32[3,8,34]{2,1,0:T(8,128)S(1)}, u32[]{:S(2)}, u32[]{:S(2)}) collective-permute-start(f32[3,8,34]{2,1,0:T(8,128)S(1)} %pad_maximum_fusion.20), channel_id=1, source_target_pairs={{0,2},{2,0},{1,3},{3,1},{4,6},{6,4},{5,7},{7,5},{8,10},{10,8},{9,1... | collective-permute-start | bytes 9800 | tf_op jit(solution)/shard_map/ppermute | solution.py:22
  86.8 2.1 %collective-permute-done.18 = f32[3,8,34]{2,1,0:T(8,128)S(1)} collective-permute-done((f32[3,8,34]{2,1,0:T(8,128)S(1)}, f32[3,8,34]{2,1,0:T(8,128)S(1)}, u32[]{:S(2)}, u32[]{:S(2)}) %collective-permute-start.18) | collective-permute-done | bytes 3296 | tf_op jit(solution)/shard_map/ppermute | solution.py:22
  89.1 2.0 %collective-permute-start.19 = (f32[3,8,153]{2,1,0:T(8,128)S(1)}, f32[3,8,153]{2,1,0:T(8,128)S(1)}, u32[]{:S(2)}, u32[]{:S(2)}) collective-permute-start(f32[3,8,153]{2,1,0:T(8,128)S(1)} %pad_maximum_fusion.6), channel_id=1, source_target_pairs={{0,12},{4,0},{8,4},{12,8},{1,13},{5,1},{9,5},{13,9},{2,14},{6,2},{... | collective-permute-start | bytes 44072 | tf_op jit(solution)/shard_map/ppermute | solution.py:22
  91.1 1.8 %collective-permute-done.19 = f32[3,8,153]{2,1,0:T(8,128)S(1)} collective-permute-done((f32[3,8,153]{2,1,0:T(8,128)S(1)}, f32[3,8,153]{2,1,0:T(8,128)S(1)}, u32[]{:S(2)}, u32[]{:S(2)}) %collective-permute-start.19) | collective-permute-done | bytes 14720 | tf_op jit(solution)/shard_map/ppermute | solution.py:22
  104.3 3.1 %collective-permute-done.22 = f32[3,8,153]{2,1,0:T(8,128)S(1)} collective-permute-done((f32[3,8,153]{2,1,0:T(8,128)S(1)}, f32[3,8,153]{2,1,0:T(8,128)S(1)}, u32[]{:S(2)}, u32[]{:S(2)}) %collective-permute-start.22) | collective-permute-done | bytes 14720 | tf_op jit(solution)/shard_map/ppermute | solution.py:22
  107.5 1.5 %collective-permute-start.23 = (f32[3,8,34]{2,1,0:T(8,128)S(1)}, f32[3,8,34]{2,1,0:T(8,128)S(1)}, u32[]{:S(2)}, u32[]{:S(2)}) collective-permute-start(f32[3,8,34]{2,1,0:T(8,128)S(1)} %pad_maximum_fusion.23), channel_id=1, source_target_pairs={{0,2},{2,0},{1,3},{3,1},{4,6},{6,4},{5,7},{7,5},{8,10},{10,8},{9,1... | collective-permute-start | bytes 9800 | tf_op jit(solution)/shard_map/ppermute | solution.py:22
  109.9 1.3 %collective-permute-done.23 = f32[3,8,34]{2,1,0:T(8,128)S(1)} collective-permute-done((f32[3,8,34]{2,1,0:T(8,128)S(1)}, f32[3,8,34]{2,1,0:T(8,128)S(1)}, u32[]{:S(2)}, u32[]{:S(2)}) %collective-permute-start.23) | collective-permute-done | bytes 3296 | tf_op jit(solution)/shard_map/ppermute | solution.py:22
  111.5 1.4 %multiply_reduce_fusion = (f32[]{:T(128)}, f32[3,8,128]{2,1,0:T(8,128)}) fusion(f32[3,8,178]{2,1,0:T(8,128)S(1)} %concatenate.159, s32[178]{0:T(256)S(1)} %copy-done.4, f32[3,8,307]{2,1,0:T(8,128)S(1)} %fusion.57, f32[3,8,128]{2,1,0:T(8,128)S(1)} %pad_add_fusion, f32[3,8,128]{2,1,0:T(8,128)S(1)} %pad_add_fusion.2), kind=kOutput, calls=%fused_computation.183 | convolution fusion | flops 6606079 | bytes 66956 | tf_op jit(solution)/shard_map/dot_general | solution.py:149
  114.9 1.6 %collective-permute-start.25 = (f32[3,2]{1,0:T(4,128)S(1)}, f32[3,2]{1,0:T(4,128)S(1)}, u32[]{:S(2)}, u32[]{:S(2)}) collective-permute-start(f32[3,2]{1,0:T(4,128)S(1)} %fusion.140), channel_id=1, source_target_pairs={{0,2},{2,0},{1,3},{3,1},{4,6},{6,4},{5,7},{7,5},{8,10},{10,8},{9,1... | collective-permute-start | bytes 80 | tf_op jit(solution)/shard_map/ppermute | solution.py:22
  116.5 2.1 %collective-permute-done.25 = f32[3,2]{1,0:T(4,128)S(1)} collective-permute-done((f32[3,2]{1,0:T(4,128)S(1)}, f32[3,2]{1,0:T(4,128)S(1)}, u32[]{:S(2)}, u32[]{:S(2)}) %collective-permute-start.25) | collective-permute-done | bytes 56 | tf_op jit(solution)/shard_map/ppermute | solution.py:22
  118.6 2.1 %collective-permute-start.28 = (f32[3,2]{1,0:T(4,128)S(1)}, f32[3,2]{1,0:T(4,128)S(1)}, u32[]{:S(2)}, u32[]{:S(2)}) collective-permute-start(f32[3,2]{1,0:T(4,128)S(1)} %fusion.181), channel_id=1, source_target_pairs={{0,12},{4,0},{8,4},{12,8},{1,13},{5,1},{9,5},{13,9},{2,14},{6,2},{... | collective-permute-start | bytes 80 | tf_op jit(solution)/shard_map/ppermute | solution.py:22
  122.2 2.9 %collective-permute-done.27 = f32[3,2]{1,0:T(4,128)S(1)} collective-permute-done((f32[3,2]{1,0:T(4,128)S(1)}, f32[3,2]{1,0:T(4,128)S(1)}, u32[]{:S(2)}, u32[]{:S(2)}) %collective-permute-start.27) | collective-permute-done | bytes 56 | tf_op jit(solution)/shard_map/ppermute | solution.py:22
  (274 shorter events, 46.4 us)
Async XLA Ops:
  0.6 13.3 %copy-start.2 = (f32[3,178]{1,0:T(4,128)S(1)}, f32[3,178]{1,0:T(4,128)}, u32[]{:S(2)}) copy-start(f32[3,178]{1,0:T(4,128)} %constant.43.clone) | copy-start | bytes 6412
  0.6 13.4 %copy-start = (f32[3,8,128]{2,1,0:T(8,128)S(1)}, f32[3,8,128]{2,1,0:T(8,128)}, u32[]{:S(2)}) copy-start(f32[3,8,128]{2,1,0:T(8,128)} %param.9) | copy-start | bytes 36868
  1.9 4.7 %collective-permute-start = (f32[3,8,34]{2,1,0:T(8,128)S(1)}, f32[3,8,34]{2,1,0:T(8,128)S(1)}, u32[]{:S(2)}, u32[]{:S(2)}) collective-permute-start(f32[3,8,34]{2,1,0:T(8,128)S(1)} %pad_maximum_fusion.8), channel_id=1, source_target_pairs={{0,2},{2,0},{1,3},{3,1},{4,6},{6,4},{5,7},{7,5},{8,10},{10,8},{9,1... | collective-permute-start | bytes 9800 | tf_op jit(solution)/shard_map/ppermute | solution.py:22
  6.8 5.7 %collective-permute-start.1 = (f32[3,8,153]{2,1,0:T(8,128)S(1)}, f32[3,8,153]{2,1,0:T(8,128)S(1)}, u32[]{:S(2)}, u32[]{:S(2)}) collective-permute-start(f32[3,8,153]{2,1,0:T(8,128)S(1)} %pad_maximum_fusion), channel_id=1, source_target_pairs={{0,12},{4,0},{8,4},{12,8},{1,13},{5,1},{9,5},{13,9},{2,14},{6,2},{... | collective-permute-start | bytes 44072 | tf_op jit(solution)/shard_map/ppermute | solution.py:22
  12.6 1.2 collective-permute-start.2
  19.0 1.2 collective-permute-start.3
  20.4 5.9 %collective-permute-start.4 = (f32[3,8,153]{2,1,0:T(8,128)S(1)}, f32[3,8,153]{2,1,0:T(8,128)S(1)}, u32[]{:S(2)}, u32[]{:S(2)}) collective-permute-start(f32[3,8,153]{2,1,0:T(8,128)S(1)} %pad_maximum_fusion.1), channel_id=1, source_target_pairs={{0,4},{4,8},{8,12},{12,0},{1,5},{5,9},{9,13},{13,1},{2,6},{6,10},{... | collective-permute-start | bytes 44072 | tf_op jit(solution)/shard_map/ppermute | solution.py:22
  26.5 3.7 %collective-permute-start.5 = (f32[3,8,34]{2,1,0:T(8,128)S(1)}, f32[3,8,34]{2,1,0:T(8,128)S(1)}, u32[]{:S(2)}, u32[]{:S(2)}) collective-permute-start(f32[3,8,34]{2,1,0:T(8,128)S(1)} %pad_maximum_fusion.11), channel_id=1, source_target_pairs={{0,2},{2,0},{1,3},{3,1},{4,6},{6,4},{5,7},{7,5},{8,10},{10,8},{9,1... | collective-permute-start | bytes 9800 | tf_op jit(solution)/shard_map/ppermute | solution.py:22
  31.5 3.7 %collective-permute-start.6 = (f32[3,8,34]{2,1,0:T(8,128)S(1)}, f32[3,8,34]{2,1,0:T(8,128)S(1)}, u32[]{:S(2)}, u32[]{:S(2)}) collective-permute-start(f32[3,8,34]{2,1,0:T(8,128)S(1)} %pad_maximum_fusion.12), channel_id=1, source_target_pairs={{0,2},{2,0},{1,3},{3,1},{4,6},{6,4},{5,7},{7,5},{8,10},{10,8},{9,1... | collective-permute-start | bytes 9800 | tf_op jit(solution)/shard_map/ppermute | solution.py:22
  35.4 3.8 %collective-permute-start.7 = (f32[3,8,153]{2,1,0:T(8,128)S(1)}, f32[3,8,153]{2,1,0:T(8,128)S(1)}, u32[]{:S(2)}, u32[]{:S(2)}) collective-permute-start(f32[3,8,153]{2,1,0:T(8,128)S(1)} %pad_maximum_fusion.2), channel_id=1, source_target_pairs={{0,12},{4,0},{8,4},{12,8},{1,13},{5,1},{9,5},{13,9},{2,14},{6,2},{... | collective-permute-start | bytes 44072 | tf_op jit(solution)/shard_map/ppermute | solution.py:22
  39.4 1.2 collective-permute-start.8
  45.8 1.2 collective-permute-start.9
  47.2 5.6 %collective-permute-start.10 = (f32[3,8,153]{2,1,0:T(8,128)S(1)}, f32[3,8,153]{2,1,0:T(8,128)S(1)}, u32[]{:S(2)}, u32[]{:S(2)}) collective-permute-start(f32[3,8,153]{2,1,0:T(8,128)S(1)} %pad_maximum_fusion.3), channel_id=1, source_target_pairs={{0,4},{4,8},{8,12},{12,0},{1,5},{5,9},{9,13},{13,1},{2,6},{6,10},{... | collective-permute-start | bytes 44072 | tf_op jit(solution)/shard_map/ppermute | solution.py:22
  53.0 3.7 %collective-permute-start.11 = (f32[3,8,34]{2,1,0:T(8,128)S(1)}, f32[3,8,34]{2,1,0:T(8,128)S(1)}, u32[]{:S(2)}, u32[]{:S(2)}) collective-permute-start(f32[3,8,34]{2,1,0:T(8,128)S(1)} %pad_maximum_fusion.15), channel_id=1, source_target_pairs={{0,2},{2,0},{1,3},{3,1},{4,6},{6,4},{5,7},{7,5},{8,10},{10,8},{9,1... | collective-permute-start | bytes 9800 | tf_op jit(solution)/shard_map/ppermute | solution.py:22
  57.9 3.7 %collective-permute-start.12 = (f32[3,8,34]{2,1,0:T(8,128)S(1)}, f32[3,8,34]{2,1,0:T(8,128)S(1)}, u32[]{:S(2)}, u32[]{:S(2)}) collective-permute-start(f32[3,8,34]{2,1,0:T(8,128)S(1)} %pad_maximum_fusion.16), channel_id=1, source_target_pairs={{0,2},{2,0},{1,3},{3,1},{4,6},{6,4},{5,7},{7,5},{8,10},{10,8},{9,1... | collective-permute-start | bytes 9800 | tf_op jit(solution)/shard_map/ppermute | solution.py:22
  61.9 4.0 %collective-permute-start.13 = (f32[3,8,153]{2,1,0:T(8,128)S(1)}, f32[3,8,153]{2,1,0:T(8,128)S(1)}, u32[]{:S(2)}, u32[]{:S(2)}) collective-permute-start(f32[3,8,153]{2,1,0:T(8,128)S(1)} %pad_maximum_fusion.4), channel_id=1, source_target_pairs={{0,12},{4,0},{8,4},{12,8},{1,13},{5,1},{9,5},{13,9},{2,14},{6,2},{... | collective-permute-start | bytes 44072 | tf_op jit(solution)/shard_map/ppermute | solution.py:22
  66.0 1.2 collective-permute-start.14
  72.4 1.2 collective-permute-start.15
  73.8 5.6 %collective-permute-start.16 = (f32[3,8,153]{2,1,0:T(8,128)S(1)}, f32[3,8,153]{2,1,0:T(8,128)S(1)}, u32[]{:S(2)}, u32[]{:S(2)}) collective-permute-start(f32[3,8,153]{2,1,0:T(8,128)S(1)} %pad_maximum_fusion.5), channel_id=1, source_target_pairs={{0,4},{4,8},{8,12},{12,0},{1,5},{5,9},{9,13},{13,1},{2,6},{6,10},{... | collective-permute-start | bytes 44072 | tf_op jit(solution)/shard_map/ppermute | solution.py:22
  79.6 3.7 %collective-permute-start.17 = (f32[3,8,34]{2,1,0:T(8,128)S(1)}, f32[3,8,34]{2,1,0:T(8,128)S(1)}, u32[]{:S(2)}, u32[]{:S(2)}) collective-permute-start(f32[3,8,34]{2,1,0:T(8,128)S(1)} %pad_maximum_fusion.19), channel_id=1, source_target_pairs={{0,2},{2,0},{1,3},{3,1},{4,6},{6,4},{5,7},{7,5},{8,10},{10,8},{9,1... | collective-permute-start | bytes 9800 | tf_op jit(solution)/shard_map/ppermute | solution.py:22
  84.7 26.8 %copy-start.3 = (f32[3,8,128]{2,1,0:T(8,128)}, f32[3,8,128]{2,1,0:T(8,128)S(1)}, u32[]{:S(2)}) copy-start(f32[3,8,128]{2,1,0:T(8,128)S(1)} %pad_add_fusion) | copy-start | bytes 36868
  85.2 3.7 %collective-permute-start.18 = (f32[3,8,34]{2,1,0:T(8,128)S(1)}, f32[3,8,34]{2,1,0:T(8,128)S(1)}, u32[]{:S(2)}, u32[]{:S(2)}) collective-permute-start(f32[3,8,34]{2,1,0:T(8,128)S(1)} %pad_maximum_fusion.20), channel_id=1, source_target_pairs={{0,2},{2,0},{1,3},{3,1},{4,6},{6,4},{5,7},{7,5},{8,10},{10,8},{9,1... | collective-permute-start | bytes 9800 | tf_op jit(solution)/shard_map/ppermute | solution.py:22
  89.1 3.8 %collective-permute-start.19 = (f32[3,8,153]{2,1,0:T(8,128)S(1)}, f32[3,8,153]{2,1,0:T(8,128)S(1)}, u32[]{:S(2)}, u32[]{:S(2)}) collective-permute-start(f32[3,8,153]{2,1,0:T(8,128)S(1)} %pad_maximum_fusion.6), channel_id=1, source_target_pairs={{0,12},{4,0},{8,4},{12,8},{1,13},{5,1},{9,5},{13,9},{2,14},{6,2},{... | collective-permute-start | bytes 44072 | tf_op jit(solution)/shard_map/ppermute | solution.py:22
  93.1 1.2 collective-permute-start.20
  100.3 1.2 collective-permute-start.21
  101.8 5.6 %collective-permute-start.22 = (f32[3,8,153]{2,1,0:T(8,128)S(1)}, f32[3,8,153]{2,1,0:T(8,128)S(1)}, u32[]{:S(2)}, u32[]{:S(2)}) collective-permute-start(f32[3,8,153]{2,1,0:T(8,128)S(1)} %pad_maximum_fusion.7), channel_id=1, source_target_pairs={{0,4},{4,8},{8,12},{12,0},{1,5},{5,9},{9,13},{13,1},{2,6},{6,10},{... | collective-permute-start | bytes 44072 | tf_op jit(solution)/shard_map/ppermute | solution.py:22
  107.5 3.7 %collective-permute-start.23 = (f32[3,8,34]{2,1,0:T(8,128)S(1)}, f32[3,8,34]{2,1,0:T(8,128)S(1)}, u32[]{:S(2)}, u32[]{:S(2)}) collective-permute-start(f32[3,8,34]{2,1,0:T(8,128)S(1)} %pad_maximum_fusion.23), channel_id=1, source_target_pairs={{0,2},{2,0},{1,3},{3,1},{4,6},{6,4},{5,7},{7,5},{8,10},{10,8},{9,1... | collective-permute-start | bytes 9800 | tf_op jit(solution)/shard_map/ppermute | solution.py:22
  113.7 1.2 collective-permute-start.24
  114.9 3.7 %collective-permute-start.25 = (f32[3,2]{1,0:T(4,128)S(1)}, f32[3,2]{1,0:T(4,128)S(1)}, u32[]{:S(2)}, u32[]{:S(2)}) collective-permute-start(f32[3,2]{1,0:T(4,128)S(1)} %fusion.140), channel_id=1, source_target_pairs={{0,2},{2,0},{1,3},{3,1},{4,6},{6,4},{5,7},{7,5},{8,10},{10,8},{9,1... | collective-permute-start | bytes 80 | tf_op jit(solution)/shard_map/ppermute | solution.py:22
  118.6 3.6 %collective-permute-start.28 = (f32[3,2]{1,0:T(4,128)S(1)}, f32[3,2]{1,0:T(4,128)S(1)}, u32[]{:S(2)}, u32[]{:S(2)}) collective-permute-start(f32[3,2]{1,0:T(4,128)S(1)} %fusion.181), channel_id=1, source_target_pairs={{0,12},{4,0},{8,4},{12,8},{1,13},{5,1},{9,5},{13,9},{2,14},{6,2},{... | collective-permute-start | bytes 80 | tf_op jit(solution)/shard_map/ppermute | solution.py:22
  120.6 4.5 %collective-permute-start.27 = (f32[3,2]{1,0:T(4,128)S(1)}, f32[3,2]{1,0:T(4,128)S(1)}, u32[]{:S(2)}, u32[]{:S(2)}) collective-permute-start(f32[3,2]{1,0:T(4,128)S(1)} %fusion.181), channel_id=1, source_target_pairs={{0,8},{4,12},{8,0},{12,4},{1,9},{5,13},{9,1},{13,5},{2,10},{6,14},... | collective-permute-start | bytes 80 | tf_op jit(solution)/shard_map/ppermute | solution.py:22
  120.7 5.4 %collective-permute-start.26 = (f32[3,2]{1,0:T(4,128)S(1)}, f32[3,2]{1,0:T(4,128)S(1)}, u32[]{:S(2)}, u32[]{:S(2)}) collective-permute-start(f32[3,2]{1,0:T(4,128)S(1)} %fusion.181), channel_id=1, source_target_pairs={{0,4},{4,8},{8,12},{12,0},{1,5},{5,9},{9,13},{13,1},{2,6},{6,10},{... | collective-permute-start | bytes 80 | tf_op jit(solution)/shard_map/ppermute | solution.py:22
  (3 other events, 33.7 us)

commit v2 on v1

--- a/solution.py
+++ b/solution.py
@@ -1,7 +1,11 @@
+import functools
+
 import jax
 import jax.numpy as jnp
 import numpy as np
 from jax import lax
+from jax.experimental import pallas as pl
+from jax.experimental.pallas import tpu as pltpu
 from jax.sharding import PartitionSpec as P
 
 CX = 1
@@ -243,9 +247,461 @@
     return (positions, velocities, energies / bead_total)
 
 
+LANES = 128
+ROWS = 24
+MAX_REPLICATED = 16
+
+
+def split_rows(value):
+    high = value.astype(jnp.bfloat16).astype(jnp.float32)
+    return jnp.concatenate([high, value - high], axis=0).astype(jnp.bfloat16)
+
+
+def joined(value):
+    return value[:ROWS] + value[ROWS:]
+
+
+class Grid:
+    def __init__(self, mesh, slot_count, halo_count):
+        self.gx, self.gy, self.gz = (mesh.shape[a] for a in ("gx", "gy", "gz"))
+        self.domains = self.gx * self.gy * self.gz
+        self.lists = self.gx * self.gy
+        self.blocks = slot_count // LANES
+        self.padded = (self.blocks + 7) // 8 * 8
+        self.dummy = LANES + halo_count
+        self.slots = 2 * self.blocks * LANES
+        sizes = zone_sizes()
+        self.zones = []
+        start = 0
+        for direction, size in zip(zone_list[1:], sizes[1:]):
+            self.zones.append((direction, start, start + size))
+            start += size
+
+    def domain(self, i, j, direction):
+        i = lax.rem(i + direction[0], self.gx) if not isinstance(i, int) else (i + direction[0]) % self.gx
+        j = lax.rem(j + direction[1], self.gy) if not isinstance(j, int) else (j + direction[1]) % self.gy
+        return (i * self.gy + j) * self.gz + direction[2] % self.gz
+
+    def rows_of(self, i, j, direction):
+        row = self.domain(i, j, direction) * 8
+        return pl.ds(row if isinstance(row, int) else pl.multiple_of(row, 8), 8)
+
+
+def lanes_of(shape):
+    return lax.broadcasted_iota(jnp.int32, shape, 1)
+
+
+def take_lanes(source, index):
+    return jnp.take_along_axis(source, index, axis=1, mode="promise_in_bounds")
+
+
+def build_tables(grid, near_ref, far_ref, pair_row, send_row, ids_ref, weight_ref, index_ref, table_ref, zone_ref):
+    blocks = grid.blocks
+    lane = lanes_of((8, LANES))
+    own_code = lanes_of((LANES, LANES)).astype(jnp.float32).astype(jnp.bfloat16)
+    first_code = (lanes_of((LANES, LANES)) + LANES).astype(jnp.float32).astype(jnp.bfloat16)
+    rest_code = (-1 - lanes_of((LANES, LANES))).astype(jnp.float32).astype(jnp.bfloat16)
+    one = jnp.ones((LANES, LANES), jnp.bfloat16)
+    zero = jnp.zeros((LANES, LANES), jnp.bfloat16)
+
+    def send_of(number, row):
+        source = near_ref if number % grid.gz == 0 else far_ref
+        return source[number // grid.gz, pl.ds(send_row + row, 1), :]
+
+    for number in range(grid.lists):
+        i, j = number // grid.gy, number % grid.gy
+        to_x = send_of(grid.domain(i, j, zone_list[0]), 0)
+        rest = jnp.zeros((1, LANES), jnp.float32)
+        for direction, start, stop in grid.zones:
+            row = send_of(grid.domain(i, j, direction), 1)
+            rest = jnp.where((lane[:1] >= start) & (lane[:1] < stop), row, rest)
+        both = jnp.concatenate([to_x, rest] + [jnp.zeros((6, LANES), jnp.float32)], axis=0)
+        index_ref[number] = both.astype(jnp.int32)
+
+    def one_list(number, carry):
+        first = near_ref[number, pl.ds(pair_row, blocks), :]
+        second = near_ref[number, pl.ds(pair_row + blocks, blocks), :]
+        fill = jnp.full((grid.padded - blocks, LANES), float(grid.dummy), jnp.float32)
+        parts = [[first, fill], [second, fill]] if grid.padded > blocks else [[first], [second]]
+        first, second = (jnp.concatenate(p, axis=0) for p in parts)
+        ids_ref[0, number] = first.astype(jnp.int32)
+        ids_ref[1, number] = second.astype(jnp.int32)
+        usable = jnp.where(first < float(grid.dummy), 1.0, 0.0)
+        weight_ref[number] = jnp.where(first == second, 0.5, 1.0) * usable
+        both = index_ref[number].astype(jnp.float32)
+        codes = jnp.concatenate([first, second], axis=0)
+        codes = jnp.where(codes < 2.0 * LANES, codes, 2.0 * LANES - 1.0 - codes)
+        turned = jnp.transpose(jnp.concatenate([codes, both], axis=0))
+        for side in range(2):
+            for block in range(blocks):
+                at = side * grid.padded + block
+                column = jnp.broadcast_to(turned[:, at : at + 1], (LANES, LANES)).astype(jnp.bfloat16)
+                rows = pl.ds((side * blocks + block) * LANES, LANES)
+                for part, code in enumerate((own_code, first_code, rest_code)):
+                    table_ref[number, rows, pl.ds(part * LANES, LANES)] = jnp.where(column == code, one, zero)
+        at = 2 * grid.padded
+        column = jnp.broadcast_to(turned[:, at : at + 1], (LANES, LANES)).astype(jnp.bfloat16)
+        zone_ref[number, :, pl.ds(0, LANES)] = jnp.where(column == own_code, one, zero)
+        column = jnp.broadcast_to(turned[:, at + 1 : at + 2], (LANES, LANES)).astype(jnp.bfloat16)
+        slot = lax.broadcasted_iota(jnp.int32, (LANES, LANES), 0).astype(jnp.float32).astype(jnp.bfloat16)
+        for part, (direction, start, stop) in enumerate(grid.zones):
+            here = (column == own_code) & (slot >= start) & (slot < stop)
+            zone_ref[number, :, pl.ds((part + 1) * LANES, LANES)] = jnp.where(here, one, zero)
+        return carry
+
+    lax.fori_loop(0, grid.lists, one_list, 0)
+
+
+def gather_and_push(grid, number, x_ref, ids_ref, weight_ref, index_ref, ext_ref, push_ref, energy_ref):
+    i, j = lax.div(number, grid.gy), lax.rem(number, grid.gy)
+    lane = lanes_of((8, LANES))
+    cell = (CX, CY, CZ)
+    to_x = jnp.broadcast_to(index_ref[number, pl.ds(0, 1), :], (8, LANES))
+    rest = jnp.broadcast_to(index_ref[number, pl.ds(1, 1), :], (8, LANES))
+    for c in range(3):
+        ext_ref[c, 0] = x_ref[c, grid.rows_of(i, j, (0, 0, 0)), :]
+        shift = float(zone_list[0][c] * cell[c])
+        ext_ref[c, 1] = take_lanes(x_ref[c, grid.rows_of(i, j, zone_list[0]), :], to_x) + shift
+        value = jnp.zeros((8, LANES), jnp.float32)
+        for direction, start, stop in grid.zones:
+            shift = float(direction[c] * cell[c])
+            got = take_lanes(x_ref[c, grid.rows_of(i, j, direction), :], rest) + shift
+            value = jnp.where((lane >= start) & (lane < stop), got, value)
+        ext_ref[c, 2] = value
+    for group in range(grid.padded // 8):
+        sides = []
+        for side in range(2):
+            ids = ids_ref[side, number, pl.ds(8 * group, 8), :]
+            low = ids & (LANES - 1)
+            in_own = ids < LANES
+            in_first = ids < 2 * LANES
+            coords = []
+            for c in range(3):
+                line = []
+                for bead in range(8):
+                    a, b, d = (
+                        take_lanes(jnp.broadcast_to(ext_ref[c, part, pl.ds(bead, 1), :], (8, LANES)), low)
+                        for part in range(3)
+                    )
+                    line.append(jnp.where(in_own, a, jnp.where(in_first, b, d)))
+                coords.append(line)
+            sides.append(coords)
+        weight = weight_ref[number, pl.ds(8 * group, 8), :]
+        scale = weight * (6.0 * strength)
+        energy = None
+        on_second = [[None] * 8 for _ in range(3)]
+        for k in range(8):
+            on_first = [None] * 3
+            for l in range(8):
+                apart = [sides[0][c][k] - sides[1][c][l] for c in range(3)]
+                scaled = apart[0] * apart[0] + apart[1] * apart[1] + apart[2] * apart[2]
+                intersect = jnp.maximum(1.0 - scaled, 0.0)
+                square = intersect * intersect
+                cube = square * intersect
+                energy = cube if energy is None else energy + cube
+                for c in range(3):
+                    pushing = square * apart[c]
+                    on_first[c] = pushing if l == 0 else on_first[c] + pushing
+                    on_second[c][l] = pushing if k == 0 else on_second[c][l] + pushing
+            for c in range(3):
+                row = (8 * group) * ROWS + c * 8 + k
+                push_ref[pl.ds(row, 8, stride=ROWS), :] = on_first[c] * scale
+        for c in range(3):
+            for l in range(8):
+                row = (grid.padded + 8 * group) * ROWS + c * 8 + l
+                push_ref[pl.ds(row, 8, stride=ROWS), :] = -(on_second[c][l] * scale)
+        own_beads = jnp.where(weight == 0.5, 8.0, 0.0)
+        energy_ref[...] += strength * weight * (energy - own_beads)
+
+
+def scatter(grid, number, push_ref, table_ref, force_ref, halo_ref):
+    pieces = []
+    for side in range(2):
+        for block in range(grid.blocks):
+            pieces.append(push_ref[pl.ds((side * grid.padded + block) * ROWS, ROWS), :])
+    pushes = split_rows(jnp.concatenate(pieces, axis=1))
+    sums = joined(jnp.dot(pushes, table_ref[number], preferred_element_type=jnp.float32))
+    row = pl.multiple_of(number * grid.gz * 8, 8)
+    for c in range(3):
+        force_ref[pl.ds(c * grid.domains * 8 + row, 8), :] = sums[8 * c : 8 * c + 8, :LANES]
+    halo_ref[number] = sums[:, LANES:]
+
+
+def pair_forces(grid, x_ref, tables, force_ref, scratch):
+    ids_ref, weight_ref, index_ref, table_ref, zone_ref = tables
+    ext_a, ext_b, push_a, push_b, halo_ref, energy_ref = scratch
+    force_ref[...] = jnp.zeros(force_ref.shape, jnp.float32)
+    energy_ref[...] = jnp.zeros((8, LANES), jnp.float32)
+
+    def forward(number, ext_ref, push_ref):
+        gather_and_push(grid, number, x_ref, ids_ref, weight_ref, index_ref, ext_ref, push_ref, energy_ref)
+
+    def back(number, push_ref):
+        scatter(grid, number, push_ref, table_ref, force_ref, halo_ref)
+
+    forward(0, ext_a, push_a)
+
+    def two(m, carry):
+        back(2 * m, push_a)
+        forward(2 * m + 1, ext_b, push_b)
+        back(2 * m + 1, push_b)
+        forward(2 * m + 2, ext_a, push_a)
+        return carry
+
+    lax.fori_loop(0, grid.lists // 2 - 1, two, 0)
+    back(grid.lists - 2, push_a)
+    forward(grid.lists - 1, ext_b, push_b)
+    back(grid.lists - 1, push_b)
+    for number in range(grid.lists):
+        i, j = number // grid.gy, number % grid.gy
+        halo = halo_ref[number]
+        to_x = joined(
+            jnp.dot(split_rows(halo[:, :LANES]), zone_ref[number, :, pl.ds(0, LANES)], preferred_element_type=jnp.float32)
+        )
+        rest = joined(
+            jnp.dot(
+                split_rows(halo[:, LANES:]),
+                zone_ref[number, :, pl.ds(LANES, len(grid.zones) * LANES)],
+                preferred_element_type=jnp.float32,
+            )
+        )
+        targets = [(zone_list[0], to_x)]
+        for part, (direction, start, stop) in enumerate(grid.zones):
+            targets.append((direction, rest[:, part * LANES : (part + 1) * LANES]))
+        for direction, value in targets:
+            row = grid.domain(i, j, direction) * 8
+            for c in range(3):
+                force_ref[pl.ds(c * grid.domains * 8 + row, 8), :] += value[8 * c : 8 * c + 8]
+    force_ref[pl.ds(3 * grid.domains * 8, 8), :] = energy_ref[...]
+
+
+def start_kernel(grid, layout, near_ref, far_ref, *refs):
+    x_ref, v_ref, rest_ref, flag_ref, ids_ref, weight_ref, index_ref, table_ref, zone_ref, force_ref = refs[:10]
+    scratch = refs[10:]
+    for number in range(grid.domains):
+        source = near_ref if number % grid.gz == 0 else far_ref
+        at = number // grid.gz
+        rows = pl.ds(number * 8, 8)
+        for c in range(3):
+            x_ref[c, rows, :] = source[at, pl.ds(layout["positions"] + 8 * c, 8), :]
+            v_ref[c, rows, :] = source[at, pl.ds(layout["velocities"] + 8 * c, 8), :]
+        flag_ref[rows, :] = source[at, pl.ds(layout["flags"], 8), :]
+    rest_ref[...] = link_length([x_ref[c] for c in range(3)])
+    build_tables(grid, near_ref, far_ref, layout["pairs"], layout["sends"], ids_ref, weight_ref, index_ref, table_ref, zone_ref)
+    pair_forces(grid, x_ref, (ids_ref, weight_ref, index_ref, table_ref, zone_ref), force_ref, scratch)
+
+
+def up(value):
+    return pltpu.roll(value, value.shape[0] - 1, 0)
+
+
+def down(value):
+    return pltpu.roll(value, 1, 0)
+
+
+def dot3(a, b):
+    return a[0] * b[0] + a[1] * b[1] + a[2] * b[2]
+
+
+def links_of(x):
+    return [c - up(c) for c in x]
+
+
+def link_length(x):
+    vectors = links_of(x)
+    return jnp.sqrt(dot3(vectors, vectors))
+
+
+def expand_rows(coupling, before, source):
+    series = source
+    result = source
+    for expansion in range(NORDER):
+        series = before * down(series) + coupling * up(series)
+        result = result + series
+    return result
+
+
+def apply_rows(x, directions, solution):
+    moved = []
+    for c in range(3):
+        shift = directions[c] * (root_half * solution)
+        moved.append(x[c] - shift + down(shift))
+    return moved
+
+
+def constrain_rows(previous, updated, rest, flags):
+    old = links_of(previous)
+    length = jnp.maximum(jnp.sqrt(dot3(old, old)), 0.2)
+    directions = [c / length for c in old]
+    coupling = 0.5 * dot3(directions, [up(c) for c in directions]) * flags * up(flags)
+    before = down(coupling)
+    projected = dot3(directions, links_of(updated))
+    solution = expand_rows(coupling, before, flags * (root_half * (projected - rest)))
+    updated = apply_rows(updated, directions, solution)
+    vectors = links_of(updated)
+    squared = dot3(vectors, vectors)
+    target = jnp.sqrt(jnp.maximum(2.0 * rest * rest - squared, 0.25 * rest * rest))
+    solution = expand_rows(coupling, before, flags * (root_half * (rest - target)))
+    return apply_rows(updated, directions, solution)
+
+
+def total_force(grid, own_ref, got_refs):
+    size = grid.domains * 8
+    total = []
+    for c in range(3):
+        pieces = []
+        for number in range(grid.domains):
+            base, k = number // grid.gz * grid.gz, number % grid.gz
+            value = own_ref[pl.ds(c * size + number * 8, 8), :]
+            for by, ref in enumerate(got_refs, 1):
+                value = value + ref[pl.ds(c * size + (base + (k - by) % grid.gz) * 8, 8), :]
+            pieces.append(value)
+        total.append(jnp.concatenate(pieces, axis=0))
+    return total
+
+
+def energy_row(grid, own_ref, got_refs, v, row, previous):
+    rows = pl.ds(3 * grid.domains * 8, 8)
+    potential = own_ref[rows, :]
+    for ref in got_refs:
+        potential = potential + ref[rows, :]
+    kinetic = 0.5 * dot3(v, v)
+    lane = lanes_of((8, LANES))
+    at = lax.broadcasted_iota(jnp.int32, (8, LANES), 0) == row
+    previous = jnp.where(at & (lane == 0), jnp.sum(potential), previous)
+    return jnp.where(at & (lane == 1), jnp.sum(kinetic), previous)
+
+
+def step_kernel(grid, step, x_ref, v_ref, rest_ref, flag_ref, ids_ref, weight_ref, index_ref, table_ref, zone_ref, energies_ref, own_ref, *refs):
+    got_refs, refs = refs[: grid.gz - 1], refs[grid.gz - 1 :]
+    moved_ref, half_ref, energy_out_ref, force_ref = refs[:4]
+    scratch = refs[4:]
+    force = total_force(grid, own_ref, got_refs)
+    x = [x_ref[c] for c in range(3)]
+    v = [v_ref[c] for c in range(3)]
+    if step > 0:
+        v = [v[c] + (0.5 * time_step) * force[c] for c in range(3)]
+        energy_out_ref[...] = energy_row(grid, own_ref, got_refs, v, step - 1, energies_ref[...])
+    else:
+        energy_out_ref[...] = energies_ref[...]
+    half = [v[c] + (0.5 * time_step) * force[c] for c in range(3)]
+    moved = constrain_rows(x, [x[c] + time_step * half[c] for c in range(3)], rest_ref[...], flag_ref[...])
+    for c in range(3):
+        moved_ref[c] = moved[c]
+        half_ref[c] = (moved[c] - x[c]) / time_step
+    pair_forces(grid, moved_ref, (ids_ref, weight_ref, index_ref, table_ref, zone_ref), force_ref, scratch)
+
+
+def last_kernel(grid, v_ref, energies_ref, own_ref, *refs):
+    got_refs, (speed_ref, energy_out_ref) = refs[: grid.gz - 1], refs[grid.gz - 1 :]
+    force = total_force(grid, own_ref, got_refs)
+    v = [v_ref[c] + (0.5 * time_step) * force[c] for c in range(3)]
+    for c in range(3):
+        speed_ref[c] = v[c][:8]
+    energy_out_ref[...] = energy_row(grid, own_ref, got_refs, v, ITERS - 1, energies_ref[...])
+
+
+def from_ahead(value, steps):
+    names = [a for a, by in zip(("gx", "gy", "gz"), steps) if by]
+    if not names:
+        return value
+    counts = [lax.axis_size(a) for a in names]
+    pairs = []
+    for target in np.ndindex(*counts):
+        source = [(t + by) % n for t, by, n in zip(target, [s for s in steps if s], counts)]
+        pairs.append(tuple(int(np.ravel_multi_index(p, counts)) for p in (source, target)))
+    return lax.ppermute(value, tuple(names), pairs)
+
+
+def replicated(grid, positions, velocities, send_list, pair_list, constraint_flags):
+    clusters = positions.shape[2]
+    sends = jnp.pad(send_list, (0, -send_list.shape[0] % LANES)).reshape(-1, LANES)
+    parts = dict(
+        positions=positions.reshape(ROWS, clusters),
+        velocities=velocities.reshape(ROWS, clusters),
+        flags=jnp.pad(constraint_flags.astype(jnp.float32), ((0, 1), (0, 0))),
+        pairs=pair_list.astype(jnp.float32).reshape(-1, LANES),
+        sends=sends.astype(jnp.float32),
+    )
+    layout, row = {}, 0
+    for name, value in parts.items():
+        layout[name] = row
+        row += value.shape[0]
+    pack = jnp.concatenate(list(parts.values()) + [jnp.zeros((-row % 8, LANES), jnp.float32)], axis=0)
+    near = jnp.stack([from_ahead(pack, (i, j, 0)) for i in range(grid.gx) for j in range(grid.gy)])
+    far = from_ahead(near, (0, 0, 1))
+    f32, i32, b16 = jnp.float32, jnp.int32, jnp.bfloat16
+    n, rows = grid.lists, grid.domains * 8
+    cube = jax.ShapeDtypeStruct((3, rows, LANES), f32)
+    plane = jax.ShapeDtypeStruct((rows, LANES), f32)
+    small = jax.ShapeDtypeStruct((8, LANES), f32)
+    forces = jax.ShapeDtypeStruct((3 * rows + 8, LANES), f32)
+    table_shapes = [
+        jax.ShapeDtypeStruct((2, n, grid.padded, LANES), i32),
+        jax.ShapeDtypeStruct((n, grid.padded, LANES), f32),
+        jax.ShapeDtypeStruct((n, 8, LANES), i32),
+        jax.ShapeDtypeStruct((n, grid.slots, 3 * LANES), b16),
+        jax.ShapeDtypeStruct((n, LANES, len(zone_list) * LANES), b16),
+    ]
+    scratch = [
+        pltpu.VMEM((3, 3, 8, LANES), f32),
+        pltpu.VMEM((3, 3, 8, LANES), f32),
+        pltpu.VMEM((2 * grid.padded * ROWS, LANES), f32),
+        pltpu.VMEM((2 * grid.padded * ROWS, LANES), f32),
+        pltpu.VMEM((n, ROWS, 2 * LANES), f32),
+        pltpu.VMEM((8, LANES), f32),
+    ]
+    params = pltpu.CompilerParams(vmem_limit_bytes=VMEM_LIMIT)
+
+    def call(kernel, shapes, scratch, *values):
+        return pl.pallas_call(kernel, out_shape=shapes, scratch_shapes=scratch, compiler_params=params)(*values)
+
+    x, v, rest, flags, *rest_out = call(
+        functools.partial(start_kernel, grid, layout), [cube, cube, plane, plane] + table_shapes + [forces], scratch, near, far
+    )
+    tables, force = rest_out[:5], rest_out[5]
+    energies = jnp.zeros((8, LANES), f32)
+    for step in range(ITERS):
+        got = [from_ahead(force, (0, 0, by)) for by in range(1, grid.gz)]
+        x, v, energies, force = call(
+            functools.partial(step_kernel, grid, step),
+            [cube, cube, small, forces],
+            scratch,
+            x, v, rest, flags, *tables, energies, force, *got,
+        )
+    got = [from_ahead(force, (0, 0, by)) for by in range(1, grid.gz)]
+    speed, energies = call(
+        functools.partial(last_kernel, grid), [jax.ShapeDtypeStruct((3, 8, LANES), f32), small], [], v, energies, force, *got
+    )
+    bead_total = 8 * clusters * grid.domains
+    return (x[:, :8], speed, energies[:ITERS, :2] / bead_total)
+
+
+def can_replicate(grid, positions, send_list, pair_list):
+    return (
+        grid.domains <= MAX_REPLICATED
+        and grid.lists % 2 == 0
+        and grid.gz == 2
+        and positions.shape[2] == LANES
+        and zone_sizes()[0] == LANES
+        and pair_list.shape[1] % LANES == 0
+        and sum(zone_sizes()) == send_list.shape[0]
+        and send_list.shape[0] - LANES < LANES
+    )
+
+
+VMEM_LIMIT = 58 * 1024 * 1024
+
+
 def solution(mesh):
+    def on_any(positions, velocities, send_list, pair_list, constraint_flags):
+        grid = Grid(mesh, pair_list.shape[1], send_list.shape[0])
+        if can_replicate(grid, positions, send_list, pair_list):
+            return replicated(grid, positions, velocities, send_list, pair_list, constraint_flags)
+        return on_device(positions, velocities, send_list, pair_list, constraint_flags)
+
     return jax.shard_map(
-        on_device,
+        on_any,
         mesh=mesh,
         in_specs=(
             P(None, None, ("runs", "gx", "gy", "gz")),

time: 127 us -> 114 us (0.90)
  Pallas kernels: 0 us -> 73 us
  waiting for transfers between devices: 57.1 us -> 12.4 us
  matrix products: 20.1 us -> 0 us
  starting transfers between devices: 29.9 us -> 17.9 us
  between operations: 5.33 us -> 0.74 us
  other arithmetic: 6.97 us -> 2.78 us
    pallas_call x0 -> x5, Pallas kernels: none -> 73 us  [call(): pl.pallas_call(kernel, out_shape=shapes, scratch_shapes=scratch, compiler...]
    ppermute x29 -> x12, waiting for transfers between devices: 57.1 us -> 12.4 us  [from_ahead(): return lax.ppermute(value, tuple(names), pairs)]
    dot_general x24 -> x0, matrix products: 20.1 us -> none  [the longest x4 4.36 us: domain_forces(): lax.dot_general(on_first, tables[0], contract, precision=lax.Precision.HI...]
    ppermute x29 -> x12, starting transfers between devices: 29.9 us -> 17.9 us  [from_ahead(): return lax.ppermute(value, tuple(names), pairs)]
    slice x93 -> x1, local copies, waits for them, and re-layouts: 5.95 us -> 1.31 us  [replicated(): return (x[:, :8], speed, energies[:ITERS, :2] / bead_total)]
    reduce_sum x21 -> x0, other arithmetic: 3.82 us -> none  [the longest x4 2.02 us: domain_forces(): on_first = jnp.sum(pushing, axis=2).reshape(24, slot_count)]
    unnamed x13 -> x20, local copies, waits for them, and re-layouts: 0.7 us -> 3.58 us
    convert_element_type x1 -> x3, other arithmetic: 0.01 us -> 2.09 us  [the longest x1 0.72 us: replicated(): pair_list.astype(jnp.float32).reshape(-1, LANES)]
  transfers between devices with their start and end apart: 29 -> 12, of which waited for: 29 -> 8; matrix products, arithmetic and copies ran while one was open for 2% -> 1% of each run, Pallas kernels for 0% -> 0%
where the time goes in v2:
time: 114 us
  Pallas kernels  73 us (64%)
  starting transfers between devices  17.9 us (16%)
  waiting for transfers between devices  12.4 us (11%)
  local copies, waits for them, and re-layouts  6.98 us (6%)
  other arithmetic  2.78 us (2%)
    pallas_call x5, Pallas kernels, call(): pl.pallas_call(kernel, out_shape=shapes, scratch_shapes=scratch, compiler...  73 us
    ppermute x12, starting transfers between devices, from_ahead(): return lax.ppermute(value, tuple(names), pairs)  17.9 us
    ppermute x12, waiting for transfers between devices, from_ahead(): return lax.ppermute(value, tuple(names), pairs)  12.4 us
    unnamed x20, local copies, waits for them, and re-layouts  3.58 us
  transfers between devices with their start and end apart: 12, of which 8 were waited for; matrix products, arithmetic and copies ran while one was open for 1% of the time, Pallas kernels for 0%

profile of v2, /device:TPU:0, one launch (start us, length us, event | category | flops | bytes accessed | tf_op | source)
XLA Modules:
  0.0 113.9 jit_solution(7441214365155498949)
XLA Ops:
  0.6 0.7 convert_bitcast_fusion
  1.3 0.7 convert_element_type.14
  2.0 0.7 convert_element_type.15
  2.8 1.4 %concatenate.3 = f32[88,128]{1,0:T(8,128)S(1)} concatenate(f32[24,128]{1,0:T(8,128)} %bitcast.20, f32[24,128]{1,0:T(8,128)} %bitcast.21, f32[8,128]{1,0:T(8,128)S(1)} %pad.8, f32[28,128]{1,0:T(8,128)S(1)} %reshape.19, f32[2,128]{1,0:T(2,128)S(1)} %convert_bitcast_fusion, f32[2,128]{1,0:T(2,128)S(1)} %broadcast_in_dim.6), dimensions={0} | concatenate | bytes 90112 | tf_op jit(solution)/shard_map/concatenate | solution.py:630
  4.2 4.0 %collective-permute-start.6 = (f32[88,128]{1,0:T(8,128)S(1)}, f32[88,128]{1,0:T(8,128)S(1)}, u32[]{:S(2)}, u32[]{:S(2)}) collective-permute-start(f32[88,128]{1,0:T(8,128)S(1)} %concatenate.3), channel_id=1, source_target_pairs={{14,0},{12,2},{2,4},{0,6},{6,8},{4,10},{10,12},{8,14},{15,1},{13,3... | collective-permute-start | bytes 135176 | tf_op jit(solution)/shard_map/ppermute | solution.py:613
  8.2 1.6 %collective-permute-start.5 = (f32[88,128]{1,0:T(8,128)S(1)}, f32[88,128]{1,0:T(8,128)S(1)}, u32[]{:S(2)}, u32[]{:S(2)}) collective-permute-start(f32[88,128]{1,0:T(8,128)S(1)} %concatenate.3), channel_id=1, source_target_pairs={{12,0},{0,4},{4,8},{8,12},{13,1},{1,5},{5,9},{9,13},{14,2},{2,6},{... | collective-permute-start | bytes 135176 | tf_op jit(solution)/shard_map/ppermute | solution.py:613
  9.8 1.1 collective-permute-start.4
  10.9 1.8 %collective-permute-start.3 = (f32[88,128]{1,0:T(8,128)S(1)}, f32[88,128]{1,0:T(8,128)S(1)}, u32[]{:S(2)}, u32[]{:S(2)}) collective-permute-start(f32[88,128]{1,0:T(8,128)S(1)} %concatenate.3), channel_id=1, source_target_pairs={{8,0},{12,4},{0,8},{4,12},{9,1},{13,5},{1,9},{5,13},{10,2},{14,6},... | collective-permute-start | bytes 135176 | tf_op jit(solution)/shard_map/ppermute | solution.py:613
  12.7 1.5 %collective-permute-start = (f32[88,128]{1,0:T(8,128)S(1)}, f32[88,128]{1,0:T(8,128)S(1)}, u32[]{:S(2)}, u32[]{:S(2)}) collective-permute-start(f32[88,128]{1,0:T(8,128)S(1)} %concatenate.3), channel_id=1, source_target_pairs={{2,0},{0,2},{3,1},{1,3},{6,4},{4,6},{7,5},{5,7},{10,8},{8,10},{11,... | collective-permute-start | bytes 135176 | tf_op jit(solution)/shard_map/ppermute | solution.py:613
  14.2 2.6 %collective-permute-done = f32[88,128]{1,0:T(8,128)S(1)} collective-permute-done((f32[88,128]{1,0:T(8,128)S(1)}, f32[88,128]{1,0:T(8,128)S(1)}, u32[]{:S(2)}, u32[]{:S(2)}) %collective-permute-start) | collective-permute-done | bytes 45088 | tf_op jit(solution)/shard_map/ppermute | solution.py:613
  16.8 2.5 %collective-permute-start.1 = (f32[88,128]{1,0:T(8,128)S(1)}, f32[88,128]{1,0:T(8,128)S(1)}, u32[]{:S(2)}, u32[]{:S(2)}) collective-permute-start(f32[88,128]{1,0:T(8,128)S(1)} %concatenate.3), channel_id=1, source_target_pairs={{4,0},{8,4},{12,8},{0,12},{5,1},{9,5},{13,9},{1,13},{6,2},{10,6},{... | collective-permute-start | bytes 135176 | tf_op jit(solution)/shard_map/ppermute | solution.py:613
  19.2 1.7 %collective-permute-done.1 = f32[88,128]{1,0:T(8,128)S(1)} collective-permute-done((f32[88,128]{1,0:T(8,128)S(1)}, f32[88,128]{1,0:T(8,128)S(1)}, u32[]{:S(2)}, u32[]{:S(2)}) %collective-permute-start.1) | collective-permute-done | bytes 45088 | tf_op jit(solution)/shard_map/ppermute | solution.py:613
  20.9 4.8 %collective-permute-start.2 = (f32[88,128]{1,0:T(8,128)S(1)}, f32[88,128]{1,0:T(8,128)S(1)}, u32[]{:S(2)}, u32[]{:S(2)}) collective-permute-start(f32[88,128]{1,0:T(8,128)S(1)} %concatenate.3), channel_id=1, source_target_pairs={{6,0},{4,2},{10,4},{8,6},{14,8},{12,10},{2,12},{0,14},{7,1},{5,3},... | collective-permute-start | bytes 135176 | tf_op jit(solution)/shard_map/ppermute | solution.py:613
  25.8 1.7 %collective-permute-done.2 = f32[88,128]{1,0:T(8,128)S(1)} collective-permute-done((f32[88,128]{1,0:T(8,128)S(1)}, f32[88,128]{1,0:T(8,128)S(1)}, u32[]{:S(2)}, u32[]{:S(2)}) %collective-permute-start.2) | collective-permute-done | bytes 45088 | tf_op jit(solution)/shard_map/ppermute | solution.py:613
  27.7 1.7 %collective-permute-done.7.far_ref = f32[8,88,128]{2,1,0:T(8,128)S(1)} collective-permute-done((f32[8,88,128]{2,1,0:T(8,128)S(1)}, f32[8,88,128]{2,1,0:T(8,128)S(1)}, u32[]{:S(2)}, u32[]{:S(2)}) %collective-permute-start.7) | collective-permute-done | bytes 360480 | tf_op jit(solution)/shard_map/ppermute | solution.py:613
  29.3 0.8 copy-done.1
  30.1 20.5 %shard_map.76 = (f32[3,128,128]{2,1,0:T(8,128)}, f32[3,128,128]{2,1,0:T(8,128)}, f32[128,128]{1,0:T(8,128)}, f32[128,128]{1,0:T(8,128)}, s32[2,8,16,128]{3,2,1,0...) custom-call(f32[8,88,128]{2,1,0:T(8,128)} %copy-done, ...), custom_call_target="tpu_custom_call" | custom-call | tf_op jit(solution)/shard_map/pallas_call | solution.py:657
  50.7 1.5 %collective-permute-done.8.refs_0_ = f32[392,128]{1,0:T(8,128)S(1)} collective-permute-done((f32[392,128]{1,0:T(8,128)}, f32[392,128]{1,0:T(8,128)S(1)}, u32[]{:S(2)}, u32[]{:S(2)}) %collective-permute-start.8) | collective-permute-done | bytes 200736 | tf_op jit(solution)/shard_map/ppermute | solution.py:613
  52.2 0.6 broadcast_in_dim.7.energies_ref
  52.9 16.8 %shard_map.77 = (f32[3,128,128]{2,1,0:T(8,128)}, f32[3,128,128]{2,1,0:T(8,128)}, f32[8,128]{1,0:T(8,128)}, f32[392,128]{1,0:T(8,128)}) custom-call(f32[3,128,128]{2,1,0:T(8,128)} %get-tuple-element.27.x_ref, f32[3,128,128]{2,1,0:T(8,128)} %get-tuple-element.28.v_ref, f32[128,128]{1,0:T(8,128)} %get-tuple-element.29.rest_ref, ...), custom_call_target="tpu_custom_call" | custom-call | tf_op jit(solution)/shard_map/pallas_call | solution.py:657
  69.9 1.5 %collective-permute-done.9.refs_0_ = f32[392,128]{1,0:T(8,128)S(1)} collective-permute-done((f32[392,128]{1,0:T(8,128)}, f32[392,128]{1,0:T(8,128)S(1)}, u32[]{:S(2)}, u32[]{:S(2)}) %collective-permute-start.9) | collective-permute-done | bytes 200736 | tf_op jit(solution)/shard_map/ppermute | solution.py:613
  71.4 0.7 copy-done.4
  72.1 17.0 %shard_map.78 = (f32[3,128,128]{2,1,0:T(8,128)}, f32[3,128,128]{2,1,0:T(8,128)}, f32[8,128]{1,0:T(8,128)}, f32[392,128]{1,0:T(8,128)}) custom-call(f32[3,128,128]{2,1,0:T(8,128)} %get-tuple-element.37.x_ref, f32[3,128,128]{2,1,0:T(8,128)} %get-tuple-element.38.v_ref, f32[128,128]{1,0:T(8,128)} %get-tuple-element.29.rest_ref, ...), custom_call_target="tpu_custom_call" | custom-call | tf_op jit(solution)/shard_map/pallas_call | solution.py:657
  89.2 1.5 %collective-permute-done.10.refs_0_ = f32[392,128]{1,0:T(8,128)S(1)} collective-permute-done((f32[392,128]{1,0:T(8,128)}, f32[392,128]{1,0:T(8,128)S(1)}, u32[]{:S(2)}, u32[]{:S(2)}) %collective-permute-start.10) | collective-permute-done | bytes 200736 | tf_op jit(solution)/shard_map/ppermute | solution.py:613
  90.8 0.7 copy-done.2
  91.5 16.9 %shard_map.79 = (f32[3,128,128]{2,1,0:T(8,128)}, f32[3,128,128]{2,1,0:T(8,128)}, f32[8,128]{1,0:T(8,128)}, f32[392,128]{1,0:T(8,128)}) custom-call(f32[3,128,128]{2,1,0:T(8,128)} %get-tuple-element.41.x_ref, f32[3,128,128]{2,1,0:T(8,128)} %get-tuple-element.42.v_ref, f32[128,128]{1,0:T(8,128)} %get-tuple-element.29.rest_ref, ...), custom_call_target="tpu_custom_call" | custom-call | tf_op jit(solution)/shard_map/pallas_call | solution.py:657
  108.4 1.3 %slice.6 = f32[3,8,128]{2,1,0:T(8,128)} slice(f32[3,128,128]{2,1,0:T(8,128)} %get-tuple-element.45), slice={[0:3], [0:8], [0:128]} | slice | bytes 24576 | tf_op jit(solution)/shard_map/slice | solution.py:677
  109.8 0.2 collective-permute-done.11.refs_0_
  110.0 0.7 copy-done.5
  110.6 1.9 %shard_map.80 = (f32[3,8,128]{2,1,0:T(8,128)}, f32[8,128]{1,0:T(8,128)}) custom-call(f32[3,128,128]{2,1,0:T(8,128)} %get-tuple-element.46.v_ref, f32[8,128]{1,0:T(8,128)} %get-tuple-element.47.energies_ref, f32[392,128]{1,0:T(8,128)} %get-tuple-element.48.own_ref, f32[392,128]{1,0:T(8,128)} %copy-done.5), custom_call_target="tpu_custom_call" | custom-call | tf_op jit(solution)/shard_map/pallas_call | solution.py:657
  112.5 0.7 slice_multiply_fusion
  113.2 0.7 copy.8
  (28 shorter events, 0.8 us)
Async XLA Ops:
  4.2 23.3 %collective-permute-start.6 = (f32[88,128]{1,0:T(8,128)S(1)}, f32[88,128]{1,0:T(8,128)S(1)}, u32[]{:S(2)}, u32[]{:S(2)}) collective-permute-start(f32[88,128]{1,0:T(8,128)S(1)} %concatenate.3), channel_id=1, source_target_pairs={{14,0},{12,2},{2,4},{0,6},{6,8},{4,10},{10,12},{8,14},{15,1},{13,3... | collective-permute-start | bytes 135176 | tf_op jit(solution)/shard_map/ppermute | solution.py:613
  8.2 19.3 %collective-permute-start.5 = (f32[88,128]{1,0:T(8,128)S(1)}, f32[88,128]{1,0:T(8,128)S(1)}, u32[]{:S(2)}, u32[]{:S(2)}) collective-permute-start(f32[88,128]{1,0:T(8,128)S(1)} %concatenate.3), channel_id=1, source_target_pairs={{12,0},{0,4},{4,8},{8,12},{13,1},{1,5},{5,9},{9,13},{14,2},{2,6},{... | collective-permute-start | bytes 135176 | tf_op jit(solution)/shard_map/ppermute | solution.py:613
  9.8 17.7 %collective-permute-start.4 = (f32[88,128]{1,0:T(8,128)S(1)}, f32[88,128]{1,0:T(8,128)S(1)}, u32[]{:S(2)}, u32[]{:S(2)}) collective-permute-start(f32[88,128]{1,0:T(8,128)S(1)} %concatenate.3), channel_id=1, source_target_pairs={{10,0},{8,2},{14,4},{12,6},{2,8},{0,10},{6,12},{4,14},{11,1},{9,3}... | collective-permute-start | bytes 135176 | tf_op jit(solution)/shard_map/ppermute | solution.py:613
  10.9 16.6 %collective-permute-start.3 = (f32[88,128]{1,0:T(8,128)S(1)}, f32[88,128]{1,0:T(8,128)S(1)}, u32[]{:S(2)}, u32[]{:S(2)}) collective-permute-start(f32[88,128]{1,0:T(8,128)S(1)} %concatenate.3), channel_id=1, source_target_pairs={{8,0},{12,4},{0,8},{4,12},{9,1},{13,5},{1,9},{5,13},{10,2},{14,6},... | collective-permute-start | bytes 135176 | tf_op jit(solution)/shard_map/ppermute | solution.py:613
  12.7 4.1 %collective-permute-start = (f32[88,128]{1,0:T(8,128)S(1)}, f32[88,128]{1,0:T(8,128)S(1)}, u32[]{:S(2)}, u32[]{:S(2)}) collective-permute-start(f32[88,128]{1,0:T(8,128)S(1)} %concatenate.3), channel_id=1, source_target_pairs={{2,0},{0,2},{3,1},{1,3},{6,4},{4,6},{7,5},{5,7},{10,8},{8,10},{11,... | collective-permute-start | bytes 135176 | tf_op jit(solution)/shard_map/ppermute | solution.py:613
  16.8 4.2 %collective-permute-start.1 = (f32[88,128]{1,0:T(8,128)S(1)}, f32[88,128]{1,0:T(8,128)S(1)}, u32[]{:S(2)}, u32[]{:S(2)}) collective-permute-start(f32[88,128]{1,0:T(8,128)S(1)} %concatenate.3), channel_id=1, source_target_pairs={{4,0},{8,4},{12,8},{0,12},{5,1},{9,5},{13,9},{1,13},{6,2},{10,6},{... | collective-permute-start | bytes 135176 | tf_op jit(solution)/shard_map/ppermute | solution.py:613
  20.9 6.5 %collective-permute-start.2 = (f32[88,128]{1,0:T(8,128)S(1)}, f32[88,128]{1,0:T(8,128)S(1)}, u32[]{:S(2)}, u32[]{:S(2)}) collective-permute-start(f32[88,128]{1,0:T(8,128)S(1)} %concatenate.3), channel_id=1, source_target_pairs={{6,0},{4,2},{10,4},{8,6},{14,8},{12,10},{2,12},{0,14},{7,1},{5,3},... | collective-permute-start | bytes 135176 | tf_op jit(solution)/shard_map/ppermute | solution.py:613
  27.6 1.8 %copy-start = (f32[8,88,128]{2,1,0:T(8,128)}, f32[8,88,128]{2,1,0:T(8,128)S(1)}, u32[]{:S(2)}) copy-start(f32[8,88,128]{2,1,0:T(8,128)S(1)} %bitcast_dynamic-update-slice_fusion.near_ref) | copy-start | bytes 1081348
  27.6 1.7 %collective-permute-start.7 = (f32[8,88,128]{2,1,0:T(8,128)S(1)}, f32[8,88,128]{2,1,0:T(8,128)S(1)}, u32[]{:S(2)}, u32[]{:S(2)}) collective-permute-start(f32[8,88,128]{2,1,0:T(8,128)S(1)} %bitcast_dynamic-update-slice_fusion.near_ref), channel_id=1, source_target_pairs={{1,0},{0,1},{3,2},{2,3},{5,4},{4,5},{7,6},{6,7},{9,8},{8,9},{11,10... | collective-permute-start | bytes 1081352 | tf_op jit(solution)/shard_map/ppermute | solution.py:613
  29.3 0.8 copy-start.1
  50.6 1.7 %collective-permute-start.8 = (f32[392,128]{1,0:T(8,128)}, f32[392,128]{1,0:T(8,128)S(1)}, u32[]{:S(2)}, u32[]{:S(2)}) collective-permute-start(f32[392,128]{1,0:T(8,128)} %get-tuple-element.36.own_ref), channel_id=1, source_target_pairs={{1,0},{0,1},{3,2},{2,3},{5,4},{4,5},{7,6},{6,7},{9,8},{8,9},{11,10... | collective-permute-start | bytes 602120 | tf_op jit(solution)/shard_map/ppermute | solution.py:613
  52.2 0.7 copy-start.3
  69.7 1.7 %collective-permute-start.9 = (f32[392,128]{1,0:T(8,128)}, f32[392,128]{1,0:T(8,128)S(1)}, u32[]{:S(2)}, u32[]{:S(2)}) collective-permute-start(f32[392,128]{1,0:T(8,128)} %get-tuple-element.40.own_ref), channel_id=1, source_target_pairs={{1,0},{0,1},{3,2},{2,3},{5,4},{4,5},{7,6},{6,7},{9,8},{8,9},{11,10... | collective-permute-start | bytes 602120 | tf_op jit(solution)/shard_map/ppermute | solution.py:613
  71.4 0.7 copy-start.4
  89.1 1.7 %collective-permute-start.10 = (f32[392,128]{1,0:T(8,128)}, f32[392,128]{1,0:T(8,128)S(1)}, u32[]{:S(2)}, u32[]{:S(2)}) collective-permute-start(f32[392,128]{1,0:T(8,128)} %get-tuple-element.44.own_ref), channel_id=1, source_target_pairs={{1,0},{0,1},{3,2},{2,3},{5,4},{4,5},{7,6},{6,7},{9,8},{8,9},{11,10... | collective-permute-start | bytes 602120 | tf_op jit(solution)/shard_map/ppermute | solution.py:613
  90.8 0.7 copy-start.2
  108.3 1.7 %collective-permute-start.11 = (f32[392,128]{1,0:T(8,128)}, f32[392,128]{1,0:T(8,128)S(1)}, u32[]{:S(2)}, u32[]{:S(2)}) collective-permute-start(f32[392,128]{1,0:T(8,128)} %get-tuple-element.48.own_ref), channel_id=1, source_target_pairs={{1,0},{0,1},{3,2},{2,3},{5,4},{4,5},{7,6},{6,7},{9,8},{8,9},{11,10... | collective-permute-start | bytes 602120 | tf_op jit(solution)/shard_map/ppermute | solution.py:613
  110.0 0.7 copy-start.5

commit v3 on v2

--- a/solution.py
+++ b/solution.py
@@ -690,7 +690,7 @@
     )
 
 
-VMEM_LIMIT = 58 * 1024 * 1024
+VMEM_LIMIT = 16 * 1024 * 1024
 
 
 def solution(mesh):

time: 114 us -> 74.7 us (0.66)
  Pallas kernels: 73 us -> 38.2 us
  local copies, waits for them, and re-layouts: 6.98 us -> 2.76 us
    pallas_call x5, Pallas kernels: 73 us -> 38.2 us  [call(): pl.pallas_call(kernel, out_shape=shapes, scratch_shapes=scratch, compiler...]
    unnamed x20 -> x8, local copies, waits for them, and re-layouts: 3.58 us -> 0.68 us
where the time goes in v3:
time: 74.7 us; the launch traced here: 74.3 us
  Pallas kernels  38.2 us (51%)
  starting transfers between devices  18.2 us (24%)
  waiting for transfers between devices  12.3 us (16%)
  local copies, waits for them, and re-layouts  2.76 us (4%)
  other arithmetic  2.09 us (3%)
  between operations  0.75 us (1%)
    pallas_call x5, Pallas kernels, call(): pl.pallas_call(kernel, out_shape=shapes, scratch_shapes=scratch, compiler...  38.2 us
    ppermute x12, starting transfers between devices, from_ahead(): return lax.ppermute(value, tuple(names), pairs)  18.2 us
    ppermute x12, waiting for transfers between devices, from_ahead(): return lax.ppermute(value, tuple(names), pairs)  12.3 us
  transfers between devices with their start and end apart: 12, of which 8 were waited for; matrix products, arithmetic and copies ran while one was open for 1% of the time, Pallas kernels for 0%

profile of v3, /device:TPU:0, one launch (start us, length us, event | category | flops | bytes accessed | tf_op | source)
XLA Modules:
  0.0 74.3 jit_solution(7687737015385313622)
XLA Ops:
  0.6 0.7 convert_bitcast_fusion
  1.3 0.7 convert_element_type.14
  2.0 0.7 convert_element_type.15
  2.8 1.4 %concatenate.3 = f32[88,128]{1,0:T(8,128)S(1)} concatenate(f32[24,128]{1,0:T(8,128)} %bitcast.20, f32[24,128]{1,0:T(8,128)} %bitcast.21, f32[8,128]{1,0:T(8,128)S(1)} %pad.8, f32[28,128]{1,0:T(8,128)S(1)} %reshape.19, f32[2,128]{1,0:T(2,128)S(1)} %convert_bitcast_fusion, f32[2,128]{1,0:T(2,128)S(1)} %broadcast_in_dim.6), dimensions={0} | concatenate | bytes 90112 | tf_op jit(solution)/shard_map/concatenate | solution.py:630
  4.2 4.0 %collective-permute-start.6 = (f32[88,128]{1,0:T(8,128)S(1)}, f32[88,128]{1,0:T(8,128)S(1)}, u32[]{:S(2)}, u32[]{:S(2)}) collective-permute-start(f32[88,128]{1,0:T(8,128)S(1)} %concatenate.3), channel_id=1, source_target_pairs={{14,0},{12,2},{2,4},{0,6},{6,8},{4,10},{10,12},{8,14},{15,1},{13,3... | collective-permute-start | bytes 135176 | tf_op jit(solution)/shard_map/ppermute | solution.py:613
  8.2 1.6 %collective-permute-start.5 = (f32[88,128]{1,0:T(8,128)S(1)}, f32[88,128]{1,0:T(8,128)S(1)}, u32[]{:S(2)}, u32[]{:S(2)}) collective-permute-start(f32[88,128]{1,0:T(8,128)S(1)} %concatenate.3), channel_id=1, source_target_pairs={{12,0},{0,4},{4,8},{8,12},{13,1},{1,5},{5,9},{9,13},{14,2},{2,6},{... | collective-permute-start | bytes 135176 | tf_op jit(solution)/shard_map/ppermute | solution.py:613
  9.8 1.1 %collective-permute-start.4 = (f32[88,128]{1,0:T(8,128)S(1)}, f32[88,128]{1,0:T(8,128)S(1)}, u32[]{:S(2)}, u32[]{:S(2)}) collective-permute-start(f32[88,128]{1,0:T(8,128)S(1)} %concatenate.3), channel_id=1, source_target_pairs={{10,0},{8,2},{14,4},{12,6},{2,8},{0,10},{6,12},{4,14},{11,1},{9,3}... | collective-permute-start | bytes 135176 | tf_op jit(solution)/shard_map/ppermute | solution.py:613
  10.9 1.8 %collective-permute-start.3 = (f32[88,128]{1,0:T(8,128)S(1)}, f32[88,128]{1,0:T(8,128)S(1)}, u32[]{:S(2)}, u32[]{:S(2)}) collective-permute-start(f32[88,128]{1,0:T(8,128)S(1)} %concatenate.3), channel_id=1, source_target_pairs={{8,0},{12,4},{0,8},{4,12},{9,1},{13,5},{1,9},{5,13},{10,2},{14,6},... | collective-permute-start | bytes 135176 | tf_op jit(solution)/shard_map/ppermute | solution.py:613
  12.7 1.5 %collective-permute-start = (f32[88,128]{1,0:T(8,128)S(1)}, f32[88,128]{1,0:T(8,128)S(1)}, u32[]{:S(2)}, u32[]{:S(2)}) collective-permute-start(f32[88,128]{1,0:T(8,128)S(1)} %concatenate.3), channel_id=1, source_target_pairs={{2,0},{0,2},{3,1},{1,3},{6,4},{4,6},{7,5},{5,7},{10,8},{8,10},{11,... | collective-permute-start | bytes 135176 | tf_op jit(solution)/shard_map/ppermute | solution.py:613
  14.2 2.6 %collective-permute-done = f32[88,128]{1,0:T(8,128)S(1)} collective-permute-done((f32[88,128]{1,0:T(8,128)S(1)}, f32[88,128]{1,0:T(8,128)S(1)}, u32[]{:S(2)}, u32[]{:S(2)}) %collective-permute-start) | collective-permute-done | bytes 45088 | tf_op jit(solution)/shard_map/ppermute | solution.py:613
  16.8 2.5 %collective-permute-start.1 = (f32[88,128]{1,0:T(8,128)S(1)}, f32[88,128]{1,0:T(8,128)S(1)}, u32[]{:S(2)}, u32[]{:S(2)}) collective-permute-start(f32[88,128]{1,0:T(8,128)S(1)} %concatenate.3), channel_id=1, source_target_pairs={{4,0},{8,4},{12,8},{0,12},{5,1},{9,5},{13,9},{1,13},{6,2},{10,6},{... | collective-permute-start | bytes 135176 | tf_op jit(solution)/shard_map/ppermute | solution.py:613
  19.2 1.7 %collective-permute-done.1 = f32[88,128]{1,0:T(8,128)S(1)} collective-permute-done((f32[88,128]{1,0:T(8,128)S(1)}, f32[88,128]{1,0:T(8,128)S(1)}, u32[]{:S(2)}, u32[]{:S(2)}) %collective-permute-start.1) | collective-permute-done | bytes 45088 | tf_op jit(solution)/shard_map/ppermute | solution.py:613
  20.9 4.8 %collective-permute-start.2 = (f32[88,128]{1,0:T(8,128)S(1)}, f32[88,128]{1,0:T(8,128)S(1)}, u32[]{:S(2)}, u32[]{:S(2)}) collective-permute-start(f32[88,128]{1,0:T(8,128)S(1)} %concatenate.3), channel_id=1, source_target_pairs={{6,0},{4,2},{10,4},{8,6},{14,8},{12,10},{2,12},{0,14},{7,1},{5,3},... | collective-permute-start | bytes 135176 | tf_op jit(solution)/shard_map/ppermute | solution.py:613
  25.8 1.7 %collective-permute-done.2 = f32[88,128]{1,0:T(8,128)S(1)} collective-permute-done((f32[88,128]{1,0:T(8,128)S(1)}, f32[88,128]{1,0:T(8,128)S(1)}, u32[]{:S(2)}, u32[]{:S(2)}) %collective-permute-start.2) | collective-permute-done | bytes 45088 | tf_op jit(solution)/shard_map/ppermute | solution.py:613
  27.5 0.0 collective-permute-done.5
  27.6 0.1 collective-permute-start.7
  27.7 1.7 %collective-permute-done.7.far_ref = f32[8,88,128]{2,1,0:T(8,128)S(1)} collective-permute-done((f32[8,88,128]{2,1,0:T(8,128)S(1)}, f32[8,88,128]{2,1,0:T(8,128)S(1)}, u32[]{:S(2)}, u32[]{:S(2)}) %collective-permute-start.7) | collective-permute-done | bytes 360480 | tf_op jit(solution)/shard_map/ppermute | solution.py:613
  29.3 13.0 %shard_map.76 = (f32[3,128,128]{2,1,0:T(8,128)S(1)}, f32[3,128,128]{2,1,0:T(8,128)S(1)}, f32[128,128]{1,0:T(8,128)S(1)}, f32[128,128]{1,0:T(8,128)S(1)}, s32[2,8...) custom-call(f32[8,88,128]{2,1,0:T(8,128)S(1)} %bitcast_dynamic-updat, ...), custom_call_target="tpu_custom_call" | custom-call | tf_op jit(solution)/shard_map/pallas_call | solution.py:657
  42.3 0.2 collective-permute-start.8
  42.6 1.3 %collective-permute-done.8.refs_0_ = f32[392,128]{1,0:T(8,128)S(1)} collective-permute-done((f32[392,128]{1,0:T(8,128)S(1)}, f32[392,128]{1,0:T(8,128)S(1)}, u32[]{:S(2)}, u32[]{:S(2)}) %collective-permute-start.8) | collective-permute-done | bytes 200736 | tf_op jit(solution)/shard_map/ppermute | solution.py:613
  43.9 8.1 %shard_map.77 = (f32[3,128,128]{2,1,0:T(8,128)S(1)}, f32[3,128,128]{2,1,0:T(8,128)S(1)}, f32[8,128]{1,0:T(8,128)S(1)}, f32[392,128]{1,0:T(8,128)S(1)}) custom-call(f32[3,128,128]{2,1,0:T(8,128)S(1)} %get-tuple-element.27.x_ref, f32[3,128,128]{2,1,0:T(8,128)S(1)} %get-tuple-element.28.v_ref, f32[128,128]{1,0:T(8,128)S(1)} %get-tuple-element.29.rest_ref, ...), custom_call_target="tpu_custom_call" | custom-call | tf_op jit(solution)/shard_map/pallas_call | solution.py:657
  52.0 0.2 collective-permute-start.9
  52.2 1.3 %collective-permute-done.9.refs_0_ = f32[392,128]{1,0:T(8,128)S(1)} collective-permute-done((f32[392,128]{1,0:T(8,128)S(1)}, f32[392,128]{1,0:T(8,128)S(1)}, u32[]{:S(2)}, u32[]{:S(2)}) %collective-permute-start.9) | collective-permute-done | bytes 200736 | tf_op jit(solution)/shard_map/ppermute | solution.py:613
  53.5 8.3 %shard_map.78 = (f32[3,128,128]{2,1,0:T(8,128)S(1)}, f32[3,128,128]{2,1,0:T(8,128)S(1)}, f32[8,128]{1,0:T(8,128)S(1)}, f32[392,128]{1,0:T(8,128)S(1)}) custom-call(f32[3,128,128]{2,1,0:T(8,128)S(1)} %get-tuple-element.37.x_ref, f32[3,128,128]{2,1,0:T(8,128)S(1)} %get-tuple-element.38.v_ref, f32[128,128]{1,0:T(8,128)S(1)} %get-tuple-element.29.rest_ref, ...), custom_call_target="tpu_custom_call" | custom-call | tf_op jit(solution)/shard_map/pallas_call | solution.py:657
  61.8 0.2 collective-permute-start.10
  62.0 1.3 %collective-permute-done.10.refs_0_ = f32[392,128]{1,0:T(8,128)S(1)} collective-permute-done((f32[392,128]{1,0:T(8,128)S(1)}, f32[392,128]{1,0:T(8,128)S(1)}, u32[]{:S(2)}, u32[]{:S(2)}) %collective-permute-start.10) | collective-permute-done | bytes 200736 | tf_op jit(solution)/shard_map/ppermute | solution.py:613
  63.3 8.1 %shard_map.79 = (f32[3,128,128]{2,1,0:T(8,128)S(1)}, f32[3,128,128]{2,1,0:T(8,128)S(1)}, f32[8,128]{1,0:T(8,128)S(1)}, f32[392,128]{1,0:T(8,128)S(1)}) custom-call(f32[3,128,128]{2,1,0:T(8,128)S(1)} %get-tuple-element.41.x_ref, f32[3,128,128]{2,1,0:T(8,128)S(1)} %get-tuple-element.42.v_ref, f32[128,128]{1,0:T(8,128)S(1)} %get-tuple-element.29.rest_ref, ...), custom_call_target="tpu_custom_call" | custom-call | tf_op jit(solution)/shard_map/pallas_call | solution.py:657
  71.5 0.2 collective-permute-start.11
  71.7 0.6 slice.6
  72.3 0.7 collective-permute-done.11.refs_0_
  73.0 0.6 shard_map.80
  73.6 0.7 copy.8
  (16 shorter events, 0.1 us)
Async XLA Ops:
  4.2 23.3 %collective-permute-start.6 = (f32[88,128]{1,0:T(8,128)S(1)}, f32[88,128]{1,0:T(8,128)S(1)}, u32[]{:S(2)}, u32[]{:S(2)}) collective-permute-start(f32[88,128]{1,0:T(8,128)S(1)} %concatenate.3), channel_id=1, source_target_pairs={{14,0},{12,2},{2,4},{0,6},{6,8},{4,10},{10,12},{8,14},{15,1},{13,3... | collective-permute-start | bytes 135176 | tf_op jit(solution)/shard_map/ppermute | solution.py:613
  8.2 19.3 %collective-permute-start.5 = (f32[88,128]{1,0:T(8,128)S(1)}, f32[88,128]{1,0:T(8,128)S(1)}, u32[]{:S(2)}, u32[]{:S(2)}) collective-permute-start(f32[88,128]{1,0:T(8,128)S(1)} %concatenate.3), channel_id=1, source_target_pairs={{12,0},{0,4},{4,8},{8,12},{13,1},{1,5},{5,9},{9,13},{14,2},{2,6},{... | collective-permute-start | bytes 135176 | tf_op jit(solution)/shard_map/ppermute | solution.py:613
  9.8 17.7 %collective-permute-start.4 = (f32[88,128]{1,0:T(8,128)S(1)}, f32[88,128]{1,0:T(8,128)S(1)}, u32[]{:S(2)}, u32[]{:S(2)}) collective-permute-start(f32[88,128]{1,0:T(8,128)S(1)} %concatenate.3), channel_id=1, source_target_pairs={{10,0},{8,2},{14,4},{12,6},{2,8},{0,10},{6,12},{4,14},{11,1},{9,3}... | collective-permute-start | bytes 135176 | tf_op jit(solution)/shard_map/ppermute | solution.py:613
  10.9 16.6 %collective-permute-start.3 = (f32[88,128]{1,0:T(8,128)S(1)}, f32[88,128]{1,0:T(8,128)S(1)}, u32[]{:S(2)}, u32[]{:S(2)}) collective-permute-start(f32[88,128]{1,0:T(8,128)S(1)} %concatenate.3), channel_id=1, source_target_pairs={{8,0},{12,4},{0,8},{4,12},{9,1},{13,5},{1,9},{5,13},{10,2},{14,6},... | collective-permute-start | bytes 135176 | tf_op jit(solution)/shard_map/ppermute | solution.py:613
  12.7 4.1 %collective-permute-start = (f32[88,128]{1,0:T(8,128)S(1)}, f32[88,128]{1,0:T(8,128)S(1)}, u32[]{:S(2)}, u32[]{:S(2)}) collective-permute-start(f32[88,128]{1,0:T(8,128)S(1)} %concatenate.3), channel_id=1, source_target_pairs={{2,0},{0,2},{3,1},{1,3},{6,4},{4,6},{7,5},{5,7},{10,8},{8,10},{11,... | collective-permute-start | bytes 135176 | tf_op jit(solution)/shard_map/ppermute | solution.py:613
  16.8 4.2 %collective-permute-start.1 = (f32[88,128]{1,0:T(8,128)S(1)}, f32[88,128]{1,0:T(8,128)S(1)}, u32[]{:S(2)}, u32[]{:S(2)}) collective-permute-start(f32[88,128]{1,0:T(8,128)S(1)} %concatenate.3), channel_id=1, source_target_pairs={{4,0},{8,4},{12,8},{0,12},{5,1},{9,5},{13,9},{1,13},{6,2},{10,6},{... | collective-permute-start | bytes 135176 | tf_op jit(solution)/shard_map/ppermute | solution.py:613
  20.9 6.5 %collective-permute-start.2 = (f32[88,128]{1,0:T(8,128)S(1)}, f32[88,128]{1,0:T(8,128)S(1)}, u32[]{:S(2)}, u32[]{:S(2)}) collective-permute-start(f32[88,128]{1,0:T(8,128)S(1)} %concatenate.3), channel_id=1, source_target_pairs={{6,0},{4,2},{10,4},{8,6},{14,8},{12,10},{2,12},{0,14},{7,1},{5,3},... | collective-permute-start | bytes 135176 | tf_op jit(solution)/shard_map/ppermute | solution.py:613
  27.6 1.7 %collective-permute-start.7 = (f32[8,88,128]{2,1,0:T(8,128)S(1)}, f32[8,88,128]{2,1,0:T(8,128)S(1)}, u32[]{:S(2)}, u32[]{:S(2)}) collective-permute-start(f32[8,88,128]{2,1,0:T(8,128)S(1)} %bitcast_dynamic-update-slice_fusion.near_ref), channel_id=1, source_target_pairs={{1,0},{0,1},{3,2},{2,3},{5,4},{4,5},{7,6},{6,7},{9,8},{8,9},{11,10... | collective-permute-start | bytes 1081352 | tf_op jit(solution)/shard_map/ppermute | solution.py:613
  42.3 1.5 %collective-permute-start.8 = (f32[392,128]{1,0:T(8,128)S(1)}, f32[392,128]{1,0:T(8,128)S(1)}, u32[]{:S(2)}, u32[]{:S(2)}) collective-permute-start(f32[392,128]{1,0:T(8,128)S(1)} %get-tuple-element.36.own_ref), channel_id=1, source_target_pairs={{1,0},{0,1},{3,2},{2,3},{5,4},{4,5},{7,6},{6,7},{9,8},{8,9},{11,10... | collective-permute-start | bytes 602120 | tf_op jit(solution)/shard_map/ppermute | solution.py:613
  52.0 1.5 %collective-permute-start.9 = (f32[392,128]{1,0:T(8,128)S(1)}, f32[392,128]{1,0:T(8,128)S(1)}, u32[]{:S(2)}, u32[]{:S(2)}) collective-permute-start(f32[392,128]{1,0:T(8,128)S(1)} %get-tuple-element.40.own_ref), channel_id=1, source_target_pairs={{1,0},{0,1},{3,2},{2,3},{5,4},{4,5},{7,6},{6,7},{9,8},{8,9},{11,10... | collective-permute-start | bytes 602120 | tf_op jit(solution)/shard_map/ppermute | solution.py:613
  61.8 1.5 %collective-permute-start.10 = (f32[392,128]{1,0:T(8,128)S(1)}, f32[392,128]{1,0:T(8,128)S(1)}, u32[]{:S(2)}, u32[]{:S(2)}) collective-permute-start(f32[392,128]{1,0:T(8,128)S(1)} %get-tuple-element.44.own_ref), channel_id=1, source_target_pairs={{1,0},{0,1},{3,2},{2,3},{5,4},{4,5},{7,6},{6,7},{9,8},{8,9},{11,10... | collective-permute-start | bytes 602120 | tf_op jit(solution)/shard_map/ppermute | solution.py:613
  71.5 1.5 %collective-permute-start.11 = (f32[392,128]{1,0:T(8,128)S(1)}, f32[392,128]{1,0:T(8,128)S(1)}, u32[]{:S(2)}, u32[]{:S(2)}) collective-permute-start(f32[392,128]{1,0:T(8,128)S(1)} %get-tuple-element.48.own_ref), channel_id=1, source_target_pairs={{1,0},{0,1},{3,2},{2,3},{5,4},{4,5},{7,6},{6,7},{9,8},{8,9},{11,10... | collective-permute-start | bytes 602120 | tf_op jit(solution)/shard_map/ppermute | solution.py:613

commit v4 on v3

--- a/solution.py
+++ b/solution.py
@@ -560,16 +560,16 @@
     return total
 
 
-def energy_row(grid, own_ref, got_refs, v, row, previous):
+def energy_row(grid, own_ref, got_refs, v, step, previous):
     rows = pl.ds(3 * grid.domains * 8, 8)
     potential = own_ref[rows, :]
     for ref in got_refs:
         potential = potential + ref[rows, :]
     kinetic = 0.5 * dot3(v, v)
-    lane = lanes_of((8, LANES))
-    at = lax.broadcasted_iota(jnp.int32, (8, LANES), 0) == row
-    previous = jnp.where(at & (lane == 0), jnp.sum(potential), previous)
-    return jnp.where(at & (lane == 1), jnp.sum(kinetic), previous)
+    here = lanes_of((8, LANES)) == step
+    row = lax.broadcasted_iota(jnp.int32, (8, LANES), 0)
+    previous = jnp.where(here & (row == 0), jnp.sum(potential), previous)
+    return jnp.where(here & (row == 1), jnp.sum(kinetic), previous)
 
 
 def step_kernel(grid, step, x_ref, v_ref, rest_ref, flag_ref, ids_ref, weight_ref, index_ref, table_ref, zone_ref, energies_ref, own_ref, *refs):
@@ -592,13 +592,44 @@
     pair_forces(grid, moved_ref, (ids_ref, weight_ref, index_ref, table_ref, zone_ref), force_ref, scratch)
 
 
-def last_kernel(grid, v_ref, energies_ref, own_ref, *refs):
-    got_refs, (speed_ref, energy_out_ref) = refs[: grid.gz - 1], refs[grid.gz - 1 :]
+def last_kernel(grid, bead_total, x_ref, v_ref, energies_ref, own_ref, *refs):
+    got_refs, refs = refs[: grid.gz - 1], refs[grid.gz - 1 :]
+    targets, (place_ref, speed_ref, energy_out_ref), sems = refs[:3], refs[3:6], refs[6]
     force = total_force(grid, own_ref, got_refs)
     v = [v_ref[c] + (0.5 * time_step) * force[c] for c in range(3)]
     for c in range(3):
+        place_ref[c] = x_ref[c, pl.ds(0, 8), :]
         speed_ref[c] = v[c][:8]
-    energy_out_ref[...] = energy_row(grid, own_ref, got_refs, v, ITERS - 1, energies_ref[...])
+    energies = energy_row(grid, own_ref, got_refs, v, ITERS - 1, energies_ref[...])
+    energy_out_ref[...] = energies[:2, :ITERS] / bead_total
+    moved_together((place_ref, speed_ref, energy_out_ref), targets, sems)
+
+
+def moved_together(sources, targets, sems):
+    copies = [pltpu.make_async_copy(a, b, sems.at[n]) for n, (a, b) in enumerate(zip(sources, targets))]
+    for copy in copies:
+        copy.start()
+    for copy in copies:
+        copy.wait()
+
+
+def pack_kernel(grid, layout, *refs):
+    sources, out_ref, held, sems = refs[:5], refs[5], refs[6:11], refs[11]
+    moved_together(sources, held, sems)
+    x_ref, v_ref, flag_ref, pair_ref, send_ref = held
+    out_ref[...] = jnp.zeros(out_ref.shape, jnp.float32)
+    for c in range(3):
+        out_ref[pl.ds(layout["positions"] + 8 * c, 8), :] = x_ref[c]
+        out_ref[pl.ds(layout["velocities"] + 8 * c, 8), :] = v_ref[c]
+    out_ref[pl.ds(layout["flags"], 7), :] = flag_ref[...].astype(jnp.float32)
+    for side in range(2):
+        for block in range(grid.blocks):
+            row = layout["pairs"] + side * grid.blocks + block
+            ids = pair_ref[pl.ds(side, 1), pl.ds(block * LANES, LANES)]
+            out_ref[pl.ds(row, 1), :] = ids.astype(jnp.float32)
+    out_ref[pl.ds(layout["sends"], 1), :] = send_ref[:, :LANES].astype(jnp.float32)
+    rest = send_ref.shape[1] - LANES
+    out_ref[pl.ds(layout["sends"] + 1, 1), pl.ds(0, rest)] = send_ref[:, LANES:].astype(jnp.float32)
 
 
 def from_ahead(value, steps):
@@ -615,20 +646,29 @@
 
 def replicated(grid, positions, velocities, send_list, pair_list, constraint_flags):
     clusters = positions.shape[2]
-    sends = jnp.pad(send_list, (0, -send_list.shape[0] % LANES)).reshape(-1, LANES)
-    parts = dict(
-        positions=positions.reshape(ROWS, clusters),
-        velocities=velocities.reshape(ROWS, clusters),
-        flags=jnp.pad(constraint_flags.astype(jnp.float32), ((0, 1), (0, 0))),
-        pairs=pair_list.astype(jnp.float32).reshape(-1, LANES),
-        sends=sends.astype(jnp.float32),
-    )
+    heights = dict(positions=ROWS, velocities=ROWS, flags=8, pairs=2 * grid.blocks, sends=2)
     layout, row = {}, 0
-    for name, value in parts.items():
+    for name, height in heights.items():
         layout[name] = row
-        row += value.shape[0]
-    pack = jnp.concatenate(list(parts.values()) + [jnp.zeros((-row % 8, LANES), jnp.float32)], axis=0)
-    near = jnp.stack([from_ahead(pack, (i, j, 0)) for i in range(grid.gx) for j in range(grid.gy)])
+        row += height
+    params = pltpu.CompilerParams(vmem_limit_bytes=VMEM_LIMIT)
+
+    def call(kernel, shapes, scratch, *values, **specs):
+        return pl.pallas_call(kernel, out_shape=shapes, scratch_shapes=scratch, compiler_params=params, **specs)(*values)
+
+    anywhere = pl.BlockSpec(memory_space=pltpu.MemorySpace.HBM)
+    given = (positions, velocities, constraint_flags, pair_list, send_list.reshape(1, -1))
+    given = [pltpu.with_memory_space_constraint(value, pltpu.MemorySpace.HBM) for value in given]
+
+    pack = call(
+        functools.partial(pack_kernel, grid, layout),
+        jax.ShapeDtypeStruct((row + -row % 8, LANES), jnp.float32),
+        [pltpu.VMEM(value.shape, value.dtype) for value in given] + [pltpu.SemaphoreType.DMA((len(given),))],
+        *given,
+        in_specs=[anywhere] * len(given),
+    )
+    column = jnp.stack([from_ahead(pack, (0, j, 0)) for j in range(grid.gy)])
+    near = jnp.concatenate([from_ahead(column, (i, 0, 0)) for i in range(grid.gx)], axis=0)
     far = from_ahead(near, (0, 0, 1))
     f32, i32, b16 = jnp.float32, jnp.int32, jnp.bfloat16
     n, rows = grid.lists, grid.domains * 8
@@ -651,11 +691,6 @@
         pltpu.VMEM((n, ROWS, 2 * LANES), f32),
         pltpu.VMEM((8, LANES), f32),
     ]
-    params = pltpu.CompilerParams(vmem_limit_bytes=VMEM_LIMIT)
-
-    def call(kernel, shapes, scratch, *values):
-        return pl.pallas_call(kernel, out_shape=shapes, scratch_shapes=scratch, compiler_params=params)(*values)
-
     x, v, rest, flags, *rest_out = call(
         functools.partial(start_kernel, grid, layout), [cube, cube, plane, plane] + table_shapes + [forces], scratch, near, far
     )
@@ -670,11 +705,16 @@
             x, v, rest, flags, *tables, energies, force, *got,
         )
     got = [from_ahead(force, (0, 0, by)) for by in range(1, grid.gz)]
-    speed, energies = call(
-        functools.partial(last_kernel, grid), [jax.ShapeDtypeStruct((3, 8, LANES), f32), small], [], v, energies, force, *got
-    )
-    bead_total = 8 * clusters * grid.domains
-    return (x[:, :8], speed, energies[:ITERS, :2] / bead_total)
+    own = jax.ShapeDtypeStruct((3, 8, LANES), f32)
+    shapes = [own, own, jax.ShapeDtypeStruct((2, ITERS), f32)]
+    place, speed, energies = call(
+        functools.partial(last_kernel, grid, 8 * clusters * grid.domains),
+        shapes,
+        [pltpu.VMEM(shape.shape, f32) for shape in shapes] + [pltpu.SemaphoreType.DMA((len(shapes),))],
+        x, v, energies, force, *got,
+        out_specs=[anywhere] * len(shapes),
+    )
+    return (place, speed, energies.T)
 
 
 def can_replicate(grid, positions, send_list, pair_list):

time: 74.7 us -> 63.2 us (0.85)
  starting transfers between devices: 18.2 us -> 10 us
  local copies, waits for them, and re-layouts: 2.76 us -> 0.03 us
  other arithmetic: 2.09 us -> 0.01 us
  Pallas kernels: 38.2 us -> 39.2 us
    ppermute x12 -> x9, starting transfers between devices: 18.2 us -> 10 us  [from_ahead(): return lax.ppermute(value, tuple(names), pairs)]
    convert_element_type x3 -> x0, other arithmetic: 2.09 us -> none  [the longest x1 0.72 us: replicated(): pair_list.astype(jnp.float32).reshape(-1, LANES)]
    concatenate x1, local copies, waits for them, and re-layouts: 1.44 us -> 0.01 us  [replicated(): jnp.concatenate([from_ahead(column, (i, 0, 0)) for i in range(grid.gx)],...]
    pallas_call x5 -> x6, Pallas kernels: 38.2 us -> 39.2 us  [call(): pl.pallas_call(kernel, out_shape=shapes, scratch_shapes=scratch, compiler...]
    ppermute x12 -> x9, waiting for transfers between devices: 12.3 us -> 12.9 us  [from_ahead(): return lax.ppermute(value, tuple(names), pairs)]
  transfers between devices with their start and end apart: 12 -> 9, of which waited for: 8 -> 8; matrix products, arithmetic and copies ran while one was open for 1% -> 0% of each run, Pallas kernels for 0% -> 0%
where the time goes in v4:
time: 63.2 us; the launch traced here: 63 us
  Pallas kernels  39.2 us (62%)
  waiting for transfers between devices  12.9 us (20%)
  starting transfers between devices  10 us (16%)
  between operations  0.87 us (1%)
    pallas_call x6, Pallas kernels, call(): pl.pallas_call(kernel, out_shape=shapes, scratch_shapes=scratch, compiler...  39.2 us
    ppermute x9, waiting for transfers between devices, from_ahead(): return lax.ppermute(value, tuple(names), pairs)  12.9 us
    ppermute x9, starting transfers between devices, from_ahead(): return lax.ppermute(value, tuple(names), pairs)  10 us
  transfers between devices with their start and end apart: 9, of which 8 were waited for; matrix products, arithmetic and copies ran while one was open for 0% of the time, Pallas kernels for 0%

profile of v4, /device:TPU:0, one launch (start us, length us, event | category | flops | bytes accessed | tf_op | source)
XLA Modules:
  0.0 63.0 jit_solution(17181348880206271416)
XLA Ops:
  0.6 0.8 %shard_map.76 = f32[88,128]{1,0:T(8,128)S(1)} custom-call(f32[3,8,128]{2,1,0:T(8,128)} %refs_0_.1, f32[3,8,128]{2,1,0:T(8,128)} %refs_1_.1, s32[7,128]{1,0:T(8,128)} %refs_2_.1, s32[2,1792]{1,0:T(2,128)} %refs_3_.1, s32[1,178]{1,0:T(1,128)} %bitcast.8), custom_call_target="tpu_custom_call" | custom-call | tf_op jit(solution)/shard_map/pallas_call | solution.py:657
  1.5 3.0 %collective-permute-start = (f32[88,128]{1,0:T(8,128)S(1)}, f32[88,128]{1,0:T(8,128)S(1)}, u32[]{:S(2)}, u32[]{:S(2)}) collective-permute-start(f32[88,128]{1,0:T(8,128)S(1)} %shard_map.76), channel_id=1, source_target_pairs={{2,0},{0,2},{3,1},{1,3},{6,4},{4,6},{7,5},{5,7},{10,8},{8,10},{11,... | collective-permute-start | bytes 135176 | tf_op jit(solution)/shard_map/ppermute | solution.py:644
  4.5 2.0 %collective-permute-done = f32[88,128]{1,0:T(8,128)S(1)} collective-permute-done((f32[88,128]{1,0:T(8,128)S(1)}, f32[88,128]{1,0:T(8,128)S(1)}, u32[]{:S(2)}, u32[]{:S(2)}) %collective-permute-start) | collective-permute-done | bytes 45088 | tf_op jit(solution)/shard_map/ppermute | solution.py:644
  6.5 2.2 %collective-permute-start.3 = (f32[2,88,128]{2,1,0:T(8,128)S(1)}, f32[2,88,128]{2,1,0:T(8,128)S(1)}, u32[]{:S(2)}, u32[]{:S(2)}) collective-permute-start(f32[2,88,128]{2,1,0:T(8,128)S(1)} %pad_maximum_fusion), channel_id=1, source_target_pairs={{12,0},{0,4},{4,8},{8,12},{13,1},{1,5},{5,9},{9,13},{14,2},{2,6},{... | collective-permute-start | bytes 270344 | tf_op jit(solution)/shard_map/ppermute | solution.py:644
  8.7 2.6 %collective-permute-start.2 = (f32[2,88,128]{2,1,0:T(8,128)S(1)}, f32[2,88,128]{2,1,0:T(8,128)S(1)}, u32[]{:S(2)}, u32[]{:S(2)}) collective-permute-start(f32[2,88,128]{2,1,0:T(8,128)S(1)} %pad_maximum_fusion), channel_id=1, source_target_pairs={{8,0},{12,4},{0,8},{4,12},{9,1},{13,5},{1,9},{5,13},{10,2},{14,6},... | collective-permute-start | bytes 270344 | tf_op jit(solution)/shard_map/ppermute | solution.py:644
  11.3 1.3 %collective-permute-start.1 = (f32[2,88,128]{2,1,0:T(8,128)S(1)}, f32[2,88,128]{2,1,0:T(8,128)S(1)}, u32[]{:S(2)}, u32[]{:S(2)}) collective-permute-start(f32[2,88,128]{2,1,0:T(8,128)S(1)} %pad_maximum_fusion), channel_id=1, source_target_pairs={{4,0},{8,4},{12,8},{0,12},{5,1},{9,5},{13,9},{1,13},{6,2},{10,6},{... | collective-permute-start | bytes 270344 | tf_op jit(solution)/shard_map/ppermute | solution.py:644
  12.6 3.6 %collective-permute-done.1 = f32[2,88,128]{2,1,0:T(8,128)S(1)} collective-permute-done((f32[2,88,128]{2,1,0:T(8,128)S(1)}, f32[2,88,128]{2,1,0:T(8,128)S(1)}, u32[]{:S(2)}, u32[]{:S(2)}) %collective-permute-start.1) | collective-permute-done | bytes 90144 | tf_op jit(solution)/shard_map/ppermute | solution.py:644
  16.3 0.3 collective-permute-done.2
  16.6 0.0 collective-permute-done.3
  16.6 0.1 collective-permute-start.4
  16.7 1.7 %collective-permute-done.4.far_ref = f32[8,88,128]{2,1,0:T(8,128)S(1)} collective-permute-done((f32[8,88,128]{2,1,0:T(8,128)S(1)}, f32[8,88,128]{2,1,0:T(8,128)S(1)}, u32[]{:S(2)}, u32[]{:S(2)}) %collective-permute-start.4) | collective-permute-done | bytes 360480 | tf_op jit(solution)/shard_map/ppermute | solution.py:644
  18.4 13.0 %shard_map.77 = (f32[3,128,128]{2,1,0:T(8,128)S(1)}, f32[3,128,128]{2,1,0:T(8,128)S(1)}, f32[128,128]{1,0:T(8,128)S(1)}, f32[128,128]{1,0:T(8,128)S(1)}, s32[2,8...) custom-call(f32[8,88,128]{2,1,0:T(8,128)S(1)} %constant_dynamic-upda, ...), custom_call_target="tpu_custom_call" | custom-call | tf_op jit(solution)/shard_map/pallas_call | solution.py:657
  31.4 0.2 collective-permute-start.5
  31.6 1.3 %collective-permute-done.5.refs_0_ = f32[392,128]{1,0:T(8,128)S(1)} collective-permute-done((f32[392,128]{1,0:T(8,128)S(1)}, f32[392,128]{1,0:T(8,128)S(1)}, u32[]{:S(2)}, u32[]{:S(2)}) %collective-permute-start.5) | collective-permute-done | bytes 200736 | tf_op jit(solution)/shard_map/ppermute | solution.py:644
  32.9 8.1 %shard_map.78 = (f32[3,128,128]{2,1,0:T(8,128)S(1)}, f32[3,128,128]{2,1,0:T(8,128)S(1)}, f32[8,128]{1,0:T(8,128)S(1)}, f32[392,128]{1,0:T(8,128)S(1)}) custom-call(f32[3,128,128]{2,1,0:T(8,128)S(1)} %get-tuple-element.28.x_ref, f32[3,128,128]{2,1,0:T(8,128)S(1)} %get-tuple-element.29.v_ref, f32[128,128]{1,0:T(8,128)S(1)} %get-tuple-element.30.rest_ref, ...), custom_call_target="tpu_custom_call" | custom-call | tf_op jit(solution)/shard_map/pallas_call | solution.py:657
  41.0 0.2 collective-permute-start.6
  41.2 1.3 %collective-permute-done.6.refs_0_ = f32[392,128]{1,0:T(8,128)S(1)} collective-permute-done((f32[392,128]{1,0:T(8,128)S(1)}, f32[392,128]{1,0:T(8,128)S(1)}, u32[]{:S(2)}, u32[]{:S(2)}) %collective-permute-start.6) | collective-permute-done | bytes 200736 | tf_op jit(solution)/shard_map/ppermute | solution.py:644
  42.6 8.3 %shard_map.79 = (f32[3,128,128]{2,1,0:T(8,128)S(1)}, f32[3,128,128]{2,1,0:T(8,128)S(1)}, f32[8,128]{1,0:T(8,128)S(1)}, f32[392,128]{1,0:T(8,128)S(1)}) custom-call(f32[3,128,128]{2,1,0:T(8,128)S(1)} %get-tuple-element.38.x_ref, f32[3,128,128]{2,1,0:T(8,128)S(1)} %get-tuple-element.39.v_ref, f32[128,128]{1,0:T(8,128)S(1)} %get-tuple-element.30.rest_ref, ...), custom_call_target="tpu_custom_call" | custom-call | tf_op jit(solution)/shard_map/pallas_call | solution.py:657
  50.9 0.2 collective-permute-start.7
  51.1 1.3 %collective-permute-done.7.refs_0_ = f32[392,128]{1,0:T(8,128)S(1)} collective-permute-done((f32[392,128]{1,0:T(8,128)S(1)}, f32[392,128]{1,0:T(8,128)S(1)}, u32[]{:S(2)}, u32[]{:S(2)}) %collective-permute-start.7) | collective-permute-done | bytes 200736 | tf_op jit(solution)/shard_map/ppermute | solution.py:644
  52.4 8.1 %shard_map.80 = (f32[3,128,128]{2,1,0:T(8,128)S(1)}, f32[3,128,128]{2,1,0:T(8,128)S(1)}, f32[8,128]{1,0:T(8,128)S(1)}, f32[392,128]{1,0:T(8,128)S(1)}) custom-call(f32[3,128,128]{2,1,0:T(8,128)S(1)} %get-tuple-element.42.x_ref, f32[3,128,128]{2,1,0:T(8,128)S(1)} %get-tuple-element.43.v_ref, f32[128,128]{1,0:T(8,128)S(1)} %get-tuple-element.30.rest_ref, ...), custom_call_target="tpu_custom_call" | custom-call | tf_op jit(solution)/shard_map/pallas_call | solution.py:657
  60.5 0.2 collective-permute-start.8
  60.7 1.3 %collective-permute-done.8.refs_0_ = f32[392,128]{1,0:T(8,128)S(1)} collective-permute-done((f32[392,128]{1,0:T(8,128)S(1)}, f32[392,128]{1,0:T(8,128)S(1)}, u32[]{:S(2)}, u32[]{:S(2)}) %collective-permute-start.8) | collective-permute-done | bytes 200736 | tf_op jit(solution)/shard_map/ppermute | solution.py:644
  62.0 0.8 %shard_map.81 = (f32[3,8,128]{2,1,0:T(8,128)}, f32[3,8,128]{2,1,0:T(8,128)}, f32[2,3]{1,0:T(2,128)}) custom-call(f32[3,128,128]{2,1,0:T(8,128)S(1)} %get-tuple-element.46.x_ref, f32[3,128,128]{2,1,0:T(8,128)S(1)} %get-tuple-element.47.v_ref, f32[8,128]{1,0:T(8,128)S(1)} %get-tuple-element.48.energies_ref, f32[392,128]{1,0:T(8,128)S(1)} %get-tuple-element.49.own_ref, ...), custom_call_target="tpu_custom_call" | custom-call | tf_op jit(solution)/shard_map/pallas_call | solution.py:657
  (7 shorter events, 0.0 us)
Async XLA Ops:
  1.5 5.1 %collective-permute-start = (f32[88,128]{1,0:T(8,128)S(1)}, f32[88,128]{1,0:T(8,128)S(1)}, u32[]{:S(2)}, u32[]{:S(2)}) collective-permute-start(f32[88,128]{1,0:T(8,128)S(1)} %shard_map.76), channel_id=1, source_target_pairs={{2,0},{0,2},{3,1},{1,3},{6,4},{4,6},{7,5},{5,7},{10,8},{8,10},{11,... | collective-permute-start | bytes 135176 | tf_op jit(solution)/shard_map/ppermute | solution.py:644
  6.5 10.1 %collective-permute-start.3 = (f32[2,88,128]{2,1,0:T(8,128)S(1)}, f32[2,88,128]{2,1,0:T(8,128)S(1)}, u32[]{:S(2)}, u32[]{:S(2)}) collective-permute-start(f32[2,88,128]{2,1,0:T(8,128)S(1)} %pad_maximum_fusion), channel_id=1, source_target_pairs={{12,0},{0,4},{4,8},{8,12},{13,1},{1,5},{5,9},{9,13},{14,2},{2,6},{... | collective-permute-start | bytes 270344 | tf_op jit(solution)/shard_map/ppermute | solution.py:644
  8.7 7.9 %collective-permute-start.2 = (f32[2,88,128]{2,1,0:T(8,128)S(1)}, f32[2,88,128]{2,1,0:T(8,128)S(1)}, u32[]{:S(2)}, u32[]{:S(2)}) collective-permute-start(f32[2,88,128]{2,1,0:T(8,128)S(1)} %pad_maximum_fusion), channel_id=1, source_target_pairs={{8,0},{12,4},{0,8},{4,12},{9,1},{13,5},{1,9},{5,13},{10,2},{14,6},... | collective-permute-start | bytes 270344 | tf_op jit(solution)/shard_map/ppermute | solution.py:644
  11.3 5.0 %collective-permute-start.1 = (f32[2,88,128]{2,1,0:T(8,128)S(1)}, f32[2,88,128]{2,1,0:T(8,128)S(1)}, u32[]{:S(2)}, u32[]{:S(2)}) collective-permute-start(f32[2,88,128]{2,1,0:T(8,128)S(1)} %pad_maximum_fusion), channel_id=1, source_target_pairs={{4,0},{8,4},{12,8},{0,12},{5,1},{9,5},{13,9},{1,13},{6,2},{10,6},{... | collective-permute-start | bytes 270344 | tf_op jit(solution)/shard_map/ppermute | solution.py:644
  16.6 1.7 %collective-permute-start.4 = (f32[8,88,128]{2,1,0:T(8,128)S(1)}, f32[8,88,128]{2,1,0:T(8,128)S(1)}, u32[]{:S(2)}, u32[]{:S(2)}) collective-permute-start(f32[8,88,128]{2,1,0:T(8,128)S(1)} %constant_dynamic-update-slice_fusion.near_ref), channel_id=1, source_target_pairs={{1,0},{0,1},{3,2},{2,3},{5,4},{4,5},{7,6},{6,7},{9,8},{8,9},{11,10... | collective-permute-start | bytes 1081352 | tf_op jit(solution)/shard_map/ppermute | solution.py:644
  31.4 1.5 %collective-permute-start.5 = (f32[392,128]{1,0:T(8,128)S(1)}, f32[392,128]{1,0:T(8,128)S(1)}, u32[]{:S(2)}, u32[]{:S(2)}) collective-permute-start(f32[392,128]{1,0:T(8,128)S(1)} %get-tuple-element.37.own_ref), channel_id=1, source_target_pairs={{1,0},{0,1},{3,2},{2,3},{5,4},{4,5},{7,6},{6,7},{9,8},{8,9},{11,10... | collective-permute-start | bytes 602120 | tf_op jit(solution)/shard_map/ppermute | solution.py:644
  41.0 1.5 %collective-permute-start.6 = (f32[392,128]{1,0:T(8,128)S(1)}, f32[392,128]{1,0:T(8,128)S(1)}, u32[]{:S(2)}, u32[]{:S(2)}) collective-permute-start(f32[392,128]{1,0:T(8,128)S(1)} %get-tuple-element.41.own_ref), channel_id=1, source_target_pairs={{1,0},{0,1},{3,2},{2,3},{5,4},{4,5},{7,6},{6,7},{9,8},{8,9},{11,10... | collective-permute-start | bytes 602120 | tf_op jit(solution)/shard_map/ppermute | solution.py:644
  50.9 1.5 %collective-permute-start.7 = (f32[392,128]{1,0:T(8,128)S(1)}, f32[392,128]{1,0:T(8,128)S(1)}, u32[]{:S(2)}, u32[]{:S(2)}) collective-permute-start(f32[392,128]{1,0:T(8,128)S(1)} %get-tuple-element.45.own_ref), channel_id=1, source_target_pairs={{1,0},{0,1},{3,2},{2,3},{5,4},{4,5},{7,6},{6,7},{9,8},{8,9},{11,10... | collective-permute-start | bytes 602120 | tf_op jit(solution)/shard_map/ppermute | solution.py:644
  60.5 1.5 %collective-permute-start.8 = (f32[392,128]{1,0:T(8,128)S(1)}, f32[392,128]{1,0:T(8,128)S(1)}, u32[]{:S(2)}, u32[]{:S(2)}) collective-permute-start(f32[392,128]{1,0:T(8,128)S(1)} %get-tuple-element.49.own_ref), channel_id=1, source_target_pairs={{1,0},{0,1},{3,2},{2,3},{5,4},{4,5},{7,6},{6,7},{9,8},{8,9},{11,10... | collective-permute-start | bytes 602120 | tf_op jit(solution)/shard_map/ppermute | solution.py:644

commit v5 on v4

--- a/solution.py
+++ b/solution.py
@@ -295,14 +295,51 @@
     return jnp.take_along_axis(source, index, axis=1, mode="promise_in_bounds")
 
 
-def build_tables(grid, near_ref, far_ref, pair_row, send_row, ids_ref, weight_ref, index_ref, table_ref, zone_ref):
+def rounded_iota(shape, dimension, start=0):
+    return (lax.broadcasted_iota(jnp.int32, shape, dimension) + start).astype(jnp.float32).astype(jnp.bfloat16)
+
+
+def table_kernel(grid, pair_row, near_ref, ids_ref, weight_ref, table_ref, spread_ref, turned_ref):
     blocks = grid.blocks
-    lane = lanes_of((8, LANES))
-    own_code = lanes_of((LANES, LANES)).astype(jnp.float32).astype(jnp.bfloat16)
-    first_code = (lanes_of((LANES, LANES)) + LANES).astype(jnp.float32).astype(jnp.bfloat16)
-    rest_code = (-1 - lanes_of((LANES, LANES))).astype(jnp.float32).astype(jnp.bfloat16)
-    one = jnp.ones((LANES, LANES), jnp.bfloat16)
-    zero = jnp.zeros((LANES, LANES), jnp.bfloat16)
+    square = (LANES, LANES)
+    codes_of = (rounded_iota(square, 1), rounded_iota(square, 1, LANES), -rounded_iota(square, 1, 1))
+    one, zero = jnp.ones(square, jnp.bfloat16), jnp.zeros(square, jnp.bfloat16)
+    row = rounded_iota(square, 0)
+    for at in range(2 * blocks):
+        place = at // blocks * grid.padded + at % blocks
+        spread_ref[:, pl.ds(at * LANES, LANES)] = jnp.where(row == place, one, zero)
+    for number in range(grid.lists):
+        sides = []
+        for side in range(2):
+            ids = near_ref[number, pl.ds(pair_row + side * blocks, blocks), :]
+            fill = jnp.full((grid.padded - blocks, LANES), float(grid.dummy), jnp.float32)
+            sides.append(jnp.concatenate([ids, fill], axis=0) if grid.padded > blocks else ids)
+            ids_ref[side, number] = sides[side].astype(jnp.int32)
+        usable = jnp.where(sides[0] < float(grid.dummy), 1.0, 0.0)
+        weight_ref[number] = jnp.where(sides[0] == sides[1], 0.5, 1.0) * usable
+        codes = jnp.concatenate(sides, axis=0)
+        codes = jnp.where(codes < 2.0 * LANES, codes, 2.0 * LANES - 1.0 - codes)
+        empty = jnp.zeros((LANES - 2 * grid.padded, LANES), jnp.float32)
+        turned_ref[number] = jnp.transpose(jnp.concatenate([codes, empty], axis=0)).astype(jnp.bfloat16)
+
+    def one_list(number, carry):
+        wide = jnp.dot(turned_ref[number], spread_ref[...], preferred_element_type=jnp.float32)
+        for at in range(2 * blocks):
+            column = wide[:, at * LANES : (at + 1) * LANES].astype(jnp.bfloat16)
+            for part, code in enumerate(codes_of):
+                hot = jnp.where(column == code, one, zero)
+                table_ref[number, part, pl.ds(at * LANES, LANES), :] = hot
+        return carry
+
+    lax.fori_loop(0, grid.lists, one_list, 0)
+
+
+def build_zones(grid, near_ref, far_ref, send_row, index_ref, zone_ref):
+    square = (LANES, LANES)
+    lane = lanes_of((1, LANES))
+    own_code = rounded_iota(square, 1)
+    slot = rounded_iota(square, 0)
+    one, zero = jnp.ones(square, jnp.bfloat16), jnp.zeros(square, jnp.bfloat16)
 
     def send_of(number, row):
         source = near_ref if number % grid.gz == 0 else far_ref
@@ -314,39 +351,18 @@
         rest = jnp.zeros((1, LANES), jnp.float32)
         for direction, start, stop in grid.zones:
             row = send_of(grid.domain(i, j, direction), 1)
-            rest = jnp.where((lane[:1] >= start) & (lane[:1] < stop), row, rest)
+            rest = jnp.where((lane >= start) & (lane < stop), row, rest)
         both = jnp.concatenate([to_x, rest] + [jnp.zeros((6, LANES), jnp.float32)], axis=0)
         index_ref[number] = both.astype(jnp.int32)
 
     def one_list(number, carry):
-        first = near_ref[number, pl.ds(pair_row, blocks), :]
-        second = near_ref[number, pl.ds(pair_row + blocks, blocks), :]
-        fill = jnp.full((grid.padded - blocks, LANES), float(grid.dummy), jnp.float32)
-        parts = [[first, fill], [second, fill]] if grid.padded > blocks else [[first], [second]]
-        first, second = (jnp.concatenate(p, axis=0) for p in parts)
-        ids_ref[0, number] = first.astype(jnp.int32)
-        ids_ref[1, number] = second.astype(jnp.int32)
-        usable = jnp.where(first < float(grid.dummy), 1.0, 0.0)
-        weight_ref[number] = jnp.where(first == second, 0.5, 1.0) * usable
-        both = index_ref[number].astype(jnp.float32)
-        codes = jnp.concatenate([first, second], axis=0)
-        codes = jnp.where(codes < 2.0 * LANES, codes, 2.0 * LANES - 1.0 - codes)
-        turned = jnp.transpose(jnp.concatenate([codes, both], axis=0))
-        for side in range(2):
-            for block in range(blocks):
-                at = side * grid.padded + block
-                column = jnp.broadcast_to(turned[:, at : at + 1], (LANES, LANES)).astype(jnp.bfloat16)
-                rows = pl.ds((side * blocks + block) * LANES, LANES)
-                for part, code in enumerate((own_code, first_code, rest_code)):
-                    table_ref[number, rows, pl.ds(part * LANES, LANES)] = jnp.where(column == code, one, zero)
-        at = 2 * grid.padded
-        column = jnp.broadcast_to(turned[:, at : at + 1], (LANES, LANES)).astype(jnp.bfloat16)
-        zone_ref[number, :, pl.ds(0, LANES)] = jnp.where(column == own_code, one, zero)
-        column = jnp.broadcast_to(turned[:, at + 1 : at + 2], (LANES, LANES)).astype(jnp.bfloat16)
-        slot = lax.broadcasted_iota(jnp.int32, (LANES, LANES), 0).astype(jnp.float32).astype(jnp.bfloat16)
+        turned = jnp.transpose(index_ref[number].astype(jnp.float32))
+        column = jnp.broadcast_to(turned[:, 0:1], square).astype(jnp.bfloat16)
+        zone_ref[number, 0] = jnp.where(column == own_code, one, zero)
+        column = jnp.broadcast_to(turned[:, 1:2], square).astype(jnp.bfloat16)
         for part, (direction, start, stop) in enumerate(grid.zones):
             here = (column == own_code) & (slot >= start) & (slot < stop)
-            zone_ref[number, :, pl.ds((part + 1) * LANES, LANES)] = jnp.where(here, one, zero)
+            zone_ref[number, part + 1] = jnp.where(here, one, zero)
         return carry
 
     lax.fori_loop(0, grid.lists, one_list, 0)
@@ -389,27 +405,33 @@
         weight = weight_ref[number, pl.ds(8 * group, 8), :]
         scale = weight * (6.0 * strength)
         energy = None
-        on_second = [[None] * 8 for _ in range(3)]
-        for k in range(8):
-            on_first = [None] * 3
-            for l in range(8):
-                apart = [sides[0][c][k] - sides[1][c][l] for c in range(3)]
-                scaled = apart[0] * apart[0] + apart[1] * apart[1] + apart[2] * apart[2]
-                intersect = jnp.maximum(1.0 - scaled, 0.0)
-                square = intersect * intersect
-                cube = square * intersect
-                energy = cube if energy is None else energy + cube
-                for c in range(3):
-                    pushing = square * apart[c]
-                    on_first[c] = pushing if l == 0 else on_first[c] + pushing
-                    on_second[c][l] = pushing if k == 0 else on_second[c][l] + pushing
+        partial = [None] * 8
+        for half in range(2):
+            beads = range(4 * half, 4 * half + 4)
+            second = {l: [sides[1][c][l] for c in range(3)] for l in beads}
+            on_second = {l: None for l in beads}
+            for k in range(8):
+                on_first = partial[k]
+                first = [sides[0][c][k] for c in range(3)]
+                for l in beads:
+                    apart = [first[c] - second[l][c] for c in range(3)]
+                    scaled = apart[0] * apart[0] + apart[1] * apart[1] + apart[2] * apart[2]
+                    intersect = jnp.maximum(1.0 - scaled, 0.0)
+                    square = intersect * intersect
+                    cube = square * intersect
+                    energy = cube if energy is None else energy + cube
+                    pushing = [square * apart[c] for c in range(3)]
+                    on_first = pushing if on_first is None else [on_first[c] + pushing[c] for c in range(3)]
+                    on_second[l] = pushing if k == 0 else [on_second[l][c] + pushing[c] for c in range(3)]
+                partial[k] = on_first
+                if half == 1:
+                    for c in range(3):
+                        row = (8 * group) * ROWS + c * 8 + k
+                        push_ref[pl.ds(row, 8, stride=ROWS), :] = on_first[c] * scale
             for c in range(3):
-                row = (8 * group) * ROWS + c * 8 + k
-                push_ref[pl.ds(row, 8, stride=ROWS), :] = on_first[c] * scale
-        for c in range(3):
-            for l in range(8):
-                row = (grid.padded + 8 * group) * ROWS + c * 8 + l
-                push_ref[pl.ds(row, 8, stride=ROWS), :] = -(on_second[c][l] * scale)
+                for l in beads:
+                    row = (grid.padded + 8 * group) * ROWS + c * 8 + l
+                    push_ref[pl.ds(row, 8, stride=ROWS), :] = on_second[l][c] * (-scale)
         own_beads = jnp.where(weight == 0.5, 8.0, 0.0)
         energy_ref[...] += strength * weight * (energy - own_beads)
 
@@ -420,7 +442,8 @@
         for block in range(grid.blocks):
             pieces.append(push_ref[pl.ds((side * grid.padded + block) * ROWS, ROWS), :])
     pushes = split_rows(jnp.concatenate(pieces, axis=1))
-    sums = joined(jnp.dot(pushes, table_ref[number], preferred_element_type=jnp.float32))
+    table = jnp.concatenate([table_ref[number, part] for part in range(3)], axis=1)
+    sums = joined(jnp.dot(pushes, table, preferred_element_type=jnp.float32))
     row = pl.multiple_of(number * grid.gz * 8, 8)
     for c in range(3):
         force_ref[pl.ds(c * grid.domains * 8 + row, 8), :] = sums[8 * c : 8 * c + 8, :LANES]
@@ -456,12 +479,12 @@
         i, j = number // grid.gy, number % grid.gy
         halo = halo_ref[number]
         to_x = joined(
-            jnp.dot(split_rows(halo[:, :LANES]), zone_ref[number, :, pl.ds(0, LANES)], preferred_element_type=jnp.float32)
+            jnp.dot(split_rows(halo[:, :LANES]), zone_ref[number, 0], preferred_element_type=jnp.float32)
         )
         rest = joined(
             jnp.dot(
                 split_rows(halo[:, LANES:]),
-                zone_ref[number, :, pl.ds(LANES, len(grid.zones) * LANES)],
+                jnp.concatenate([zone_ref[number, part + 1] for part in range(len(grid.zones))], axis=1),
                 preferred_element_type=jnp.float32,
             )
         )
@@ -475,9 +498,9 @@
     force_ref[pl.ds(3 * grid.domains * 8, 8), :] = energy_ref[...]
 
 
-def start_kernel(grid, layout, near_ref, far_ref, *refs):
-    x_ref, v_ref, rest_ref, flag_ref, ids_ref, weight_ref, index_ref, table_ref, zone_ref, force_ref = refs[:10]
-    scratch = refs[10:]
+def start_kernel(grid, layout, near_ref, far_ref, ids_ref, weight_ref, table_ref, *refs):
+    x_ref, v_ref, rest_ref, flag_ref, index_ref, zone_ref, force_ref = refs[:7]
+    scratch = refs[7:]
     for number in range(grid.domains):
         source = near_ref if number % grid.gz == 0 else far_ref
         at = number // grid.gz
@@ -487,7 +510,7 @@
             v_ref[c, rows, :] = source[at, pl.ds(layout["velocities"] + 8 * c, 8), :]
         flag_ref[rows, :] = source[at, pl.ds(layout["flags"], 8), :]
     rest_ref[...] = link_length([x_ref[c] for c in range(3)])
-    build_tables(grid, near_ref, far_ref, layout["pairs"], layout["sends"], ids_ref, weight_ref, index_ref, table_ref, zone_ref)
+    build_zones(grid, near_ref, far_ref, layout["sends"], index_ref, zone_ref)
     pair_forces(grid, x_ref, (ids_ref, weight_ref, index_ref, table_ref, zone_ref), force_ref, scratch)
 
 
@@ -676,12 +699,19 @@
     plane = jax.ShapeDtypeStruct((rows, LANES), f32)
     small = jax.ShapeDtypeStruct((8, LANES), f32)
     forces = jax.ShapeDtypeStruct((3 * rows + 8, LANES), f32)
-    table_shapes = [
-        jax.ShapeDtypeStruct((2, n, grid.padded, LANES), i32),
-        jax.ShapeDtypeStruct((n, grid.padded, LANES), f32),
+    ids, weight, table = call(
+        functools.partial(table_kernel, grid, layout["pairs"]),
+        [
+            jax.ShapeDtypeStruct((2, n, grid.padded, LANES), i32),
+            jax.ShapeDtypeStruct((n, grid.padded, LANES), f32),
+            jax.ShapeDtypeStruct((n, 3, grid.slots, LANES), b16),
+        ],
+        [pltpu.VMEM((LANES, grid.slots), b16), pltpu.VMEM((n, LANES, LANES), b16)],
+        near,
+    )
+    zone_shapes = [
         jax.ShapeDtypeStruct((n, 8, LANES), i32),
-        jax.ShapeDtypeStruct((n, grid.slots, 3 * LANES), b16),
-        jax.ShapeDtypeStruct((n, LANES, len(zone_list) * LANES), b16),
+        jax.ShapeDtypeStruct((n, len(zone_list), LANES, LANES), b16),
     ]
     scratch = [
         pltpu.VMEM((3, 3, 8, LANES), f32),
@@ -691,10 +721,13 @@
         pltpu.VMEM((n, ROWS, 2 * LANES), f32),
         pltpu.VMEM((8, LANES), f32),
     ]
-    x, v, rest, flags, *rest_out = call(
-        functools.partial(start_kernel, grid, layout), [cube, cube, plane, plane] + table_shapes + [forces], scratch, near, far
-    )
-    tables, force = rest_out[:5], rest_out[5]
+    x, v, rest, flags, index, zone, force = call(
+        functools.partial(start_kernel, grid, layout),
+        [cube, cube, plane, plane] + zone_shapes + [forces],
+        scratch,
+        near, far, ids, weight, table,
+    )
+    tables = (ids, weight, index, table, zone)
     energies = jnp.zeros((8, LANES), f32)
     for step in range(ITERS):
         got = [from_ahead(force, (0, 0, by)) for by in range(1, grid.gz)]
@@ -722,6 +755,7 @@
         grid.domains <= MAX_REPLICATED
         and grid.lists % 2 == 0
         and grid.gz == 2
+        and 2 * grid.padded <= LANES
         and positions.shape[2] == LANES
         and zone_sizes()[0] == LANES
         and pair_list.shape[1] % LANES == 0

time: 63.2 us -> 62.2 us (0.984)
  waiting for transfers between devices: 12.9 us -> 10.3 us
  starting transfers between devices: 10 us -> 11 us
    ppermute x9, waiting for transfers between devices: 12.9 us -> 10.3 us  [from_ahead(): return lax.ppermute(value, tuple(names), pairs)]
    ppermute x9, starting transfers between devices: 10 us -> 11 us  [from_ahead(): return lax.ppermute(value, tuple(names), pairs)]
    pallas_call x6 -> x7, Pallas kernels: 39.2 us -> 39.7 us  [call(): pl.pallas_call(kernel, out_shape=shapes, scratch_shapes=scratch, compiler...]
  transfers between devices with their start and end apart: 9 -> 9, of which waited for: 8 -> 7; matrix products, arithmetic and copies ran while one was open for 0% -> 0% of each run, Pallas kernels for 0% -> 8%
where the time goes in v5:
time: 62.2 us; the launch traced here: 62 us
  Pallas kernels  39.7 us (64%)
  starting transfers between devices  11 us (18%)
  waiting for transfers between devices  10.3 us (17%)
  between operations  0.89 us (1%)
    pallas_call x7, Pallas kernels, call(): pl.pallas_call(kernel, out_shape=shapes, scratch_shapes=scratch, compiler...  39.7 us
    ppermute x9, starting transfers between devices, from_ahead(): return lax.ppermute(value, tuple(names), pairs)  11 us
    ppermute x9, waiting for transfers between devices, from_ahead(): return lax.ppermute(value, tuple(names), pairs)  10.3 us
  transfers between devices with their start and end apart: 9, of which 7 were waited for; matrix products, arithmetic and copies ran while one was open for 0% of the time, Pallas kernels for 8%

profile of v5, /device:TPU:0, one launch (start us, length us, event | category | flops | bytes accessed | tf_op | source)
XLA Modules:
  0.0 62.0 jit_solution(3066890258121932922)
XLA Ops:
  0.6 0.8 %shard_map.76 = f32[88,128]{1,0:T(8,128)S(1)} custom-call(f32[3,8,128]{2,1,0:T(8,128)} %refs_0_.1, f32[3,8,128]{2,1,0:T(8,128)} %refs_1_.1, s32[7,128]{1,0:T(8,128)} %refs_2_.1, s32[2,1792]{1,0:T(2,128)} %refs_3_.1, s32[1,178]{1,0:T(1,128)} %bitcast.8), custom_call_target="tpu_custom_call" | custom-call | tf_op jit(solution)/shard_map/pallas_call | solution.py:680
  1.5 3.0 %collective-permute-start = (f32[88,128]{1,0:T(8,128)S(1)}, f32[88,128]{1,0:T(8,128)S(1)}, u32[]{:S(2)}, u32[]{:S(2)}) collective-permute-start(f32[88,128]{1,0:T(8,128)S(1)} %shard_map.76), channel_id=1, source_target_pairs={{2,0},{0,2},{3,1},{1,3},{6,4},{4,6},{7,5},{5,7},{10,8},{8,10},{11,... | collective-permute-start | bytes 135176 | tf_op jit(solution)/shard_map/ppermute | solution.py:667
  4.5 2.0 %collective-permute-done = f32[88,128]{1,0:T(8,128)S(1)} collective-permute-done((f32[88,128]{1,0:T(8,128)S(1)}, f32[88,128]{1,0:T(8,128)S(1)}, u32[]{:S(2)}, u32[]{:S(2)}) %collective-permute-start) | collective-permute-done | bytes 45088 | tf_op jit(solution)/shard_map/ppermute | solution.py:667
  6.5 2.1 %collective-permute-start.3 = (f32[2,88,128]{2,1,0:T(8,128)S(1)}, f32[2,88,128]{2,1,0:T(8,128)S(1)}, u32[]{:S(2)}, u32[]{:S(2)}) collective-permute-start(f32[2,88,128]{2,1,0:T(8,128)S(1)} %pad_maximum_fusion), channel_id=1, source_target_pairs={{12,0},{0,4},{4,8},{8,12},{13,1},{1,5},{5,9},{9,13},{14,2},{2,6},{... | collective-permute-start | bytes 270344 | tf_op jit(solution)/shard_map/ppermute | solution.py:667
  8.7 2.6 %collective-permute-start.2 = (f32[2,88,128]{2,1,0:T(8,128)S(1)}, f32[2,88,128]{2,1,0:T(8,128)S(1)}, u32[]{:S(2)}, u32[]{:S(2)}) collective-permute-start(f32[2,88,128]{2,1,0:T(8,128)S(1)} %pad_maximum_fusion), channel_id=1, source_target_pairs={{8,0},{12,4},{0,8},{4,12},{9,1},{13,5},{1,9},{5,13},{10,2},{14,6},... | collective-permute-start | bytes 270344 | tf_op jit(solution)/shard_map/ppermute | solution.py:667
  11.3 1.3 %collective-permute-start.1 = (f32[2,88,128]{2,1,0:T(8,128)S(1)}, f32[2,88,128]{2,1,0:T(8,128)S(1)}, u32[]{:S(2)}, u32[]{:S(2)}) collective-permute-start(f32[2,88,128]{2,1,0:T(8,128)S(1)} %pad_maximum_fusion), channel_id=1, source_target_pairs={{4,0},{8,4},{12,8},{0,12},{5,1},{9,5},{13,9},{1,13},{6,2},{10,6},{... | collective-permute-start | bytes 270344 | tf_op jit(solution)/shard_map/ppermute | solution.py:667
  12.6 3.6 %collective-permute-done.1 = f32[2,88,128]{2,1,0:T(8,128)S(1)} collective-permute-done((f32[2,88,128]{2,1,0:T(8,128)S(1)}, f32[2,88,128]{2,1,0:T(8,128)S(1)}, u32[]{:S(2)}, u32[]{:S(2)}) %collective-permute-start.1) | collective-permute-done | bytes 90144 | tf_op jit(solution)/shard_map/ppermute | solution.py:667
  16.3 0.3 collective-permute-done.2
  16.6 0.0 collective-permute-done.3
  16.6 0.1 collective-permute-start.4
  16.7 5.0 %shard_map.77 = (s32[2,8,16,128]{3,2,1,0:T(8,128)S(1)}, f32[8,16,128]{2,1,0:T(8,128)S(1)}, bf16[8,3,3584,128]{3,2,1,0:T(8,128)(2,1)S(1)}) custom-call(f32[8,88,128]{2,1,0:T(8,128)S(1)} %constant_dynamic-update-slice_fusion.near_ref), custom_call_target="tpu_custom_call" | custom-call | tf_op jit(solution)/shard_map/pallas_call | solution.py:680
  21.7 0.0 collective-permute-done.4.far_ref
  21.7 9.1 %shard_map.78 = (f32[3,128,128]{2,1,0:T(8,128)S(1)}, f32[3,128,128]{2,1,0:T(8,128)S(1)}, f32[128,128]{1,0:T(8,128)S(1)}, f32[128,128]{1,0:T(8,128)S(1)}, s32[8,8...) custom-call(f32[8,88,128]{2,1,0:T(8,128)S(1)} %constant_dynamic-update-slice_fusion.near_ref, ...), custom_call_target="tpu_custom_call" | custom-call | tf_op jit(solution)/shard_map/pallas_call | solution.py:680
  30.8 0.6 collective-permute-start.5
  31.4 1.1 %collective-permute-done.5.refs_0_ = f32[392,128]{1,0:T(8,128)S(1)} collective-permute-done((f32[392,128]{1,0:T(8,128)S(1)}, f32[392,128]{1,0:T(8,128)S(1)}, u32[]{:S(2)}, u32[]{:S(2)}) %collective-permute-start.5) | collective-permute-done | bytes 200736 | tf_op jit(solution)/shard_map/ppermute | solution.py:667
  32.5 7.9 %shard_map.79 = (f32[3,128,128]{2,1,0:T(8,128)S(1)}, f32[3,128,128]{2,1,0:T(8,128)S(1)}, f32[8,128]{1,0:T(8,128)S(1)}, f32[392,128]{1,0:T(8,128)S(1)}) custom-call(f32[3,128,128]{2,1,0:T(8,128)S(1)} %get-tuple-element.31.x_ref, f32[3,128,128]{2,1,0:T(8,128)S(1)} %get-tuple-element.32.v_ref, f32[128,128]{1,0:T(8,128)S(1)} %get-tuple-element.33.rest_ref, ...), custom_call_target="tpu_custom_call" | custom-call | tf_op jit(solution)/shard_map/pallas_call | solution.py:680
  40.4 0.4 collective-permute-start.6
  40.8 1.1 %collective-permute-done.6.refs_0_ = f32[392,128]{1,0:T(8,128)S(1)} collective-permute-done((f32[392,128]{1,0:T(8,128)S(1)}, f32[392,128]{1,0:T(8,128)S(1)}, u32[]{:S(2)}, u32[]{:S(2)}) %collective-permute-start.6) | collective-permute-done | bytes 200736 | tf_op jit(solution)/shard_map/ppermute | solution.py:667
  41.9 8.1 %shard_map.80 = (f32[3,128,128]{2,1,0:T(8,128)S(1)}, f32[3,128,128]{2,1,0:T(8,128)S(1)}, f32[8,128]{1,0:T(8,128)S(1)}, f32[392,128]{1,0:T(8,128)S(1)}) custom-call(f32[3,128,128]{2,1,0:T(8,128)S(1)} %get-tuple-element.38.x_ref, f32[3,128,128]{2,1,0:T(8,128)S(1)} %get-tuple-element.39.v_ref, f32[128,128]{1,0:T(8,128)S(1)} %get-tuple-element.33.rest_ref, ...), custom_call_target="tpu_custom_call" | custom-call | tf_op jit(solution)/shard_map/pallas_call | solution.py:680
  50.1 0.4 collective-permute-start.7
  50.5 1.1 %collective-permute-done.7.refs_0_ = f32[392,128]{1,0:T(8,128)S(1)} collective-permute-done((f32[392,128]{1,0:T(8,128)S(1)}, f32[392,128]{1,0:T(8,128)S(1)}, u32[]{:S(2)}, u32[]{:S(2)}) %collective-permute-start.7) | collective-permute-done | bytes 200736 | tf_op jit(solution)/shard_map/ppermute | solution.py:667
  51.6 8.0 %shard_map.81 = (f32[3,128,128]{2,1,0:T(8,128)S(1)}, f32[3,128,128]{2,1,0:T(8,128)S(1)}, f32[8,128]{1,0:T(8,128)S(1)}, f32[392,128]{1,0:T(8,128)S(1)}) custom-call(f32[3,128,128]{2,1,0:T(8,128)S(1)} %get-tuple-element.42.x_ref, f32[3,128,128]{2,1,0:T(8,128)S(1)} %get-tuple-element.43.v_ref, f32[128,128]{1,0:T(8,128)S(1)} %get-tuple-element.33.rest_ref, ...), custom_call_target="tpu_custom_call" | custom-call | tf_op jit(solution)/shard_map/pallas_call | solution.py:680
  59.5 0.4 collective-permute-start.8
  60.0 1.1 %collective-permute-done.8.refs_0_ = f32[392,128]{1,0:T(8,128)S(1)} collective-permute-done((f32[392,128]{1,0:T(8,128)S(1)}, f32[392,128]{1,0:T(8,128)S(1)}, u32[]{:S(2)}, u32[]{:S(2)}) %collective-permute-start.8) | collective-permute-done | bytes 200736 | tf_op jit(solution)/shard_map/ppermute | solution.py:667
  61.0 0.8 %shard_map.82 = (f32[3,8,128]{2,1,0:T(8,128)}, f32[3,8,128]{2,1,0:T(8,128)}, f32[2,3]{1,0:T(2,128)}) custom-call(f32[3,128,128]{2,1,0:T(8,128)S(1)} %get-tuple-element.46.x_ref, f32[3,128,128]{2,1,0:T(8,128)S(1)} %get-tuple-element.47.v_ref, f32[8,128]{1,0:T(8,128)S(1)} %get-tuple-element.48.energies_ref, f32[392,128]{1,0:T(8,128)S(1)} %get-tuple-element.49.own_ref, ...), custom_call_target="tpu_custom_call" | custom-call | tf_op jit(solution)/shard_map/pallas_call | solution.py:680
  (7 shorter events, 0.0 us)
Async XLA Ops:
  1.5 5.1 %collective-permute-start = (f32[88,128]{1,0:T(8,128)S(1)}, f32[88,128]{1,0:T(8,128)S(1)}, u32[]{:S(2)}, u32[]{:S(2)}) collective-permute-start(f32[88,128]{1,0:T(8,128)S(1)} %shard_map.76), channel_id=1, source_target_pairs={{2,0},{0,2},{3,1},{1,3},{6,4},{4,6},{7,5},{5,7},{10,8},{8,10},{11,... | collective-permute-start | bytes 135176 | tf_op jit(solution)/shard_map/ppermute | solution.py:667
  6.5 10.1 %collective-permute-start.3 = (f32[2,88,128]{2,1,0:T(8,128)S(1)}, f32[2,88,128]{2,1,0:T(8,128)S(1)}, u32[]{:S(2)}, u32[]{:S(2)}) collective-permute-start(f32[2,88,128]{2,1,0:T(8,128)S(1)} %pad_maximum_fusion), channel_id=1, source_target_pairs={{12,0},{0,4},{4,8},{8,12},{13,1},{1,5},{5,9},{9,13},{14,2},{2,6},{... | collective-permute-start | bytes 270344 | tf_op jit(solution)/shard_map/ppermute | solution.py:667
  8.7 7.9 %collective-permute-start.2 = (f32[2,88,128]{2,1,0:T(8,128)S(1)}, f32[2,88,128]{2,1,0:T(8,128)S(1)}, u32[]{:S(2)}, u32[]{:S(2)}) collective-permute-start(f32[2,88,128]{2,1,0:T(8,128)S(1)} %pad_maximum_fusion), channel_id=1, source_target_pairs={{8,0},{12,4},{0,8},{4,12},{9,1},{13,5},{1,9},{5,13},{10,2},{14,6},... | collective-permute-start | bytes 270344 | tf_op jit(solution)/shard_map/ppermute | solution.py:667
  11.3 5.0 %collective-permute-start.1 = (f32[2,88,128]{2,1,0:T(8,128)S(1)}, f32[2,88,128]{2,1,0:T(8,128)S(1)}, u32[]{:S(2)}, u32[]{:S(2)}) collective-permute-start(f32[2,88,128]{2,1,0:T(8,128)S(1)} %pad_maximum_fusion), channel_id=1, source_target_pairs={{4,0},{8,4},{12,8},{0,12},{5,1},{9,5},{13,9},{1,13},{6,2},{10,6},{... | collective-permute-start | bytes 270344 | tf_op jit(solution)/shard_map/ppermute | solution.py:667
  16.6 5.1 %collective-permute-start.4 = (f32[8,88,128]{2,1,0:T(8,128)S(1)}, f32[8,88,128]{2,1,0:T(8,128)S(1)}, u32[]{:S(2)}, u32[]{:S(2)}) collective-permute-start(f32[8,88,128]{2,1,0:T(8,128)S(1)} %constant_dynamic-update-slice_fusion.near_ref), channel_id=1, source_target_pairs={{1,0},{0,1},{3,2},{2,3},{5,4},{4,5},{7,6},{6,7},{9,8},{8,9},{11,10... | collective-permute-start | bytes 1081352 | tf_op jit(solution)/shard_map/ppermute | solution.py:667
  30.8 1.6 %collective-permute-start.5 = (f32[392,128]{1,0:T(8,128)S(1)}, f32[392,128]{1,0:T(8,128)S(1)}, u32[]{:S(2)}, u32[]{:S(2)}) collective-permute-start(f32[392,128]{1,0:T(8,128)S(1)} %get-tuple-element.37.own_ref), channel_id=1, source_target_pairs={{1,0},{0,1},{3,2},{2,3},{5,4},{4,5},{7,6},{6,7},{9,8},{8,9},{11,10... | collective-permute-start | bytes 602120 | tf_op jit(solution)/shard_map/ppermute | solution.py:667
  40.4 1.5 %collective-permute-start.6 = (f32[392,128]{1,0:T(8,128)S(1)}, f32[392,128]{1,0:T(8,128)S(1)}, u32[]{:S(2)}, u32[]{:S(2)}) collective-permute-start(f32[392,128]{1,0:T(8,128)S(1)} %get-tuple-element.41.own_ref), channel_id=1, source_target_pairs={{1,0},{0,1},{3,2},{2,3},{5,4},{4,5},{7,6},{6,7},{9,8},{8,9},{11,10... | collective-permute-start | bytes 602120 | tf_op jit(solution)/shard_map/ppermute | solution.py:667
  50.1 1.5 %collective-permute-start.7 = (f32[392,128]{1,0:T(8,128)S(1)}, f32[392,128]{1,0:T(8,128)S(1)}, u32[]{:S(2)}, u32[]{:S(2)}) collective-permute-start(f32[392,128]{1,0:T(8,128)S(1)} %get-tuple-element.45.own_ref), channel_id=1, source_target_pairs={{1,0},{0,1},{3,2},{2,3},{5,4},{4,5},{7,6},{6,7},{9,8},{8,9},{11,10... | collective-permute-start | bytes 602120 | tf_op jit(solution)/shard_map/ppermute | solution.py:667
  59.5 1.5 %collective-permute-start.8 = (f32[392,128]{1,0:T(8,128)S(1)}, f32[392,128]{1,0:T(8,128)S(1)}, u32[]{:S(2)}, u32[]{:S(2)}) collective-permute-start(f32[392,128]{1,0:T(8,128)S(1)} %get-tuple-element.49.own_ref), channel_id=1, source_target_pairs={{1,0},{0,1},{3,2},{2,3},{5,4},{4,5},{7,6},{6,7},{9,8},{8,9},{11,10... | collective-permute-start | bytes 602120 | tf_op jit(solution)/shard_map/ppermute | solution.py:667

commit v6 on v5

--- a/solution.py
+++ b/solution.py
@@ -171,7 +171,7 @@
     coupling_up = jnp.pad(coupling, ((0, 1), (0, 0)))
     series = source
     result = source
-    for expansion in range(NORDER):
+    for _ in range(NORDER):
         series = (
             coupling_down * jnp.pad(series, ((1, 0), (0, 0)))[:-1]
             + coupling_up * jnp.pad(series, ((0, 1), (0, 0)))[1:]
@@ -232,7 +232,7 @@
     send_table = (owned == send_list[None, :]).astype(jnp.float32)
     forces, potential = local_forces(positions, send_table, pair_list, tables)
     energy_rows = []
-    for iteration in range(ITERS):
+    for _ in range(ITERS):
         half_speed = velocities + 0.5 * time_step * forces
         updated = constrain(positions, positions + time_step * half_speed, rest_length, link_flags)
         half_speed = (updated - positions) / time_step
@@ -299,8 +299,10 @@
     return (lax.broadcasted_iota(jnp.int32, shape, dimension) + start).astype(jnp.float32).astype(jnp.bfloat16)
 
 
-def table_kernel(grid, pair_row, near_ref, ids_ref, weight_ref, table_ref, spread_ref, turned_ref):
+def table_kernel(grid, pair_row, first, near_ref, *refs):
+    ids_ref, weight_ref, table_ref, spread_ref, turned_ref = refs[-5:]
     blocks = grid.blocks
+    count = near_ref.shape[0] if first == 0 else grid.lists - first
     square = (LANES, LANES)
     codes_of = (rounded_iota(square, 1), rounded_iota(square, 1, LANES), -rounded_iota(square, 1, 1))
     one, zero = jnp.ones(square, jnp.bfloat16), jnp.zeros(square, jnp.bfloat16)
@@ -308,7 +310,7 @@
     for at in range(2 * blocks):
         place = at // blocks * grid.padded + at % blocks
         spread_ref[:, pl.ds(at * LANES, LANES)] = jnp.where(row == place, one, zero)
-    for number in range(grid.lists):
+    for number in range(first, first + count):
         sides = []
         for side in range(2):
             ids = near_ref[number, pl.ds(pair_row + side * blocks, blocks), :]
@@ -331,7 +333,7 @@
                 table_ref[number, part, pl.ds(at * LANES, LANES), :] = hot
         return carry
 
-    lax.fori_loop(0, grid.lists, one_list, 0)
+    lax.fori_loop(first, first + count, one_list, 0)
 
 
 def build_zones(grid, near_ref, far_ref, send_row, index_ref, zone_ref):
@@ -538,7 +540,7 @@
 def expand_rows(coupling, before, source):
     series = source
     result = source
-    for expansion in range(NORDER):
+    for _ in range(NORDER):
         series = before * down(series) + coupling * up(series)
         result = result + series
     return result
@@ -680,6 +682,7 @@
         return pl.pallas_call(kernel, out_shape=shapes, scratch_shapes=scratch, compiler_params=params, **specs)(*values)
 
     anywhere = pl.BlockSpec(memory_space=pltpu.MemorySpace.HBM)
+    whole = pl.BlockSpec(memory_space=pltpu.MemorySpace.VMEM)
     given = (positions, velocities, constraint_flags, pair_list, send_list.reshape(1, -1))
     given = [pltpu.with_memory_space_constraint(value, pltpu.MemorySpace.HBM) for value in given]
 
@@ -691,23 +694,32 @@
         in_specs=[anywhere] * len(given),
     )
     column = jnp.stack([from_ahead(pack, (0, j, 0)) for j in range(grid.gy)])
-    near = jnp.concatenate([from_ahead(column, (i, 0, 0)) for i in range(grid.gx)], axis=0)
-    far = from_ahead(near, (0, 0, 1))
     f32, i32, b16 = jnp.float32, jnp.int32, jnp.bfloat16
     n, rows = grid.lists, grid.domains * 8
     cube = jax.ShapeDtypeStruct((3, rows, LANES), f32)
     plane = jax.ShapeDtypeStruct((rows, LANES), f32)
     small = jax.ShapeDtypeStruct((8, LANES), f32)
     forces = jax.ShapeDtypeStruct((3 * rows + 8, LANES), f32)
+    shapes = [
+        jax.ShapeDtypeStruct((2, n, grid.padded, LANES), i32),
+        jax.ShapeDtypeStruct((n, grid.padded, LANES), f32),
+        jax.ShapeDtypeStruct((n, 3, grid.slots, LANES), b16),
+    ]
+    room = [pltpu.VMEM((LANES, grid.slots), b16), pltpu.VMEM((n, LANES, LANES), b16)]
+    begun = call(functools.partial(table_kernel, grid, layout["pairs"], 0), shapes, room, column)
+    ahead = [column]
+    for i in range(1, grid.gx):
+        ahead.append(from_ahead(column, (i, 0, 0)))
+    ahead, begun = lax.optimization_barrier((ahead, begun))
+    near = jnp.concatenate(ahead, axis=0)
+    far = from_ahead(near, (0, 0, 1))
     ids, weight, table = call(
-        functools.partial(table_kernel, grid, layout["pairs"]),
-        [
-            jax.ShapeDtypeStruct((2, n, grid.padded, LANES), i32),
-            jax.ShapeDtypeStruct((n, grid.padded, LANES), f32),
-            jax.ShapeDtypeStruct((n, 3, grid.slots, LANES), b16),
-        ],
-        [pltpu.VMEM((LANES, grid.slots), b16), pltpu.VMEM((n, LANES, LANES), b16)],
-        near,
+        functools.partial(table_kernel, grid, layout["pairs"], grid.gy),
+        shapes,
+        room,
+        near, *begun,
+        input_output_aliases={1: 0, 2: 1, 3: 2},
+        in_specs=[whole] + [pl.BlockSpec(memory_space=pl.ANY)] * 3,
     )
     zone_shapes = [
         jax.ShapeDtypeStruct((n, 8, LANES), i32),
@@ -755,6 +767,7 @@
         grid.domains <= MAX_REPLICATED
         and grid.lists % 2 == 0
         and grid.gz == 2
+        and grid.gx > 1
         and 2 * grid.padded <= LANES
         and positions.shape[2] == LANES
         and zone_sizes()[0] == LANES

time: 62.2 us -> 62.5 us (level)
  waiting for transfers between devices: 10.3 us -> 11.4 us
  starting transfers between devices: 11 us -> 10.2 us
    ppermute x9, waiting for transfers between devices: 10.3 us -> 11.4 us  [from_ahead(): return lax.ppermute(value, tuple(names), pairs)]
    ppermute x9, starting transfers between devices: 11 us -> 10.2 us  [from_ahead(): return lax.ppermute(value, tuple(names), pairs)]
    pallas_call x7 -> x8, Pallas kernels: 39.7 us -> 39.8 us  [call(): pl.pallas_call(kernel, out_shape=shapes, scratch_shapes=scratch, compiler...]
where the time goes in v6:
time: 62.5 us; the launch traced here: 62.3 us
  Pallas kernels  39.8 us (64%)
  waiting for transfers between devices  11.4 us (18%)
  starting transfers between devices  10.2 us (16%)
  between operations  0.9 us (1%)
    pallas_call x8, Pallas kernels, call(): pl.pallas_call(kernel, out_shape=shapes, scratch_shapes=scratch, compiler...  39.8 us
    ppermute x9, waiting for transfers between devices, from_ahead(): return lax.ppermute(value, tuple(names), pairs)  11.4 us
    ppermute x9, starting transfers between devices, from_ahead(): return lax.ppermute(value, tuple(names), pairs)  10.2 us
  transfers between devices with their start and end apart: 9, of which 7 were waited for; matrix products, arithmetic and copies ran while one was open for 0% of the time, Pallas kernels for 8%

profile of v6, /device:TPU:0, one launch (start us, length us, event | category | flops | bytes accessed | tf_op | source)
XLA Modules:
  0.0 62.3 jit_solution(3001719502070572413)
XLA Ops:
  0.6 0.8 %shard_map.76 = f32[88,128]{1,0:T(8,128)S(1)} custom-call(f32[3,8,128]{2,1,0:T(8,128)} %refs_0_.1, f32[3,8,128]{2,1,0:T(8,128)} %refs_1_.1, s32[7,128]{1,0:T(8,128)} %refs_2_.1, s32[2,1792]{1,0:T(2,128)} %refs_3_.1, s32[1,178]{1,0:T(1,128)} %bitcast.6), custom_call_target="tpu_custom_call" | custom-call | tf_op jit(solution)/shard_map/pallas_call | solution.py:682
  1.5 3.0 %collective-permute-start = (f32[88,128]{1,0:T(8,128)S(1)}, f32[88,128]{1,0:T(8,128)S(1)}, u32[]{:S(2)}, u32[]{:S(2)}) collective-permute-start(f32[88,128]{1,0:T(8,128)S(1)} %shard_map.76), channel_id=1, source_target_pairs={{2,0},{0,2},{3,1},{1,3},{6,4},{4,6},{7,5},{5,7},{10,8},{8,10},{11,... | collective-permute-start | bytes 135176 | tf_op jit(solution)/shard_map/ppermute | solution.py:669
  4.5 2.0 %collective-permute-done = f32[88,128]{1,0:T(8,128)S(1)} collective-permute-done((f32[88,128]{1,0:T(8,128)S(1)}, f32[88,128]{1,0:T(8,128)S(1)}, u32[]{:S(2)}, u32[]{:S(2)}) %collective-permute-start) | collective-permute-done | bytes 45088 | tf_op jit(solution)/shard_map/ppermute | solution.py:669
  6.5 4.2 %collective-permute-start.1 = (f32[2,88,128]{2,1,0:T(8,128)S(1)}, f32[2,88,128]{2,1,0:T(8,128)S(1)}, u32[]{:S(2)}, u32[]{:S(2)}) collective-permute-start(f32[2,88,128]{2,1,0:T(8,128)S(1)} %pad_maximum_fusion.near_ref), channel_id=1, source_target_pairs={{4,0},{8,4},{12,8},{0,12},{5,1},{9,5},{13,9},{1,13},{6,2},{10,6},{... | collective-permute-start | bytes 270344 | tf_op jit(solution)/shard_map/ppermute | solution.py:669
  10.7 0.0 collective-permute-start.2
  10.7 1.0 %collective-permute-start.3 = (f32[2,88,128]{2,1,0:T(8,128)S(1)}, f32[2,88,128]{2,1,0:T(8,128)S(1)}, u32[]{:S(2)}, u32[]{:S(2)}) collective-permute-start(f32[2,88,128]{2,1,0:T(8,128)S(1)} %pad_maximum_fusion.near_ref), channel_id=1, source_target_pairs={{12,0},{0,4},{4,8},{8,12},{13,1},{1,5},{5,9},{9,13},{14,2},{2,6},{... | collective-permute-start | bytes 270344 | tf_op jit(solution)/shard_map/ppermute | solution.py:669
  11.7 1.4 %shard_map.77 = (s32[2,8,16,128]{3,2,1,0:T(8,128)S(1)}, f32[8,16,128]{2,1,0:T(8,128)S(1)}, bf16[8,3,3584,128]{3,2,1,0:T(8,128)(2,1)S(1)}) custom-call(f32[2,88,128]{2,1,0:T(8,128)S(1)} %pad_maximum_fusion.near_ref), custom_call_target="tpu_custom_call" | custom-call | tf_op jit(solution)/shard_map/pallas_call | solution.py:682
  13.1 0.3 collective-permute-done.1
  13.4 4.7 %collective-permute-done.2 = f32[2,88,128]{2,1,0:T(8,128)S(1)} collective-permute-done((f32[2,88,128]{2,1,0:T(8,128)S(1)}, f32[2,88,128]{2,1,0:T(8,128)S(1)}, u32[]{:S(2)}, u32[]{:S(2)}) %collective-permute-start.2) | collective-permute-done | bytes 90144 | tf_op jit(solution)/shard_map/ppermute | solution.py:669
  18.1 0.0 collective-permute-done.3
  18.2 0.1 collective-permute-start.4
  18.3 3.8 %shard_map.78 = (s32[2,8,16,128]{3,2,1,0:T(8,128)S(1)}, f32[8,16,128]{2,1,0:T(8,128)S(1)}, bf16[8,3,3584,128]{3,2,1,0:T(8,128)(2,1)S(1)}) custom-call(f32[8,88,128]{2,1,0:T(8,128)S(1)} %constant_dynamic-update-slice_fusion.near_ref, s32[2,8,16,128]{3,2,1,0:T(8,128)S(1)} %get-tuple-element.45.refs_0_, ...), custom_call_target="tpu_custom_call", output_to_operand_aliasing={{0}: (1, {}), {1}: (2, {}), {2}: (3, {})} | custom-call | tf_op jit(solution)/shard_map/pallas_call | solution.py:682
  22.1 0.0 collective-permute-done.4.far_ref
  22.1 9.1 %shard_map.79 = (f32[3,128,128]{2,1,0:T(8,128)S(1)}, f32[3,128,128]{2,1,0:T(8,128)S(1)}, f32[128,128]{1,0:T(8,128)S(1)}, f32[128,128]{1,0:T(8,128)S(1)}, s32[8,8...) custom-call(f32[8,88,128]{2,1,0:T(8,128)S(1)} %constant_dynamic-update-slice_fusion.near_ref, ...), custom_call_target="tpu_custom_call" | custom-call | tf_op jit(solution)/shard_map/pallas_call | solution.py:682
  31.2 0.6 collective-permute-start.5
  31.7 1.1 %collective-permute-done.5.refs_0_ = f32[392,128]{1,0:T(8,128)S(1)} collective-permute-done((f32[392,128]{1,0:T(8,128)S(1)}, f32[392,128]{1,0:T(8,128)S(1)}, u32[]{:S(2)}, u32[]{:S(2)}) %collective-permute-start.5) | collective-permute-done | bytes 200736 | tf_op jit(solution)/shard_map/ppermute | solution.py:669
  32.8 7.9 %shard_map.80 = (f32[3,128,128]{2,1,0:T(8,128)S(1)}, f32[3,128,128]{2,1,0:T(8,128)S(1)}, f32[8,128]{1,0:T(8,128)S(1)}, f32[392,128]{1,0:T(8,128)S(1)}) custom-call(f32[3,128,128]{2,1,0:T(8,128)S(1)} %get-tuple-element.51.x_ref, f32[3,128,128]{2,1,0:T(8,128)S(1)} %get-tuple-element.52.v_ref, f32[128,128]{1,0:T(8,128)S(1)} %get-tuple-element.53.rest_ref, ...), custom_call_target="tpu_custom_call" | custom-call | tf_op jit(solution)/shard_map/pallas_call | solution.py:682
  40.7 0.4 collective-permute-start.6
  41.2 1.1 %collective-permute-done.6.refs_0_ = f32[392,128]{1,0:T(8,128)S(1)} collective-permute-done((f32[392,128]{1,0:T(8,128)S(1)}, f32[392,128]{1,0:T(8,128)S(1)}, u32[]{:S(2)}, u32[]{:S(2)}) %collective-permute-start.6) | collective-permute-done | bytes 200736 | tf_op jit(solution)/shard_map/ppermute | solution.py:669
  42.3 8.1 %shard_map.81 = (f32[3,128,128]{2,1,0:T(8,128)S(1)}, f32[3,128,128]{2,1,0:T(8,128)S(1)}, f32[8,128]{1,0:T(8,128)S(1)}, f32[392,128]{1,0:T(8,128)S(1)}) custom-call(f32[3,128,128]{2,1,0:T(8,128)S(1)} %get-tuple-element.58.x_ref, f32[3,128,128]{2,1,0:T(8,128)S(1)} %get-tuple-element.59.v_ref, f32[128,128]{1,0:T(8,128)S(1)} %get-tuple-element.53.rest_ref, ...), custom_call_target="tpu_custom_call" | custom-call | tf_op jit(solution)/shard_map/pallas_call | solution.py:682
  50.4 0.4 collective-permute-start.7
  50.8 1.1 %collective-permute-done.7.refs_0_ = f32[392,128]{1,0:T(8,128)S(1)} collective-permute-done((f32[392,128]{1,0:T(8,128)S(1)}, f32[392,128]{1,0:T(8,128)S(1)}, u32[]{:S(2)}, u32[]{:S(2)}) %collective-permute-start.7) | collective-permute-done | bytes 200736 | tf_op jit(solution)/shard_map/ppermute | solution.py:669
  51.9 8.0 %shard_map.82 = (f32[3,128,128]{2,1,0:T(8,128)S(1)}, f32[3,128,128]{2,1,0:T(8,128)S(1)}, f32[8,128]{1,0:T(8,128)S(1)}, f32[392,128]{1,0:T(8,128)S(1)}) custom-call(f32[3,128,128]{2,1,0:T(8,128)S(1)} %get-tuple-element.62.x_ref, f32[3,128,128]{2,1,0:T(8,128)S(1)} %get-tuple-element.63.v_ref, f32[128,128]{1,0:T(8,128)S(1)} %get-tuple-element.53.rest_ref, ...), custom_call_target="tpu_custom_call" | custom-call | tf_op jit(solution)/shard_map/pallas_call | solution.py:682
  59.9 0.4 collective-permute-start.8
  60.3 1.1 %collective-permute-done.8.refs_0_ = f32[392,128]{1,0:T(8,128)S(1)} collective-permute-done((f32[392,128]{1,0:T(8,128)S(1)}, f32[392,128]{1,0:T(8,128)S(1)}, u32[]{:S(2)}, u32[]{:S(2)}) %collective-permute-start.8) | collective-permute-done | bytes 200736 | tf_op jit(solution)/shard_map/ppermute | solution.py:669
  61.4 0.8 %shard_map.83 = (f32[3,8,128]{2,1,0:T(8,128)}, f32[3,8,128]{2,1,0:T(8,128)}, f32[2,3]{1,0:T(2,128)}) custom-call(f32[3,128,128]{2,1,0:T(8,128)S(1)} %get-tuple-element.66.x_ref, f32[3,128,128]{2,1,0:T(8,128)S(1)} %get-tuple-element.67.v_ref, f32[8,128]{1,0:T(8,128)S(1)} %get-tuple-element.68.energies_ref, f32[392,128]{1,0:T(8,128)S(1)} %get-tuple-element.69.own_ref, ...), custom_call_target="tpu_custom_call" | custom-call | tf_op jit(solution)/shard_map/pallas_call | solution.py:682
  (6 shorter events, 0.0 us)
Async XLA Ops:
  1.5 5.1 %collective-permute-start = (f32[88,128]{1,0:T(8,128)S(1)}, f32[88,128]{1,0:T(8,128)S(1)}, u32[]{:S(2)}, u32[]{:S(2)}) collective-permute-start(f32[88,128]{1,0:T(8,128)S(1)} %shard_map.76), channel_id=1, source_target_pairs={{2,0},{0,2},{3,1},{1,3},{6,4},{4,6},{7,5},{5,7},{10,8},{8,10},{11,... | collective-permute-start | bytes 135176 | tf_op jit(solution)/shard_map/ppermute | solution.py:669
  6.5 6.9 %collective-permute-start.1 = (f32[2,88,128]{2,1,0:T(8,128)S(1)}, f32[2,88,128]{2,1,0:T(8,128)S(1)}, u32[]{:S(2)}, u32[]{:S(2)}) collective-permute-start(f32[2,88,128]{2,1,0:T(8,128)S(1)} %pad_maximum_fusion.near_ref), channel_id=1, source_target_pairs={{4,0},{8,4},{12,8},{0,12},{5,1},{9,5},{13,9},{1,13},{6,2},{10,6},{... | collective-permute-start | bytes 270344 | tf_op jit(solution)/shard_map/ppermute | solution.py:669
  10.7 7.4 %collective-permute-start.2 = (f32[2,88,128]{2,1,0:T(8,128)S(1)}, f32[2,88,128]{2,1,0:T(8,128)S(1)}, u32[]{:S(2)}, u32[]{:S(2)}) collective-permute-start(f32[2,88,128]{2,1,0:T(8,128)S(1)} %pad_maximum_fusion.near_ref), channel_id=1, source_target_pairs={{8,0},{12,4},{0,8},{4,12},{9,1},{13,5},{1,9},{5,13},{10,2},{14,6},... | collective-permute-start | bytes 270344 | tf_op jit(solution)/shard_map/ppermute | solution.py:669
  10.7 7.4 %collective-permute-start.3 = (f32[2,88,128]{2,1,0:T(8,128)S(1)}, f32[2,88,128]{2,1,0:T(8,128)S(1)}, u32[]{:S(2)}, u32[]{:S(2)}) collective-permute-start(f32[2,88,128]{2,1,0:T(8,128)S(1)} %pad_maximum_fusion.near_ref), channel_id=1, source_target_pairs={{12,0},{0,4},{4,8},{8,12},{13,1},{1,5},{5,9},{9,13},{14,2},{2,6},{... | collective-permute-start | bytes 270344 | tf_op jit(solution)/shard_map/ppermute | solution.py:669
  18.2 3.9 %collective-permute-start.4 = (f32[8,88,128]{2,1,0:T(8,128)S(1)}, f32[8,88,128]{2,1,0:T(8,128)S(1)}, u32[]{:S(2)}, u32[]{:S(2)}) collective-permute-start(f32[8,88,128]{2,1,0:T(8,128)S(1)} %constant_dynamic-update-slice_fusion.near_ref), channel_id=1, source_target_pairs={{1,0},{0,1},{3,2},{2,3},{5,4},{4,5},{7,6},{6,7},{9,8},{8,9},{11,10... | collective-permute-start | bytes 1081352 | tf_op jit(solution)/shard_map/ppermute | solution.py:669
  31.2 1.6 %collective-permute-start.5 = (f32[392,128]{1,0:T(8,128)S(1)}, f32[392,128]{1,0:T(8,128)S(1)}, u32[]{:S(2)}, u32[]{:S(2)}) collective-permute-start(f32[392,128]{1,0:T(8,128)S(1)} %get-tuple-element.57.own_ref), channel_id=1, source_target_pairs={{1,0},{0,1},{3,2},{2,3},{5,4},{4,5},{7,6},{6,7},{9,8},{8,9},{11,10... | collective-permute-start | bytes 602120 | tf_op jit(solution)/shard_map/ppermute | solution.py:669
  40.7 1.5 %collective-permute-start.6 = (f32[392,128]{1,0:T(8,128)S(1)}, f32[392,128]{1,0:T(8,128)S(1)}, u32[]{:S(2)}, u32[]{:S(2)}) collective-permute-start(f32[392,128]{1,0:T(8,128)S(1)} %get-tuple-element.61.own_ref), channel_id=1, source_target_pairs={{1,0},{0,1},{3,2},{2,3},{5,4},{4,5},{7,6},{6,7},{9,8},{8,9},{11,10... | collective-permute-start | bytes 602120 | tf_op jit(solution)/shard_map/ppermute | solution.py:669
  50.4 1.5 %collective-permute-start.7 = (f32[392,128]{1,0:T(8,128)S(1)}, f32[392,128]{1,0:T(8,128)S(1)}, u32[]{:S(2)}, u32[]{:S(2)}) collective-permute-start(f32[392,128]{1,0:T(8,128)S(1)} %get-tuple-element.65.own_ref), channel_id=1, source_target_pairs={{1,0},{0,1},{3,2},{2,3},{5,4},{4,5},{7,6},{6,7},{9,8},{8,9},{11,10... | collective-permute-start | bytes 602120 | tf_op jit(solution)/shard_map/ppermute | solution.py:669
  59.9 1.5 %collective-permute-start.8 = (f32[392,128]{1,0:T(8,128)S(1)}, f32[392,128]{1,0:T(8,128)S(1)}, u32[]{:S(2)}, u32[]{:S(2)}) collective-permute-start(f32[392,128]{1,0:T(8,128)S(1)} %get-tuple-element.69.own_ref), channel_id=1, source_target_pairs={{1,0},{0,1},{3,2},{2,3},{5,4},{4,5},{7,6},{6,7},{9,8},{8,9},{11,10... | collective-permute-start | bytes 602120 | tf_op jit(solution)/shard_map/ppermute | solution.py:669
